TPU v7x, 512 devices: a whole 4x8x8 slice. The times are simulated.
512 devices in a mesh: dp: 64 (over x, z, y_hi), mp: 8 (over y_lo, core).
Axes of the slice: x: 4, y: 8 (y_hi: 2, y_lo: 4; y = y_hi * 4 + y_lo), z: 8, core: 2. Of those that a mesh axis runs over, the one named last changes fastest.
Arguments:
- gradient: bfloat16 [8, 32, 512, 512], P('mp', None, 'dp'), may hold values from -54 to 54
- owners: int32 [8, 32], P('mp'), may hold values from 0 to 63, as said below
- left_stats: float32 [8, 64, 512, 512], P('mp', 'dp'), may hold values from -0.2 to 20.2
- right_stats: float32 [8, 64, 512, 512], P('mp', 'dp'), may hold values from -0.2 to 20.2
- left_roots_old: bfloat16 [8, 64, 512, 512], P('mp', 'dp'), may hold values from -0.1 to 1.5
- right_roots_old: bfloat16 [8, 64, 512, 512], P('mp', 'dp'), may hold values from -0.1 to 1.5
Outputs:
- update: bfloat16 [8, 32, 512, 512], P('mp', None, 'dp')
- left_roots: bfloat16 [8, 64, 512, 512], P('mp', 'dp')
- right_roots: bfloat16 [8, 64, 512, 512], P('mp', 'dp')
Inputs may be any that keep to these rules, and one draw needn't show every extreme that they name: In each row the 32 owners are distinct. Owner o holds a block of row m exactly when owner (o + 32) mod 64 of row m holds none, and exactly when owner o of row (m + 4) mod 8 holds none.
All inputs are finite; a program needn't handle non-finite values.
Results may differ from a plain program's by a relative error of at most 0.0067.
Values may be sent and summed in bfloat16 or wider, within the bound.
No kernel may reach another device: no remote copies, remote signals or barrier semaphores. Data moves between devices by JAX's collectives and lax.ppermute only.
A program may use at most 64 MiB of HBM per device.

v0:
```python
import jax
import jax.numpy as jnp
from jax import lax
from jax.sharding import Mesh
from jax.sharding import PartitionSpec as P

ITERS = 2
DP = ("dp_0", "dp_1", "dp_2")
DP_MP = ("dp_0", "dp_1", "dp_2", "mp_0", "mp_1")
MP = ("mp_0", "mp_1")


stat_decay = 0.9
ridge_term = 0.001
tiny_term = 1e-06


def over_axes(array, axes):
    for axis in axes:
        array = lax.psum(array, axis)
    return array


def newton_root(statistic):
    dimension = statistic.shape[0]
    identity = jnp.eye(dimension, dtype=jnp.float32)
    shifted = statistic + ridge_term * identity
    norm_scale = jnp.sqrt(jnp.sum(shifted * shifted) + tiny_term)
    matrix = shifted / norm_scale
    iterate = identity
    for iteration in range(ITERS):
        factor = ((5.0 * identity - matrix) / 4.0).astype(jnp.bfloat16)
        if iteration == 0:
            iterate = norm_scale ** (-0.25) * lax.optimization_barrier(factor).astype(jnp.float32)
        else:
            iterate = jnp.dot(
                iterate.astype(jnp.bfloat16), factor, preferred_element_type=jnp.float32
            )
        if iteration + 1 < ITERS:
            factor_two = jnp.dot(factor, factor, preferred_element_type=jnp.float32).astype(
                jnp.bfloat16
            )
            factor_four = jnp.dot(
                factor_two, factor_two, preferred_element_type=jnp.float32
            ).astype(jnp.bfloat16)
            matrix = jnp.dot(
                factor_four, matrix.astype(jnp.bfloat16), preferred_element_type=jnp.float32
            )
    return iterate.astype(jnp.bfloat16)


def shards(gradient, owners, left_stats, right_stats, left_roots_old, right_roots_old):
    dp_count = lax.axis_size(DP)
    my_index = lax.axis_index(DP)
    blocks_here = gradient.shape[1]
    row_count = gradient.shape[2]
    block_width = gradient.shape[3]
    owner_table = owners[0]
    owner_ids = jnp.arange(dp_count, dtype=jnp.int32)
    selector = (owner_table[None, :] == owner_ids[:, None]).astype(jnp.bfloat16)
    flat_grad = gradient[0].reshape(blocks_here, row_count * block_width)
    outgoing = jnp.dot(selector, flat_grad, preferred_element_type=jnp.float32).astype(jnp.bfloat16)
    outgoing = outgoing.reshape(dp_count, row_count, block_width)
    arrived = lax.all_to_all(outgoing, DP, split_axis=0, concat_axis=1, tiled=True)
    grad_block = arrived[0]
    is_mine = owner_table == my_index
    mine_weight = is_mine.astype(jnp.float32)
    is_busy = jnp.any(is_mine)
    left_gram = jnp.einsum("ik,jk->ij", grad_block, grad_block, preferred_element_type=jnp.float32)
    right_gram = jnp.einsum("ki,kj->ij", grad_block, grad_block, preferred_element_type=jnp.float32)
    left_new = stat_decay * left_stats[0, 0] + left_gram / block_width
    right_new = stat_decay * right_stats[0, 0] + right_gram / block_width
    shaded = jnp.dot(grad_block, right_roots_old[0, 0], preferred_element_type=jnp.float32).astype(
        jnp.bfloat16
    )
    direction = jnp.dot(left_roots_old[0, 0], shaded, preferred_element_type=jnp.float32).astype(
        jnp.bfloat16
    )
    squares = jnp.stack(
        [
            jnp.sum(jnp.square(grad_block.astype(jnp.float32))),
            jnp.sum(jnp.square(direction.astype(jnp.float32))),
        ]
    )
    graft_terms = squares[:, None] * mine_weight[None, :]
    totals = over_axes(graft_terms, DP_MP)
    graft_scale = jnp.sqrt(totals[0] / (totals[1] + tiny_term))
    own_graft = jnp.sum(graft_scale * mine_weight)
    scaled = (own_graft * direction.astype(jnp.float32)).astype(jnp.bfloat16)
    returned = lax.all_to_all(scaled[None], DP, split_axis=1, concat_axis=0, tiled=True)
    back_flat = jnp.einsum(
        "on,or->nr",
        selector,
        returned.reshape(dp_count, row_count * block_width),
        preferred_element_type=jnp.float32,
    )
    update = back_flat.astype(jnp.bfloat16).reshape(1, blocks_here, row_count, block_width)
    zero_root = jnp.zeros((block_width, block_width), jnp.bfloat16)
    left_root, right_root = lax.cond(
        is_busy,
        lambda: (newton_root(left_new), newton_root(right_new)),
        lambda: (zero_root, zero_root),
    )
    return (update, left_root[None, None], right_root[None, None])


def solution(mesh):
    finer = Mesh(mesh.devices.reshape(4, 8, 2, 4, 2), ("dp_0", "dp_1", "dp_2", "mp_0", "mp_1"))
    placed = (
        P(MP, None, DP, None),
        P(MP, None),
        P(MP, DP, None, None),
        P(MP, DP, None, None),
        P(MP, DP, None, None),
        P(MP, DP, None, None),
    )
    return jax.shard_map(
        shards,
        mesh=finer,
        in_specs=placed,
        out_specs=(P(MP, None, DP, None), P(MP, DP, None, None), P(MP, DP, None, None)),
        check_vma=False,
    )
```

profile of v0, /device:TPU:8, one launch (start us, length us, event | category | flops | bytes accessed | tf_op | source)
XLA Modules:
  0.0 137.8 jit_solution(4903565899408529476)
XLA Ops:
  0.6 0.0 copy-start
  0.6 1.1 copy.22
  1.7 0.0 copy-start.4
  1.7 0.6 copy-done.4
  2.4 0.3 convolution_convert_fusion.6
  2.7 1.0 copy.23
  3.6 18.2 %all-to-all-start = ((bf16[64,8,512]{2,1,0:T(8,128)(2,1)}), bf16[64,8,512]{2,1,0:T(8,128)(2,1)S(1)}, u32[]{:S(2)}, u32[]{:S(2)}) async-start(bf16[64,8,512]{2,1,0:T(8,128)(2,1)} %bitcast.20), calls=%async_computation | async-start | bytes 1048576 | tf_op jit(solution)/shard_map/all_to_all | solution.py:64
  21.8 0.0 copy-start.5
  21.8 0.6 compare_reduce_fusion
  23.1 21.4 %all-to-all-done = bf16[64,8,512]{2,1,0:T(8,128)(2,1)S(1)} async-done(((bf16[64,8,512]{2,1,0:T(8,128)(2,1)}), bf16[64,8,512]{2,1,0:T(8,128)(2,1)S(1)}, u32[]{:S(2)}, u32[]{:S(2)}) %all-to-all-start) | async-done | bytes 524320 | tf_op jit(solution)/shard_map/all_to_all | solution.py:64
  44.5 0.9 multiply_reduce_fusion.2
  45.4 0.0 copy-done
  45.4 0.0 copy-done.5
  45.4 1.5 %fusion.28 = (f32[]{:T(128)}, bf16[512,512]{1,0:T(8,128)(2,1)S(1)}) fusion(bf16[1,1,512,512]{3,2,1,0:T(8,128)(2,1)S(1)} %copy-done, bf16[1,1,512,512]{3,2,1,0:T(8,128)(2,1)S(1)} %copy-done.5, bf16[64,8,512]{2,1,0:T(8,128)(2,1)S(1)} %all-to-all-done), kind=kOutput, calls=%fused_computation.54 | convolution fusion | flops 538181632 | bytes 2097156 | tf_op jit(solution)/shard_map/dot_general | solution.py:76
  47.0 1.4 pad_maximum_fusion
  48.3 0.1 broadcast_multiply_fusion
  48.4 9.1 %psum.35 = f32[2,32]{1,0:T(2,128)S(1)} all-reduce(f32[2,32]{1,0:T(2,128)S(1)} %broadcast_multiply_fusion), channel_id=1, replica_groups=mesh['dp_0'=4,'dp_1'=8,'dp_2'=2,'mp_0'=4,'mp_1'=2] {'dp_0'}, use_global_device_ids=true, to_apply=%region_2.0 | all-reduce | flops 64 | bytes 512 | tf_op jit(solution)/shard_map/psum | solution.py:20
  57.5 15.1 %psum.36 = f32[2,32]{1,0:T(2,128)S(1)} all-reduce(f32[2,32]{1,0:T(2,128)S(1)} %psum.35), channel_id=1, replica_groups=mesh['dp_0'=4,'dp_1'=8,'dp_2'=2,'mp_0'=4,'mp_1'=2] {'dp_1'}, use_global_device_ids=true, to_apply=%region_3.0 | all-reduce | flops 64 | bytes 512 | tf_op jit(solution)/shard_map/psum | solution.py:20
  72.6 8.8 %psum.37 = f32[2,32]{1,0:T(2,128)S(1)} all-reduce(f32[2,32]{1,0:T(2,128)S(1)} %psum.36), channel_id=1, replica_groups=mesh['dp_0'=4,'dp_1'=8,'dp_2'=2,'mp_0'=4,'mp_1'=2] {'dp_2'}, use_global_device_ids=true, to_apply=%region_4.0 | all-reduce | flops 64 | bytes 512 | tf_op jit(solution)/shard_map/psum | solution.py:20
  81.4 8.0 %psum.38 = f32[2,32]{1,0:T(2,128)S(1)} all-reduce(f32[2,32]{1,0:T(2,128)S(1)} %psum.37), channel_id=1, replica_groups=mesh['dp_0'=4,'dp_1'=8,'dp_2'=2,'mp_0'=4,'mp_1'=2] {'mp_0'}, use_global_device_ids=true, to_apply=%region_5.0 | all-reduce | flops 64 | bytes 512 | tf_op jit(solution)/shard_map/psum | solution.py:20
  89.5 2.5 %psum.39 = f32[2,32]{1,0:T(2,128)S(1)} all-reduce(f32[2,32]{1,0:T(2,128)S(1)} %psum.38), channel_id=1, replica_groups=mesh['dp_0'=4,'dp_1'=8,'dp_2'=2,'mp_0'=4,'mp_1'=2] {'mp_1'}, use_global_device_ids=true, to_apply=%region_6.0 | all-reduce | flops 64 | bytes 512 | tf_op jit(solution)/shard_map/psum | solution.py:20
  91.9 0.6 fusion.40
  92.5 0.7 fusion.30
  93.3 0.9 copy.17
  94.2 0.5 broadcast.158
  94.7 3.8 %reduce.4 = bf16[512,512]{1,0:T(8,128)(2,1)S(1)} reduce(bf16[512,1,512]{2,1,0:T(2,128)(2,1)S(1)} %bitcast.83, bf16[]{:T(256)} %broadcast.158), dimensions={1}, to_apply=%bitcast.64.reduce_sub_computation | reduce | bytes 1048578
  98.5 1.0 reshape.38
  99.5 7.4 %all-to-all-start.1 = ((bf16[64,2,2048]{2,1,0:T(2,128)(2,1)}), bf16[64,2,2048]{2,1,0:T(2,128)(2,1)}, u32[]{:S(2)}, u32[]{:S(2)}) async-start(bf16[64,2,2048]{2,1,0:T(2,128)(2,1)} %reshape.38), calls=%async_computation.1 | async-start | bytes 1048576 | tf_op jit(solution)/shard_map/all_to_all | solution.py:90
  106.9 0.5 fusion.34
  107.4 0.0 copy-start.1
  107.4 1.5 %convolution_bitcast_fusion = f32[512,512]{1,0:T(8,128)} fusion(bf16[64,8,512]{2,1,0:T(8,128)(2,1)S(1)} %all-to-all-done), kind=kOutput, calls=%fused_computation.49 | convolution fusion | flops 268435456 | bytes 1572864 | tf_op jit(solution)/shard_map/ki,kj->ij/dot_general | solution.py:70
  108.9 0.0 copy-done.1
  108.9 0.9 conditional.1
  108.9 0.8 broadcast_in_dim.17.clone
  109.8 0.0 copy-start.2
  109.8 0.8 copy-done.2
  110.6 19.2 %all-to-all-done.1 = bf16[64,2,2048]{2,1,0:T(2,128)(2,1)} async-done(((bf16[64,2,2048]{2,1,0:T(2,128)(2,1)}), bf16[64,2,2048]{2,1,0:T(2,128)(2,1)}, u32[]{:S(2)}, u32[]{:S(2)}) %all-to-all-start.1) | async-done | bytes 524320 | tf_op jit(solution)/shard_map/all_to_all | solution.py:90
  129.8 3.6 %reshape.39 = bf16[512,1,512]{2,1,0:T(2,128)(2,1)S(1)} reshape(bf16[64,2,2048]{2,1,0:T(2,128)(2,1)} %all-to-all-done.1) | data formatting | bytes 1048576
  133.4 3.1 %bitcast_reduce_fusion = bf16[512,512]{1,0:T(8,128)(2,1)S(1)} fusion(bf16[512,1,512]{2,1,0:T(2,128)(2,1)S(1)} %reshape.39), kind=kLoop, calls=%fused_computation.74 | loop fusion | bytes 1048576 | tf_op jit(solution)/shard_map/all_to_all | solution.py:90
  136.5 0.2 reshape.29
  136.7 0.3 convolution_convert_fusion.7
  137.0 0.8 copy.24
  (2 shorter events, 0.0 us)
Async XLA Ops:
  0.6 44.8 %copy-start = (bf16[1,1,512,512]{3,2,1,0:T(8,128)(2,1)S(1)}, bf16[1,1,512,512]{3,2,1,0:T(8,128)(2,1)}, u32[]{:S(2)}) copy-start(bf16[1,1,512,512]{3,2,1,0:T(8,128)(2,1)} %param.12) | copy-start | bytes 1572868
  1.7 0.7 copy-start.4
  3.6 40.9 %all-to-all-start = ((bf16[64,8,512]{2,1,0:T(8,128)(2,1)}), bf16[64,8,512]{2,1,0:T(8,128)(2,1)S(1)}, u32[]{:S(2)}, u32[]{:S(2)}) async-start(bf16[64,8,512]{2,1,0:T(8,128)(2,1)} %bitcast.20), calls=%async_computation | async-start | bytes 1048576 | tf_op jit(solution)/shard_map/all_to_all | solution.py:64
  21.8 23.6 %copy-start.5 = (bf16[1,1,512,512]{3,2,1,0:T(8,128)(2,1)S(1)}, bf16[1,1,512,512]{3,2,1,0:T(8,128)(2,1)}, u32[]{:S(2)}) copy-start(bf16[1,1,512,512]{3,2,1,0:T(8,128)(2,1)} %param.13) | copy-start | bytes 1572868
  99.5 30.2 %all-to-all-start.1 = ((bf16[64,2,2048]{2,1,0:T(2,128)(2,1)}), bf16[64,2,2048]{2,1,0:T(2,128)(2,1)}, u32[]{:S(2)}, u32[]{:S(2)}) async-start(bf16[64,2,2048]{2,1,0:T(2,128)(2,1)} %reshape.38), calls=%async_computation.1 | async-start | bytes 1048576 | tf_op jit(solution)/shard_map/all_to_all | solution.py:90
  107.4 1.5 %copy-start.1 = (f32[1,1,512,512]{3,2,1,0:T(8,128)S(1)}, f32[1,1,512,512]{3,2,1,0:T(8,128)}, u32[]{:S(2)}) copy-start(f32[1,1,512,512]{3,2,1,0:T(8,128)} %param.10) | copy-start | bytes 3145732
  109.8 0.8 copy-start.2
where the time goes:
time: 138 us
  blocking collectives  43.5 us (32%)
  waiting for transfers between devices  40.6 us (29%)
  starting transfers between devices  25.6 us (19%)
  local copies, waits for them, and re-layouts  14.5 us (11%)
  other arithmetic  8.12 us (6%)
  matrix products  4.02 us (3%)
  between operations  1.42 us (1%)
    psum x5, blocking collectives, over_axes(): array = lax.psum(array, axis)  43.5 us
    all_to_all x1, waiting for transfers between devices, shards(): lax.all_to_all(outgoing, DP, split_axis=0, concat_axis=1, tiled=True)  21.4 us
    all_to_all x1, waiting for transfers between devices, shards(): lax.all_to_all(scaled[None], DP, split_axis=1, concat_axis=0, tiled=True)  19.2 us
    all_to_all x1, starting transfers between devices, shards(): lax.all_to_all(outgoing, DP, split_axis=0, concat_axis=1, tiled=True)  18.2 us
    unnamed x16, local copies, waits for them, and re-layouts  9.46 us
    all_to_all x1, starting transfers between devices, shards(): lax.all_to_all(scaled[None], DP, split_axis=1, concat_axis=0, tiled=True)  7.41 us
    unnamed x1, other arithmetic  3.82 us
    all_to_all x1, local copies, waits for them, and re-layouts, shards(): lax.all_to_all(scaled[None], DP, split_axis=1, concat_axis=0, tiled=True)  3.08 us
  transfers between devices with their start and end apart: 2, of which 2 were waited for; matrix products, arithmetic and copies ran while one was open for 3% of the time, Pallas kernels for 0%

commit v1 on v0

v1 whole, which is shorter than its diff:
```python
import jax
import jax.numpy as jnp
from jax import lax
from jax.experimental import pallas as pl
from jax.experimental.pallas import tpu as pltpu
from jax.sharding import Mesh
from jax.sharding import PartitionSpec as P

ITERS = 2
DP = ("dp_0h", "dp_0l", "dp_1", "dp_2")
MP = ("mp_0", "mp_1")
NEAR = ("dp_0h", "mp_0", "mp_1")
LANES = 128
MIB = 1024 * 1024


stat_decay = 0.9
ridge_term = 0.001
tiny_term = 1e-06

SMEM = pl.BlockSpec(memory_space=pltpu.SMEM)
VMEM = pl.BlockSpec(memory_space=pltpu.VMEM)


def params(mib):
    return pltpu.CompilerParams(vmem_limit_bytes=mib * MIB)


def partner_of(owner, dp_count):
    half = dp_count // 2
    return jnp.where(owner < half, owner + half, owner - half)


def place_blocks(owners, blocks, dp_count):
    blocks_here, row_count, width = blocks.shape

    def body(owner_ref, block_ref, slot_ref):
        for j in range(blocks_here):
            owner = owner_ref[0, j]
            rows = block_ref[j]
            slot_ref[owner] = rows
            slot_ref[partner_of(owner, dp_count)] = rows

    return pl.pallas_call(
        body,
        out_shape=jax.ShapeDtypeStruct((dp_count, row_count, width), blocks.dtype),
        in_specs=[SMEM, VMEM],
        out_specs=VMEM,
        compiler_params=params(4),
        name="place_blocks",
    )(owners, blocks)


def precondition(busy, masks, grad_block, left, right, near_count):
    def body(busy_ref, mask_ref, grad_ref, left_ref, right_ref, dir_ref, norm_ref):
        @pl.when(busy_ref[0] == 1)
        def _():
            grad = grad_ref[...]
            shaded = jnp.dot(grad, right_ref[...], preferred_element_type=jnp.float32)
            direction = jnp.dot(
                left_ref[...], shaded.astype(jnp.bfloat16), preferred_element_type=jnp.float32
            ).astype(jnp.bfloat16)
            dir_ref[...] = direction
            wide = grad.astype(jnp.float32)
            grad_square = jnp.sum(wide * wide, keepdims=True)
            wide = direction.astype(jnp.float32)
            dir_square = jnp.sum(wide * wide, keepdims=True)
            row = mask_ref[0:1] * grad_square + mask_ref[1:2] * dir_square
            norm_ref[...] = jnp.broadcast_to(row[None], norm_ref.shape)

        @pl.when(busy_ref[0] == 0)
        def _():
            norm_ref[...] = jnp.zeros_like(norm_ref)

    return pl.pallas_call(
        body,
        out_shape=(
            jax.ShapeDtypeStruct(grad_block.shape, jnp.bfloat16),
            jax.ShapeDtypeStruct((near_count, 1, LANES), jnp.float32),
        ),
        in_specs=[SMEM, VMEM, VMEM, VMEM, VMEM],
        out_specs=(VMEM, VMEM),
        compiler_params=params(12),
        name="precondition",
    )(busy, masks, grad_block, left, right)


def add_norms(busy, near_norms, slots):
    def body(busy_ref, near_ref, slot_ref, out_ref, rows_ref, sem):
        del slot_ref

        @pl.when(busy_ref[0] == 0)
        def _():
            total = jnp.sum(near_ref[...], axis=0)
            high = total.astype(jnp.bfloat16).astype(jnp.float32)
            rest = total - high
            middle = rest.astype(jnp.bfloat16).astype(jnp.float32)
            low = rest - middle
            row = lax.broadcasted_iota(jnp.int32, rows_ref.shape[1:], 0)
            shape = rows_ref.shape[1:]
            packed = jnp.where(
                row == 0,
                jnp.broadcast_to(high, shape),
                jnp.where(
                    row == 1,
                    jnp.broadcast_to(middle, shape),
                    jnp.where(row == 2, jnp.broadcast_to(low, shape), 0.0),
                ),
            ).astype(jnp.bfloat16)
            rows_ref[...] = jnp.broadcast_to(packed[None], rows_ref.shape)
            copy = pltpu.make_async_copy(rows_ref, out_ref.at[:, :, 0:LANES], sem)
            copy.start()
            copy.wait()

    dp_count, row_count, _ = slots.shape
    return pl.pallas_call(
        body,
        out_shape=jax.ShapeDtypeStruct(slots.shape, slots.dtype),
        in_specs=[SMEM, VMEM, pl.BlockSpec(memory_space=pl.ANY)],
        out_specs=pl.BlockSpec(memory_space=pl.ANY),
        scratch_shapes=[
            pltpu.VMEM((dp_count, row_count, LANES), slots.dtype),
            pltpu.SemaphoreType.DMA,
        ],
        input_output_aliases={2: 0},
        compiler_params=params(4),
        name="add_norms",
    )(busy, near_norms, slots)


def scale_blocks(owners, slots):
    blocks_here = owners.shape[1]
    dp_count, row_count, width = slots.shape

    def body(owner_ref, slot_ref, out_ref):
        norms = jnp.zeros((row_count, LANES), jnp.float32)
        for j in range(blocks_here):
            idle = partner_of(owner_ref[0, j], dp_count)
            norms = norms + slot_ref[idle, :, 0:LANES].astype(jnp.float32)
        totals = norms[0:1] + (norms[1:2] + norms[2:3])
        columns = jnp.broadcast_to(totals, (LANES, LANES)).T
        ratio = jnp.sqrt(
            columns[:blocks_here] / (columns[blocks_here : 2 * blocks_here] + tiny_term)
        )
        for j in range(blocks_here):
            owner = owner_ref[0, j]
            scale = jnp.broadcast_to(ratio[j : j + 1], (row_count, LANES))
            for c in range(width // LANES):
                at = slice(c * LANES, (c + 1) * LANES)
                rows = slot_ref[owner, :, at].astype(jnp.float32)
                out_ref[j, :, at] = (scale * rows).astype(out_ref.dtype)

    return pl.pallas_call(
        body,
        out_shape=jax.ShapeDtypeStruct((blocks_here, row_count, width), slots.dtype),
        in_specs=[SMEM, VMEM],
        out_specs=VMEM,
        compiler_params=params(4),
        name="scale_blocks",
    )(owners, slots)


def refresh(busy, grad_block, left_stats, right_stats):
    order = grad_block.shape[0]
    strip = 64

    def body(busy_ref, grad_ref, left_ref, right_ref, left_out, right_out, wide, low, first):
        def one(stat_ref, out_ref, dims):
            grad = grad_ref[...]
            wide[...] = lax.dot_general(grad, grad, dims, preferred_element_type=jnp.float32)

            def shift(i, total):
                at = pl.ds(i * strip, strip)
                on_diagonal = lax.broadcasted_iota(
                    jnp.int32, (strip, order), 1
                ) == i * strip + lax.broadcasted_iota(jnp.int32, (strip, order), 0)
                shifted = stat_decay * stat_ref[at] + wide[at] / order
                shifted = shifted + jnp.where(on_diagonal, ridge_term, 0.0)
                wide[at] = shifted
                return total + jnp.sum(
                    (shifted * shifted).reshape(strip // 8, 8, order), axis=0
                )

            squares = lax.fori_loop(
                0, order // strip, shift, jnp.zeros((8, order), jnp.float32)
            )
            scale = jnp.sqrt(jnp.sum(squares, keepdims=True) + tiny_term)
            start = 1.0 / jnp.sqrt(jnp.sqrt(scale))

            def begin(i, carry):
                at = pl.ds(i * strip, strip)
                on_diagonal = lax.broadcasted_iota(
                    jnp.int32, (strip, order), 1
                ) == i * strip + lax.broadcasted_iota(jnp.int32, (strip, order), 0)
                matrix = wide[at] / scale
                factor = ((jnp.where(on_diagonal, 5.0, 0.0) - matrix) / 4.0).astype(jnp.bfloat16)
                low[0, at] = matrix.astype(jnp.bfloat16)
                low[1, at] = factor
                first[at] = (start * factor.astype(jnp.float32)).astype(jnp.bfloat16)
                return carry

            lax.fori_loop(0, order // strip, begin, 0)

            def dot(a, b):
                return jnp.dot(a, b, preferred_element_type=jnp.float32)

            low[2] = dot(low[1], low[1]).astype(jnp.bfloat16)
            low[1] = dot(low[2], low[2]).astype(jnp.bfloat16)
            wide[...] = dot(low[1], low[0])

            def again(i, carry):
                at = pl.ds(i * strip, strip)
                on_diagonal = lax.broadcasted_iota(
                    jnp.int32, (strip, order), 1
                ) == i * strip + lax.broadcasted_iota(jnp.int32, (strip, order), 0)
                low[2, at] = ((jnp.where(on_diagonal, 5.0, 0.0) - wide[at]) / 4.0).astype(
                    jnp.bfloat16
                )
                return carry

            lax.fori_loop(0, order // strip, again, 0)
            out_ref[...] = dot(first[...], low[2]).astype(jnp.bfloat16)

        @pl.when(busy_ref[0] == 1)
        def _():
            one(left_ref, left_out, (((1,), (1,)), ((), ())))
            one(right_ref, right_out, (((0,), (0,)), ((), ())))

        @pl.when(busy_ref[0] == 0)
        def _():
            left_out[...] = jnp.zeros_like(left_out)
            right_out[...] = jnp.zeros_like(right_out)

    root = jax.ShapeDtypeStruct((order, order), jnp.bfloat16)
    return pl.pallas_call(
        body,
        out_shape=(root, root),
        in_specs=[SMEM, VMEM, VMEM, VMEM],
        out_specs=(VMEM, VMEM),
        scratch_shapes=[
            pltpu.VMEM((order, order), jnp.float32),
            pltpu.VMEM((3, order, order), jnp.bfloat16),
            pltpu.VMEM((order, order), jnp.bfloat16),
        ],
        compiler_params=params(24),
        name="refresh",
    )(busy, grad_block, left_stats, right_stats)


def shards(gradient, owners, left_stats, right_stats, left_roots_old, right_roots_old):
    dp_count = lax.axis_size(DP)
    near_count = lax.axis_size(NEAR)
    my_index = lax.axis_index(DP)
    blocks_here = gradient.shape[1]
    row_count = gradient.shape[2]
    block_width = gradient.shape[3]
    is_mine = owners[0] == my_index
    busy = jnp.any(is_mine).astype(jnp.int32).reshape(1)
    mine = is_mine.astype(jnp.float32)
    masks = jnp.stack(
        [
            jnp.pad(mine, (0, LANES - blocks_here)),
            jnp.pad(mine, (blocks_here, LANES - 2 * blocks_here)),
        ]
    )
    outgoing = place_blocks(owners, gradient[0], dp_count)
    arrived = lax.all_to_all(outgoing, DP, split_axis=0, concat_axis=0, tiled=True)
    grad_block = arrived.reshape(dp_count * row_count, block_width)
    direction, norms = precondition(
        busy, masks, grad_block, left_roots_old[0, 0], right_roots_old[0, 0], near_count
    )
    near_norms = lax.all_to_all(norms, NEAR, split_axis=0, concat_axis=0, tiled=True)
    slots = add_norms(busy, near_norms, direction.reshape(dp_count, row_count, block_width))
    returned = lax.all_to_all(slots, DP, split_axis=0, concat_axis=0, tiled=True)
    left_root, right_root = refresh(busy, grad_block, left_stats[0, 0], right_stats[0, 0])
    update = scale_blocks(owners, returned)[None]
    return (update, left_root[None, None], right_root[None, None])


def solution(mesh):
    finer = Mesh(
        mesh.devices.reshape(2, 2, 8, 2, 4, 2),
        ("dp_0h", "dp_0l", "dp_1", "dp_2", "mp_0", "mp_1"),
    )
    placed = (
        P(MP, None, DP, None),
        P(MP, None),
        P(MP, DP, None, None),
        P(MP, DP, None, None),
        P(MP, DP, None, None),
        P(MP, DP, None, None),
    )
    return jax.shard_map(
        shards,
        mesh=finer,
        in_specs=placed,
        out_specs=(P(MP, None, DP, None), P(MP, DP, None, None), P(MP, DP, None, None)),
        check_vma=False,
    )
```

time: 138 us -> 86.6 us (0.63)
  blocking collectives: 43.5 us -> 11.7 us
  local copies, waits for them, and re-layouts: 14.5 us -> 1.69 us
  other arithmetic: 8.12 us -> 0.65 us
  Pallas kernels: 0 us -> 5.41 us
  matrix products: 4.02 us -> 0 us
  starting transfers between devices: 25.6 us -> 22.9 us
  waiting for transfers between devices: 40.6 us -> 42.7 us
    psum x5 -> x0, blocking collectives: 43.5 us -> none  [over_axes(): array = lax.psum(array, axis)]
    all_to_all x0 -> x1, blocking collectives: none -> 11.7 us  [shards(): lax.all_to_all(norms, NEAR, split_axis=0, concat_axis=0, tiled=True)]
    unnamed x16 -> x12, local copies, waits for them, and re-layouts: 9.46 us -> 1.61 us
    pallas_call x0 -> x5, Pallas kernels: none -> 5.41 us  [the longest x1 1.46 us: scale_blocks(): pl.pallas_call(body, out_shape=jax.ShapeDtypeStruct((blocks_here, row_cou...]
    dot_general x5 -> x0, matrix products: 4.02 us -> none  [the longest x1 1.54 us: shards(): jnp.dot(left_roots_old[0, 0], shaded, preferred_element_type=jnp.float32)]
    unnamed x1 -> x0, other arithmetic: 3.82 us -> none
    all_to_all x1 -> x0, local copies, waits for them, and re-layouts: 3.08 us -> none  [shards(): lax.all_to_all(scaled[None], DP, split_axis=1, concat_axis=0, tiled=True)]
    all_to_all x2, starting transfers between devices: 25.6 us -> 22.9 us  [the longest x1 18.3 us: shards(): lax.all_to_all(outgoing, DP, split_axis=0, concat_axis=0, tiled=True)]
  transfers between devices with their start and end apart: 2 -> 2, of which waited for: 2 -> 2; matrix products, arithmetic and copies ran while one was open for 3% -> 1% of each run, Pallas kernels for 0% -> 1%
where the time goes in v1:
time: 86.6 us; the launch traced here: 86.4 us
  waiting for transfers between devices  42.7 us (49%)
  starting transfers between devices  22.9 us (26%)
  blocking collectives  11.7 us (14%)
  Pallas kernels  5.41 us (6%)
  local copies, waits for them, and re-layouts  1.69 us (2%)
  between operations  1.35 us (2%)
    all_to_all x1, waiting for transfers between devices, shards(): lax.all_to_all(slots, DP, split_axis=0, concat_axis=0, tiled=True)  21.4 us
    all_to_all x1, waiting for transfers between devices, shards(): lax.all_to_all(outgoing, DP, split_axis=0, concat_axis=0, tiled=True)  21.4 us
    all_to_all x1, starting transfers between devices, shards(): lax.all_to_all(outgoing, DP, split_axis=0, concat_axis=0, tiled=True)  18.3 us
    all_to_all x1, blocking collectives, shards(): lax.all_to_all(norms, NEAR, split_axis=0, concat_axis=0, tiled=True)  11.7 us
    all_to_all x1, starting transfers between devices, shards(): lax.all_to_all(slots, DP, split_axis=0, concat_axis=0, tiled=True)  4.64 us
  transfers between devices with their start and end apart: 2, of which 2 were waited for; matrix products, arithmetic and copies ran while one was open for 1% of the time, Pallas kernels for 1%

profile of v1, /device:TPU:8, one launch (start us, length us, event | category | flops | bytes accessed | tf_op | source)
XLA Modules:
  0.0 86.4 jit_solution(6618419213557077111)
XLA Ops:
  0.6 0.0 copy-start.5
  0.6 0.6 copy-done.5
  1.3 0.0 copy-start.4
  1.3 0.9 %copy-done.4 = bf16[1,32,8,512]{3,2,1,0:T(8,128)(2,1)S(1)} copy-done((bf16[1,32,8,512]{3,2,1,0:T(8,128)(2,1)S(1)}, bf16[1,32,8,512]{3,2,1,0:T(8,128)(2,1)}, u32[]{:S(2)}) %copy-start.4) | copy-done | bytes 262168
  2.2 1.4 %place_blocks.1 = bf16[64,8,512]{2,1,0:T(8,128)(2,1)} custom-call(s32[1,32]{1,0:T(1,128)S(1)} %copy-done.5, bf16[32,8,512]{2,1,0:T(8,128)(2,1)S(1)} %bitcast.23), custom_call_target="tpu_custom_call" | custom-call | tf_op jit(solution)/shard_map/place_blocks/pallas_call | solution.py:44
  3.6 0.0 copy-start.2
  3.7 0.0 copy-start.3
  3.7 18.3 %all-to-all-start = ((bf16[64,8,512]{2,1,0:T(8,128)(2,1)}), bf16[64,8,512]{2,1,0:T(8,128)(2,1)S(1)}, u32[]{:S(2)}, u32[]{:S(2)}) async-start(bf16[64,8,512]{2,1,0:T(8,128)(2,1)} %place_blocks.1), calls=%async_computation | async-start | bytes 1048576 | tf_op jit(solution)/shard_map/all_to_all | solution.py:267
  21.9 0.6 fusion
  23.2 0.1 pad_bitcast_fusion.1
  23.3 21.4 %all-to-all-done = bf16[64,8,512]{2,1,0:T(8,128)(2,1)S(1)} async-done(((bf16[64,8,512]{2,1,0:T(8,128)(2,1)}), bf16[64,8,512]{2,1,0:T(8,128)(2,1)S(1)}, u32[]{:S(2)}, u32[]{:S(2)}) %all-to-all-start) | async-done | bytes 524320 | tf_op jit(solution)/shard_map/all_to_all | solution.py:267
  44.7 0.0 copy-done.2
  44.7 0.0 copy-done.3
  44.7 0.8 precondition.1
  45.5 11.7 %all_to_all.15.near_ref = f32[16,1,128]{2,1,0:T(1,128)S(1)} all-to-all(f32[16,1,128]{2,1,0:T(1,128)S(1)} %get-tuple-element.7), channel_id=1, replica_groups=mesh['dp_0h'=2,'dp_0l'=2,'dp_1'=8,'dp_2'=2,'mp_0'=4,'mp_1'=2] {'dp_0h','..., dimensions={0} | all-to-all | bytes 16384 | tf_op jit(solution)/shard_map/all_to_all | solution.py:272
  57.1 0.0 copy-start
  57.1 0.0 copy-start.1
  57.1 0.7 add_norms.1
  57.8 4.6 %all-to-all-start.2 = ((bf16[64,8,512]{2,1,0:T(8,128)(2,1)}), bf16[64,8,512]{2,1,0:T(8,128)(2,1)S(1)}, u32[]{:S(2)}, u32[]{:S(2)}) async-start(bf16[64,8,512]{2,1,0:T(8,128)(2,1)} %add_norms.1), calls=%async_computation.2 | async-start | bytes 1048576 | tf_op jit(solution)/shard_map/all_to_all | solution.py:274
  62.5 0.0 copy-done
  62.5 0.0 copy-done.1
  62.5 1.1 %refresh.1 = (bf16[512,512]{1,0:T(8,128)(2,1)}, bf16[512,512]{1,0:T(8,128)(2,1)}) custom-call(s32[1]{0:T(128)} %bitcast.busy_ref, bf16[512,512]{1,0:T(8,128)(2,1)S(1)} %bitcast.18, f32[512,512]{1,0:T(8,128)S(1)} %bitcast.19, f32[512,512]{1,0:T(8,128)S(1)} %bitcast.20), custom_call_target="tpu_custom_call" | custom-call | tf_op jit(solution)/shard_map/refresh/pallas_call | solution.py:235
  63.6 21.4 %all-to-all-done.2.slot_ref = bf16[64,8,512]{2,1,0:T(8,128)(2,1)S(1)} async-done(((bf16[64,8,512]{2,1,0:T(8,128)(2,1)}), bf16[64,8,512]{2,1,0:T(8,128)(2,1)S(1)}, u32[]{:S(2)}, u32[]{:S(2)}) %all-to-all-start.2) | async-done | bytes 524320 | tf_op jit(solution)/shard_map/all_to_all | solution.py:274
  84.9 1.5 %scale_blocks.1 = bf16[32,8,512]{2,1,0:T(8,128)(2,1)} custom-call(s32[1,32]{1,0:T(1,128)S(1)} %copy-done.5, bf16[64,8,512]{2,1,0:T(8,128)(2,1)S(1)} %all-to-all-done.2.slot_ref), custom_call_target="tpu_custom_call" | custom-call | tf_op jit(solution)/shard_map/scale_blocks/pallas_call | solution.py:153
  (1 shorter events, 0.0 us)
Async XLA Ops:
  0.6 0.7 copy-start.5
  1.3 0.9 %copy-start.4 = (bf16[1,32,8,512]{3,2,1,0:T(8,128)(2,1)S(1)}, bf16[1,32,8,512]{3,2,1,0:T(8,128)(2,1)}, u32[]{:S(2)}) copy-start(bf16[1,32,8,512]{3,2,1,0:T(8,128)(2,1)} %param.6) | copy-start | bytes 786436
  3.6 41.0 %copy-start.2 = (bf16[1,1,512,512]{3,2,1,0:T(8,128)(2,1)S(1)}, bf16[1,1,512,512]{3,2,1,0:T(8,128)(2,1)}, u32[]{:S(2)}) copy-start(bf16[1,1,512,512]{3,2,1,0:T(8,128)(2,1)} %param.10) | copy-start | bytes 1572868
  3.7 41.0 %copy-start.3 = (bf16[1,1,512,512]{3,2,1,0:T(8,128)(2,1)S(1)}, bf16[1,1,512,512]{3,2,1,0:T(8,128)(2,1)}, u32[]{:S(2)}) copy-start(bf16[1,1,512,512]{3,2,1,0:T(8,128)(2,1)} %param.11) | copy-start | bytes 1572868
  3.7 41.0 %all-to-all-start = ((bf16[64,8,512]{2,1,0:T(8,128)(2,1)}), bf16[64,8,512]{2,1,0:T(8,128)(2,1)S(1)}, u32[]{:S(2)}, u32[]{:S(2)}) async-start(bf16[64,8,512]{2,1,0:T(8,128)(2,1)} %place_blocks.1), calls=%async_computation | async-start | bytes 1048576 | tf_op jit(solution)/shard_map/all_to_all | solution.py:267
  57.1 5.4 %copy-start = (f32[1,1,512,512]{3,2,1,0:T(8,128)S(1)}, f32[1,1,512,512]{3,2,1,0:T(8,128)}, u32[]{:S(2)}) copy-start(f32[1,1,512,512]{3,2,1,0:T(8,128)} %param.8) | copy-start | bytes 3145732
  57.1 5.4 %copy-start.1 = (f32[1,1,512,512]{3,2,1,0:T(8,128)S(1)}, f32[1,1,512,512]{3,2,1,0:T(8,128)}, u32[]{:S(2)}) copy-start(f32[1,1,512,512]{3,2,1,0:T(8,128)} %param.9) | copy-start | bytes 3145732
  57.8 27.1 %all-to-all-start.2 = ((bf16[64,8,512]{2,1,0:T(8,128)(2,1)}), bf16[64,8,512]{2,1,0:T(8,128)(2,1)S(1)}, u32[]{:S(2)}, u32[]{:S(2)}) async-start(bf16[64,8,512]{2,1,0:T(8,128)(2,1)} %add_norms.1), calls=%async_computation.2 | async-start | bytes 1048576 | tf_op jit(solution)/shard_map/all_to_all | solution.py:274

commit v2 on v1

--- a/solution.py
+++ b/solution.py
@@ -10,6 +10,7 @@
 DP = ("dp_0h", "dp_0l", "dp_1", "dp_2")
 MP = ("mp_0", "mp_1")
 NEAR = ("dp_0h", "mp_0", "mp_1")
+PAIRS = ("dp_0l", "dp_1", "dp_2")
 LANES = 128
 MIB = 1024 * 1024
 
@@ -20,6 +21,7 @@
 
 SMEM = pl.BlockSpec(memory_space=pltpu.SMEM)
 VMEM = pl.BlockSpec(memory_space=pltpu.VMEM)
+ANY = pl.BlockSpec(memory_space=pl.ANY)
 
 
 def params(mib):
@@ -34,109 +36,136 @@
 def place_blocks(owners, blocks, dp_count):
     blocks_here, row_count, width = blocks.shape
 
-    def body(owner_ref, block_ref, slot_ref):
+    def body(owner_ref, block_ref, slot_ref, sems):
+        copies = []
         for j in range(blocks_here):
             owner = owner_ref[0, j]
-            rows = block_ref[j]
-            slot_ref[owner] = rows
-            slot_ref[partner_of(owner, dp_count)] = rows
+            for k, slot in enumerate((owner, partner_of(owner, dp_count))):
+                copy = pltpu.make_async_copy(block_ref.at[j], slot_ref.at[slot], sems.at[2 * j + k])
+                copy.start()
+                copies.append(copy)
+        for copy in copies:
+            copy.wait()
 
     return pl.pallas_call(
         body,
         out_shape=jax.ShapeDtypeStruct((dp_count, row_count, width), blocks.dtype),
-        in_specs=[SMEM, VMEM],
-        out_specs=VMEM,
-        compiler_params=params(4),
+        in_specs=[SMEM, ANY],
+        out_specs=ANY,
+        scratch_shapes=[pltpu.SemaphoreType.DMA((2 * blocks_here,))],
         name="place_blocks",
     )(owners, blocks)
 
 
-def precondition(busy, masks, grad_block, left, right, near_count):
-    def body(busy_ref, mask_ref, grad_ref, left_ref, right_ref, dir_ref, norm_ref):
-        @pl.when(busy_ref[0] == 1)
+def precondition(place, masks, grad_block, left, right, near_count, row_count):
+    order = grad_block.shape[0]
+    half = order // 2
+    slots = half // row_count
+
+    def body(place_ref, mask_ref, grad_ref, left_ref, right_ref, stay_ref, pass_ref, norm_ref):
+        @pl.when(place_ref[0] == 1)
         def _():
             grad = grad_ref[...]
             shaded = jnp.dot(grad, right_ref[...], preferred_element_type=jnp.float32)
-            direction = jnp.dot(
-                left_ref[...], shaded.astype(jnp.bfloat16), preferred_element_type=jnp.float32
-            ).astype(jnp.bfloat16)
-            dir_ref[...] = direction
+            shaded = shaded.astype(jnp.bfloat16)
+
+            def rows_of(which):
+                at = pl.ds(pl.multiple_of(which * half, half), half)
+                rows = jnp.dot(left_ref[at], shaded, preferred_element_type=jnp.float32)
+                return rows.astype(jnp.bfloat16)
+
+            passed = rows_of(1 - place_ref[1])
+            pass_ref[...] = passed.reshape(slots, row_count, order)
+            stays = rows_of(place_ref[1])
+            stay_ref[:, :, 0:order] = stays.reshape(slots, row_count, order)
             wide = grad.astype(jnp.float32)
             grad_square = jnp.sum(wide * wide, keepdims=True)
-            wide = direction.astype(jnp.float32)
+            wide = passed.astype(jnp.float32)
             dir_square = jnp.sum(wide * wide, keepdims=True)
+            wide = stays.astype(jnp.float32)
+            dir_square = dir_square + jnp.sum(wide * wide, keepdims=True)
             row = mask_ref[0:1] * grad_square + mask_ref[1:2] * dir_square
             norm_ref[...] = jnp.broadcast_to(row[None], norm_ref.shape)
 
-        @pl.when(busy_ref[0] == 0)
+        @pl.when(place_ref[0] == 0)
         def _():
             norm_ref[...] = jnp.zeros_like(norm_ref)
 
     return pl.pallas_call(
         body,
         out_shape=(
-            jax.ShapeDtypeStruct(grad_block.shape, jnp.bfloat16),
+            jax.ShapeDtypeStruct((slots, row_count, order + LANES), jnp.bfloat16),
+            jax.ShapeDtypeStruct((slots, row_count, order), jnp.bfloat16),
             jax.ShapeDtypeStruct((near_count, 1, LANES), jnp.float32),
         ),
         in_specs=[SMEM, VMEM, VMEM, VMEM, VMEM],
-        out_specs=(VMEM, VMEM),
+        out_specs=(VMEM, VMEM, VMEM),
         compiler_params=params(12),
         name="precondition",
-    )(busy, masks, grad_block, left, right)
-
-
-def add_norms(busy, near_norms, slots):
-    def body(busy_ref, near_ref, slot_ref, out_ref, rows_ref, sem):
+    )(place, masks, grad_block, left, right)
+
+
+def fill_slots(place, near_norms, passed, slots):
+    slot_count, row_count, width = slots.shape
+    order = width - LANES
+
+    def body(place_ref, near_ref, passed_ref, slot_ref, out_ref, rows_ref, sems):
         del slot_ref
-
-        @pl.when(busy_ref[0] == 0)
-        def _():
-            total = jnp.sum(near_ref[...], axis=0)
-            high = total.astype(jnp.bfloat16).astype(jnp.float32)
-            rest = total - high
-            middle = rest.astype(jnp.bfloat16).astype(jnp.float32)
-            low = rest - middle
-            row = lax.broadcasted_iota(jnp.int32, rows_ref.shape[1:], 0)
-            shape = rows_ref.shape[1:]
-            packed = jnp.where(
-                row == 0,
-                jnp.broadcast_to(high, shape),
-                jnp.where(
-                    row == 1,
-                    jnp.broadcast_to(middle, shape),
-                    jnp.where(row == 2, jnp.broadcast_to(low, shape), 0.0),
-                ),
-            ).astype(jnp.bfloat16)
-            rows_ref[...] = jnp.broadcast_to(packed[None], rows_ref.shape)
-            copy = pltpu.make_async_copy(rows_ref, out_ref.at[:, :, 0:LANES], sem)
-            copy.start()
-            copy.wait()
-
-    dp_count, row_count, _ = slots.shape
+        rows_copy = pltpu.make_async_copy(passed_ref, out_ref.at[:, :, 0:order], sems.at[0])
+
+        @pl.when(place_ref[0] == 0)
+        def _():
+            rows_copy.start()
+
+        total = jnp.sum(near_ref[...], axis=0)
+        high = total.astype(jnp.bfloat16).astype(jnp.float32)
+        rest = total - high
+        middle = rest.astype(jnp.bfloat16).astype(jnp.float32)
+        low = rest - middle
+        shape = rows_ref.shape[1:]
+        row = lax.broadcasted_iota(jnp.int32, shape, 0)
+        packed = jnp.where(
+            row == 0,
+            jnp.broadcast_to(high, shape),
+            jnp.where(
+                row == 1,
+                jnp.broadcast_to(middle, shape),
+                jnp.where(row == 2, jnp.broadcast_to(low, shape), 0.0),
+            ),
+        ).astype(jnp.bfloat16)
+        rows_ref[...] = jnp.broadcast_to(packed[None], rows_ref.shape)
+        norm_copy = pltpu.make_async_copy(rows_ref, out_ref.at[:, :, order:width], sems.at[1])
+        norm_copy.start()
+        norm_copy.wait()
+
+        @pl.when(place_ref[0] == 0)
+        def _():
+            rows_copy.wait()
+
     return pl.pallas_call(
         body,
         out_shape=jax.ShapeDtypeStruct(slots.shape, slots.dtype),
-        in_specs=[SMEM, VMEM, pl.BlockSpec(memory_space=pl.ANY)],
-        out_specs=pl.BlockSpec(memory_space=pl.ANY),
+        in_specs=[SMEM, VMEM, ANY, ANY],
+        out_specs=ANY,
         scratch_shapes=[
-            pltpu.VMEM((dp_count, row_count, LANES), slots.dtype),
-            pltpu.SemaphoreType.DMA,
+            pltpu.VMEM((slot_count, row_count, LANES), slots.dtype),
+            pltpu.SemaphoreType.DMA((2,)),
         ],
-        input_output_aliases={2: 0},
+        input_output_aliases={3: 0},
         compiler_params=params(4),
-        name="add_norms",
-    )(busy, near_norms, slots)
+        name="fill_slots",
+    )(place, near_norms, passed, slots)
 
 
 def scale_blocks(owners, slots):
     blocks_here = owners.shape[1]
-    dp_count, row_count, width = slots.shape
+    slot_count, row_count, width = slots.shape
+    order = width - LANES
 
     def body(owner_ref, slot_ref, out_ref):
         norms = jnp.zeros((row_count, LANES), jnp.float32)
-        for j in range(blocks_here):
-            idle = partner_of(owner_ref[0, j], dp_count)
-            norms = norms + slot_ref[idle, :, 0:LANES].astype(jnp.float32)
+        for p in range(slot_count):
+            norms = norms + slot_ref[p, :, order:width].astype(jnp.float32)
         totals = norms[0:1] + (norms[1:2] + norms[2:3])
         columns = jnp.broadcast_to(totals, (LANES, LANES)).T
         ratio = jnp.sqrt(
@@ -144,15 +173,16 @@
         )
         for j in range(blocks_here):
             owner = owner_ref[0, j]
+            slot = jnp.where(owner < slot_count, owner, owner - slot_count)
             scale = jnp.broadcast_to(ratio[j : j + 1], (row_count, LANES))
-            for c in range(width // LANES):
+            for c in range(order // LANES):
                 at = slice(c * LANES, (c + 1) * LANES)
-                rows = slot_ref[owner, :, at].astype(jnp.float32)
+                rows = slot_ref[slot, :, at].astype(jnp.float32)
                 out_ref[j, :, at] = (scale * rows).astype(out_ref.dtype)
 
     return pl.pallas_call(
         body,
-        out_shape=jax.ShapeDtypeStruct((blocks_here, row_count, width), slots.dtype),
+        out_shape=jax.ShapeDtypeStruct((blocks_here, row_count, order), slots.dtype),
         in_specs=[SMEM, VMEM],
         out_specs=VMEM,
         compiler_params=params(4),
@@ -160,11 +190,11 @@
     )(owners, slots)
 
 
-def refresh(busy, grad_block, left_stats, right_stats):
+def refresh(place, grad_block, left_stats, right_stats):
     order = grad_block.shape[0]
     strip = 64
 
-    def body(busy_ref, grad_ref, left_ref, right_ref, left_out, right_out, wide, low, first):
+    def body(place_ref, grad_ref, left_ref, right_ref, left_out, right_out, wide, low, first):
         def one(stat_ref, out_ref, dims):
             grad = grad_ref[...]
             wide[...] = lax.dot_general(grad, grad, dims, preferred_element_type=jnp.float32)
@@ -221,12 +251,12 @@
             lax.fori_loop(0, order // strip, again, 0)
             out_ref[...] = dot(first[...], low[2]).astype(jnp.bfloat16)
 
-        @pl.when(busy_ref[0] == 1)
+        @pl.when(place_ref[0] == 1)
         def _():
             one(left_ref, left_out, (((1,), (1,)), ((), ())))
             one(right_ref, right_out, (((0,), (0,)), ((), ())))
 
-        @pl.when(busy_ref[0] == 0)
+        @pl.when(place_ref[0] == 0)
         def _():
             left_out[...] = jnp.zeros_like(left_out)
             right_out[...] = jnp.zeros_like(right_out)
@@ -244,7 +274,7 @@
         ],
         compiler_params=params(24),
         name="refresh",
-    )(busy, grad_block, left_stats, right_stats)
+    )(place, grad_block, left_stats, right_stats)
 
 
 def shards(gradient, owners, left_stats, right_stats, left_roots_old, right_roots_old):
@@ -266,13 +296,15 @@
     outgoing = place_blocks(owners, gradient[0], dp_count)
     arrived = lax.all_to_all(outgoing, DP, split_axis=0, concat_axis=0, tiled=True)
     grad_block = arrived.reshape(dp_count * row_count, block_width)
-    direction, norms = precondition(
-        busy, masks, grad_block, left_roots_old[0, 0], right_roots_old[0, 0], near_count
-    )
+    place = jnp.concatenate([busy, lax.axis_index("dp_0h").astype(jnp.int32).reshape(1)])
+    stays, passes, norms = precondition(
+        place, masks, grad_block, left_roots_old[0, 0], right_roots_old[0, 0], near_count, row_count
+    )
+    passed = lax.ppermute(passes, "dp_0h", [(0, 1), (1, 0)])
     near_norms = lax.all_to_all(norms, NEAR, split_axis=0, concat_axis=0, tiled=True)
-    slots = add_norms(busy, near_norms, direction.reshape(dp_count, row_count, block_width))
-    returned = lax.all_to_all(slots, DP, split_axis=0, concat_axis=0, tiled=True)
-    left_root, right_root = refresh(busy, grad_block, left_stats[0, 0], right_stats[0, 0])
+    slots = fill_slots(place, near_norms, passed, stays)
+    returned = lax.all_to_all(slots, PAIRS, split_axis=0, concat_axis=0, tiled=True)
+    left_root, right_root = refresh(place, grad_block, left_stats[0, 0], right_stats[0, 0])
     update = scale_blocks(owners, returned)[None]
     return (update, left_root[None, None], right_root[None, None])
 

time: 86.6 us -> 102 us (1.18)
  Pallas kernels: 5.41 us -> 23.8 us
  waiting for transfers between devices: 42.7 us -> 36.7 us
  starting transfers between devices: 22.9 us -> 27.5 us
  blocking collectives: 11.7 us -> 10.1 us
    pallas_call x1, Pallas kernels: 1.41 us -> 18.2 us  [place_blocks(): pl.pallas_call(body, out_shape=jax.ShapeDtypeStruct((dp_count, row_count,...]
    all_to_all x1, waiting for transfers between devices: 21.4 us -> 16.1 us  [shards(): lax.all_to_all(slots, PAIRS, split_axis=0, concat_axis=0, tiled=True)]
    ppermute x0 -> x1, starting transfers between devices: none -> 4.57 us  [shards(): passed = lax.ppermute(passes, 'dp_0h', [(0, 1), (1, 0)])]
    all_to_all x1, blocking collectives: 11.7 us -> 10.1 us  [shards(): lax.all_to_all(norms, NEAR, split_axis=0, concat_axis=0, tiled=True)]
    pallas_call x2, Pallas kernels: 1.49 us -> 2.57 us  [the longest x1 1.29 us: fill_slots(): pl.pallas_call(body, out_shape=jax.ShapeDtypeStruct(slots.shape, slots.dt...]
  transfers between devices with their start and end apart: 2 -> 3, of which waited for: 2 -> 2; matrix products, arithmetic and copies ran while one was open for 1% -> 1% of each run, Pallas kernels for 1% -> 2%
where the time goes in v2:
time: 102 us; the launch traced here: 101 us
  waiting for transfers between devices  36.7 us (36%)
  starting transfers between devices  27.5 us (27%)
  Pallas kernels  23.8 us (23%)
  blocking collectives  10.1 us (10%)
  between operations  1.38 us (1%)
    all_to_all x1, waiting for transfers between devices, shards(): lax.all_to_all(outgoing, DP, split_axis=0, concat_axis=0, tiled=True)  20.6 us
    all_to_all x1, starting transfers between devices, shards(): lax.all_to_all(outgoing, DP, split_axis=0, concat_axis=0, tiled=True)  18.3 us
    pallas_call x1, Pallas kernels, place_blocks(): pl.pallas_call(body, out_shape=jax.ShapeDtypeStruct((dp_count, row_count,...  18.2 us
    all_to_all x1, waiting for transfers between devices, shards(): lax.all_to_all(slots, PAIRS, split_axis=0, concat_axis=0, tiled=True)  16.1 us
    all_to_all x1, blocking collectives, shards(): lax.all_to_all(norms, NEAR, split_axis=0, concat_axis=0, tiled=True)  10.1 us
    all_to_all x1, starting transfers between devices, shards(): lax.all_to_all(slots, PAIRS, split_axis=0, concat_axis=0, tiled=True)  4.66 us
    ppermute x1, starting transfers between devices, shards(): passed = lax.ppermute(passes, 'dp_0h', [(0, 1), (1, 0)])  4.57 us
  transfers between devices with their start and end apart: 3, of which 2 were waited for; matrix products, arithmetic and copies ran while one was open for 1% of the time, Pallas kernels for 2%

profile of v2, /device:TPU:8, one launch (start us, length us, event | category | flops | bytes accessed | tf_op | source)
XLA Modules:
  0.0 101.0 jit_solution(12138430550488447168)
XLA Ops:
  0.6 18.2 %place_blocks.1 = bf16[64,8,512]{2,1,0:T(8,128)(2,1)} custom-call(s32[1,32]{1,0:T(1,128)} %owner_ref.3, bf16[32,8,512]{2,1,0:T(8,128)(2,1)} %bitcast.24), custom_call_target="tpu_custom_call" | custom-call | tf_op jit(solution)/shard_map/place_blocks/pallas_call | solution.py:50
  18.9 0.0 copy-start.2
  18.9 0.0 copy-start.3
  18.9 18.3 %all-to-all-start = ((bf16[64,8,512]{2,1,0:T(8,128)(2,1)}), bf16[64,8,512]{2,1,0:T(8,128)(2,1)S(1)}, u32[]{:S(2)}, u32[]{:S(2)}) async-start(bf16[64,8,512]{2,1,0:T(8,128)(2,1)} %place_blocks.1), calls=%async_computation | async-start | bytes 1048576 | tf_op jit(solution)/shard_map/all_to_all | solution.py:297
  37.2 0.0 copy-start.4
  37.2 0.6 copy-done.4
  37.9 0.6 fusion
  39.2 0.1 pad_add_fusion.place_ref
  39.2 0.1 pad_bitcast_fusion.1
  39.3 20.6 %all-to-all-done = bf16[64,8,512]{2,1,0:T(8,128)(2,1)S(1)} async-done(((bf16[64,8,512]{2,1,0:T(8,128)(2,1)}), bf16[64,8,512]{2,1,0:T(8,128)(2,1)S(1)}, u32[]{:S(2)}, u32[]{:S(2)}) %all-to-all-start) | async-done | bytes 524320 | tf_op jit(solution)/shard_map/all_to_all | solution.py:297
  59.9 0.0 copy-done.2
  60.0 0.0 copy-done.3
  60.0 0.0 copy-start.1
  60.0 1.3 %precondition.1 = (bf16[32,8,640]{2,1,0:T(8,128)(2,1)}, bf16[32,8,512]{2,1,0:T(8,128)(2,1)S(1)}, f32[16,1,128]{2,1,0:T(1,128)S(1)}) custom-call(s32[2]{0:T(128)S(1)} %pad_add_fusion.place_ref, f32[2,128]{1,0:T(2,128)S(1)} %pad_maximum_fusion.mask_ref, bf16[512,512]{1,0:T(8,128)(2,1)S(1)} %bitcast.17, bf16[512,512]{1,0:T(8,128)(2,1)S(1)} %bitcast.21, ...), custom_call_target="tpu_custom_call" | custom-call | tf_op jit(solution)/shard_map/precondition/pallas_call | solution.py:94
  61.2 0.0 copy-start
  61.2 4.6 %collective-permute-start = (bf16[32,8,512]{2,1,0:T(8,128)(2,1)S(1)}, bf16[32,8,512]{2,1,0:T(8,128)(2,1)S(1)}, u32[]{:S(2)}, u32[]{:S(2)}) collective-permute-start(bf16[32,8,512]{2,1,0:T(8,128)(2,1)S(1)} %get-tuple-element.9), channel_id=1, source_target_pairs={{0,256},{256,0},{1,257},{257,1},{2,258},{258,2},{3,259},{259,3},{4... | collective-permute-start | bytes 786440 | tf_op jit(solution)/shard_map/ppermute | solution.py:303
  65.8 10.1 %all_to_all.15.near_ref = f32[16,1,128]{2,1,0:T(1,128)S(1)} all-to-all(f32[16,1,128]{2,1,0:T(1,128)S(1)} %get-tuple-element.8), channel_id=1, replica_groups=mesh['dp_0h'=2,'dp_0l'=2,'dp_1'=8,'dp_2'=2,'mp_0'=4,'mp_1'=2] {'dp_0h','..., dimensions={0} | all-to-all | bytes 16384 | tf_op jit(solution)/shard_map/all_to_all | solution.py:304
  75.9 0.0 collective-permute-done.passed_ref
  75.9 1.3 %fill_slots.1 = bf16[32,8,640]{2,1,0:T(8,128)(2,1)} custom-call(s32[2]{0:T(128)S(1)} %pad_add_fusion.place_ref, f32[16,1,128]{2,1,0:T(1,128)S(1)} %all_to_all.15.near_ref, bf16[32,8,512]{2,1,0:T(8,128)(2,1)S(1)} %collective-permute-done.passed_ref, bf16[32,8,640]{2,1,0:T(8,128)(2,1)} %get-tuple-element.10.slot_ref), custom_call_target="tpu_custom_call", output_to_operand_aliasing={{}: (3, {})} | custom-call | tf_op jit(solution)/shard_map/fill_slots/pallas_call | solution.py:145
  77.2 4.7 %all-to-all-start.2 = ((bf16[32,8,640]{2,1,0:T(8,128)(2,1)}), bf16[32,8,640]{2,1,0:T(8,128)(2,1)S(1)}, u32[]{:S(2)}, u32[]{:S(2)}) async-start(bf16[32,8,640]{2,1,0:T(8,128)(2,1)} %fill_slots.1), calls=%async_computation.2 | async-start | bytes 655360 | tf_op jit(solution)/shard_map/all_to_all | solution.py:306
  81.9 0.0 copy-done.1
  81.9 0.0 copy-done
  81.9 1.6 %refresh.1 = (bf16[512,512]{1,0:T(8,128)(2,1)}, bf16[512,512]{1,0:T(8,128)(2,1)}) custom-call(s32[2]{0:T(128)S(1)} %pad_add_fusion.place_ref, bf16[512,512]{1,0:T(8,128)(2,1)S(1)} %bitcast.18, f32[512,512]{1,0:T(8,128)S(1)} %bitcast.19, f32[512,512]{1,0:T(8,128)S(1)} %bitcast.20), custom_call_target="tpu_custom_call" | custom-call | tf_op jit(solution)/shard_map/refresh/pallas_call | solution.py:265
  83.5 16.1 %all-to-all-done.2.slot_ref = bf16[32,8,640]{2,1,0:T(8,128)(2,1)S(1)} async-done(((bf16[32,8,640]{2,1,0:T(8,128)(2,1)}), bf16[32,8,640]{2,1,0:T(8,128)(2,1)S(1)}, u32[]{:S(2)}, u32[]{:S(2)}) %all-to-all-start.2) | async-done | bytes 327712 | tf_op jit(solution)/shard_map/all_to_all | solution.py:306
  99.6 1.4 %scale_blocks.1 = bf16[32,8,512]{2,1,0:T(8,128)(2,1)} custom-call(s32[1,32]{1,0:T(1,128)S(1)} %copy-done.4, bf16[32,8,640]{2,1,0:T(8,128)(2,1)S(1)} %all-to-all-done.2.slot_ref), custom_call_target="tpu_custom_call" | custom-call | tf_op jit(solution)/shard_map/scale_blocks/pallas_call | solution.py:183
  (1 shorter events, 0.0 us)
Async XLA Ops:
  18.9 41.1 %copy-start.2 = (bf16[1,1,512,512]{3,2,1,0:T(8,128)(2,1)S(1)}, bf16[1,1,512,512]{3,2,1,0:T(8,128)(2,1)}, u32[]{:S(2)}) copy-start(bf16[1,1,512,512]{3,2,1,0:T(8,128)(2,1)} %param.10) | copy-start | bytes 1572868
  18.9 41.1 %copy-start.3 = (bf16[1,1,512,512]{3,2,1,0:T(8,128)(2,1)S(1)}, bf16[1,1,512,512]{3,2,1,0:T(8,128)(2,1)}, u32[]{:S(2)}) copy-start(bf16[1,1,512,512]{3,2,1,0:T(8,128)(2,1)} %param.11) | copy-start | bytes 1572868
  18.9 41.0 %all-to-all-start = ((bf16[64,8,512]{2,1,0:T(8,128)(2,1)}), bf16[64,8,512]{2,1,0:T(8,128)(2,1)S(1)}, u32[]{:S(2)}, u32[]{:S(2)}) async-start(bf16[64,8,512]{2,1,0:T(8,128)(2,1)} %place_blocks.1), calls=%async_computation | async-start | bytes 1048576 | tf_op jit(solution)/shard_map/all_to_all | solution.py:297
  37.2 0.7 copy-start.4
  60.0 21.9 %copy-start.1 = (f32[1,1,512,512]{3,2,1,0:T(8,128)S(1)}, f32[1,1,512,512]{3,2,1,0:T(8,128)}, u32[]{:S(2)}) copy-start(f32[1,1,512,512]{3,2,1,0:T(8,128)} %param.9) | copy-start | bytes 3145732
  61.2 20.6 %copy-start = (f32[1,1,512,512]{3,2,1,0:T(8,128)S(1)}, f32[1,1,512,512]{3,2,1,0:T(8,128)}, u32[]{:S(2)}) copy-start(f32[1,1,512,512]{3,2,1,0:T(8,128)} %param.8) | copy-start | bytes 3145732
  61.2 14.7 %collective-permute-start = (bf16[32,8,512]{2,1,0:T(8,128)(2,1)S(1)}, bf16[32,8,512]{2,1,0:T(8,128)(2,1)S(1)}, u32[]{:S(2)}, u32[]{:S(2)}) collective-permute-start(bf16[32,8,512]{2,1,0:T(8,128)(2,1)S(1)} %get-tuple-element.9), channel_id=1, source_target_pairs={{0,256},{256,0},{1,257},{257,1},{2,258},{258,2},{3,259},{259,3},{4... | collective-permute-start | bytes 786440 | tf_op jit(solution)/shard_map/ppermute | solution.py:303
  77.2 22.4 %all-to-all-start.2 = ((bf16[32,8,640]{2,1,0:T(8,128)(2,1)}), bf16[32,8,640]{2,1,0:T(8,128)(2,1)S(1)}, u32[]{:S(2)}, u32[]{:S(2)}) async-start(bf16[32,8,640]{2,1,0:T(8,128)(2,1)} %fill_slots.1), calls=%async_computation.2 | async-start | bytes 655360 | tf_op jit(solution)/shard_map/all_to_all | solution.py:306

commit v3 on v2

v3 whole, which is shorter than its diff:
```python
import jax
import jax.numpy as jnp
from jax import lax
from jax.experimental import pallas as pl
from jax.experimental.pallas import tpu as pltpu
from jax.sharding import Mesh
from jax.sharding import PartitionSpec as P

ITERS = 2
DP = ("dp_0h", "dp_0l", "dp_1", "dp_2")
MP = ("mp_0", "mp_1")
LANES = 128
MIB = 1024 * 1024


stat_decay = 0.9
ridge_term = 0.001
tiny_term = 1e-06

SMEM = pl.BlockSpec(memory_space=pltpu.SMEM)
VMEM = pl.BlockSpec(memory_space=pltpu.VMEM)
ANY = pl.BlockSpec(memory_space=pl.ANY)


def params(mib):
    return pltpu.CompilerParams(vmem_limit_bytes=mib * MIB)


def partner_of(owner, dp_count):
    half = dp_count // 2
    return jnp.where(owner < half, owner + half, owner - half)


def place_blocks(owners, my_index, blocks, dp_count):
    blocks_here, row_count, width = blocks.shape

    def body(owner_ref, index_ref, block_ref, slot_ref, flag_ref):
        busy = jnp.int32(0)
        mine = jnp.int32(0)
        for j in range(blocks_here):
            owner = owner_ref[0, j]
            rows = block_ref[j]
            slot_ref[owner] = rows
            slot_ref[partner_of(owner, dp_count)] = rows
            here = (owner == index_ref[0]).astype(jnp.int32)
            busy = busy + here
            mine = mine + here * j
        flag_ref[0] = busy
        flag_ref[1] = mine

    return pl.pallas_call(
        body,
        out_shape=(
            jax.ShapeDtypeStruct((dp_count, row_count, width), blocks.dtype),
            jax.ShapeDtypeStruct((2,), jnp.int32),
        ),
        in_specs=[SMEM, SMEM, VMEM],
        out_specs=(VMEM, SMEM),
        compiler_params=params(4),
        name="place_blocks",
    )(owners, my_index, blocks)


def precondition(flags, grad_block, left, right, blocks_here, mp_count, row_count):
    order = grad_block.shape[0]
    half = order // 2
    slots = order // row_count

    def body(flag_ref, grad_ref, left_ref, right_ref, stay_ref, pass_ref, norm_ref):
        @pl.when(flag_ref[0] == 1)
        def _():
            grad = grad_ref[...]
            shaded = jnp.dot(grad, right_ref[...], preferred_element_type=jnp.float32)
            direction = jnp.dot(
                left_ref[...], shaded.astype(jnp.bfloat16), preferred_element_type=jnp.float32
            ).astype(jnp.bfloat16)
            pass_ref[...] = direction[:, half:].reshape(slots, row_count, half)
            stay_ref[:, :, 0:half] = direction[:, :half].reshape(slots, row_count, half)
            wide = grad.astype(jnp.float32)
            grad_square = jnp.sum(wide * wide, keepdims=True)
            wide = direction.astype(jnp.float32)
            dir_square = jnp.sum(wide * wide, keepdims=True)
            lane = lax.broadcasted_iota(jnp.int32, (1, LANES), 1)
            row = jnp.where(lane == flag_ref[1], grad_square, 0.0)
            row = row + jnp.where(lane == flag_ref[1] + blocks_here, dir_square, 0.0)
            norm_ref[...] = jnp.broadcast_to(row[None], norm_ref.shape)

        @pl.when(flag_ref[0] == 0)
        def _():
            norm_ref[...] = jnp.zeros_like(norm_ref)

    return pl.pallas_call(
        body,
        out_shape=(
            jax.ShapeDtypeStruct((slots, row_count, half + LANES), jnp.bfloat16),
            jax.ShapeDtypeStruct((slots, row_count, half), jnp.bfloat16),
            jax.ShapeDtypeStruct((mp_count, 1, LANES), jnp.float32),
        ),
        in_specs=[SMEM, VMEM, VMEM, VMEM],
        out_specs=(VMEM, VMEM, VMEM),
        compiler_params=params(12),
        name="precondition",
    )(flags, grad_block, left, right)


def fill_slots(flags, row_norms, passed, slots):
    slot_count, row_count, width = slots.shape
    half = width - LANES

    def body(flag_ref, norm_ref, passed_ref, slot_ref, out_ref, rows_ref, sems):
        del slot_ref
        passed_copy = pltpu.make_async_copy(passed_ref, out_ref.at[:, :, 0:half], sems.at[0])

        @pl.when(flag_ref[0] == 0)
        def _():
            passed_copy.start()

        total = jnp.sum(norm_ref[...], axis=0)
        high = total.astype(jnp.bfloat16).astype(jnp.float32)
        rest = total - high
        middle = rest.astype(jnp.bfloat16).astype(jnp.float32)
        low = rest - middle
        shape = rows_ref.shape[1:]
        row = lax.broadcasted_iota(jnp.int32, shape, 0)
        packed = jnp.where(
            row == 0,
            jnp.broadcast_to(high, shape),
            jnp.where(
                row == 1,
                jnp.broadcast_to(middle, shape),
                jnp.where(row == 2, jnp.broadcast_to(low, shape), 0.0),
            ),
        ).astype(jnp.bfloat16)
        rows_ref[...] = jnp.broadcast_to(packed[None], rows_ref.shape)
        norm_copy = pltpu.make_async_copy(rows_ref, out_ref.at[:, :, half:width], sems.at[1])
        norm_copy.start()
        norm_copy.wait()

        @pl.when(flag_ref[0] == 0)
        def _():
            passed_copy.wait()

    return pl.pallas_call(
        body,
        out_shape=jax.ShapeDtypeStruct(slots.shape, slots.dtype),
        in_specs=[SMEM, VMEM, ANY, ANY],
        out_specs=ANY,
        scratch_shapes=[
            pltpu.VMEM((slot_count, row_count, LANES), slots.dtype),
            pltpu.SemaphoreType.DMA((2,)),
        ],
        input_output_aliases={3: 0},
        compiler_params=params(4),
        name="fill_slots",
    )(flags, row_norms, passed, slots)


def scale_blocks(owners, slots):
    blocks_here = owners.shape[1]
    slot_count, row_count, width = slots.shape
    half = width - LANES

    def body(owner_ref, slot_ref, out_ref):
        norms = jnp.zeros((row_count, LANES), jnp.float32)
        for p in range(slot_count):
            norms = norms + slot_ref[p, :, half:width].astype(jnp.float32)
        totals = norms[0:1] + (norms[1:2] + norms[2:3])
        columns = jnp.broadcast_to(totals, (LANES, LANES)).T
        ratio = jnp.sqrt(
            columns[:blocks_here] / (columns[blocks_here : 2 * blocks_here] + tiny_term)
        )
        for j in range(blocks_here):
            owner = owner_ref[0, j]
            scale = jnp.broadcast_to(ratio[j : j + 1], (row_count, LANES))
            for k, slot in enumerate((owner, partner_of(owner, slot_count))):
                for c in range(0, half, LANES):
                    rows = slot_ref[slot, :, c : c + LANES].astype(jnp.float32)
                    at = slice(k * half + c, k * half + c + LANES)
                    out_ref[j, :, at] = (scale * rows).astype(out_ref.dtype)

    return pl.pallas_call(
        body,
        out_shape=jax.ShapeDtypeStruct((blocks_here, row_count, 2 * half), slots.dtype),
        in_specs=[SMEM, VMEM],
        out_specs=VMEM,
        compiler_params=params(4),
        name="scale_blocks",
    )(owners, slots)


def refresh(flags, grad_block, left_stats, right_stats):
    order = grad_block.shape[0]
    strip = 64

    def body(flag_ref, grad_ref, left_ref, right_ref, left_out, right_out, wide, low, first):
        def one(stat_ref, out_ref, dims):
            grad = grad_ref[...]
            wide[...] = lax.dot_general(grad, grad, dims, preferred_element_type=jnp.float32)

            def shift(i, total):
                at = pl.ds(i * strip, strip)
                on_diagonal = lax.broadcasted_iota(
                    jnp.int32, (strip, order), 1
                ) == i * strip + lax.broadcasted_iota(jnp.int32, (strip, order), 0)
                shifted = stat_decay * stat_ref[at] + wide[at] / order
                shifted = shifted + jnp.where(on_diagonal, ridge_term, 0.0)
                wide[at] = shifted
                return total + jnp.sum(
                    (shifted * shifted).reshape(strip // 8, 8, order), axis=0
                )

            squares = lax.fori_loop(
                0, order // strip, shift, jnp.zeros((8, order), jnp.float32)
            )
            scale = jnp.sqrt(jnp.sum(squares, keepdims=True) + tiny_term)
            start = 1.0 / jnp.sqrt(jnp.sqrt(scale))

            def begin(i, carry):
                at = pl.ds(i * strip, strip)
                on_diagonal = lax.broadcasted_iota(
                    jnp.int32, (strip, order), 1
                ) == i * strip + lax.broadcasted_iota(jnp.int32, (strip, order), 0)
                matrix = wide[at] / scale
                factor = ((jnp.where(on_diagonal, 5.0, 0.0) - matrix) / 4.0).astype(jnp.bfloat16)
                low[0, at] = matrix.astype(jnp.bfloat16)
                low[1, at] = factor
                first[at] = (start * factor.astype(jnp.float32)).astype(jnp.bfloat16)
                return carry

            lax.fori_loop(0, order // strip, begin, 0)

            def dot(a, b):
                return jnp.dot(a, b, preferred_element_type=jnp.float32)

            low[2] = dot(low[1], low[1]).astype(jnp.bfloat16)
            low[1] = dot(low[2], low[2]).astype(jnp.bfloat16)
            wide[...] = dot(low[1], low[0])

            def again(i, carry):
                at = pl.ds(i * strip, strip)
                on_diagonal = lax.broadcasted_iota(
                    jnp.int32, (strip, order), 1
                ) == i * strip + lax.broadcasted_iota(jnp.int32, (strip, order), 0)
                low[2, at] = ((jnp.where(on_diagonal, 5.0, 0.0) - wide[at]) / 4.0).astype(
                    jnp.bfloat16
                )
                return carry

            lax.fori_loop(0, order // strip, again, 0)
            out_ref[...] = dot(first[...], low[2]).astype(jnp.bfloat16)

        @pl.when(flag_ref[0] == 1)
        def _():
            one(left_ref, left_out, (((1,), (1,)), ((), ())))
            one(right_ref, right_out, (((0,), (0,)), ((), ())))

        @pl.when(flag_ref[0] == 0)
        def _():
            left_out[...] = jnp.zeros_like(left_out)
            right_out[...] = jnp.zeros_like(right_out)

    root = jax.ShapeDtypeStruct((order, order), jnp.bfloat16)
    return pl.pallas_call(
        body,
        out_shape=(root, root),
        in_specs=[SMEM, VMEM, VMEM, VMEM],
        out_specs=(VMEM, VMEM),
        scratch_shapes=[
            pltpu.VMEM((order, order), jnp.float32),
            pltpu.VMEM((3, order, order), jnp.bfloat16),
            pltpu.VMEM((order, order), jnp.bfloat16),
        ],
        compiler_params=params(24),
        name="refresh",
    )(flags, grad_block, left_stats, right_stats)


def shards(gradient, owners, left_stats, right_stats, left_roots_old, right_roots_old):
    dp_count = lax.axis_size(DP)
    mp_count = lax.axis_size(MP)
    my_index = lax.axis_index(DP).astype(jnp.int32).reshape(1)
    blocks_here = gradient.shape[1]
    row_count = gradient.shape[2]
    block_width = gradient.shape[3]
    outgoing, flags = place_blocks(owners, my_index, gradient[0], dp_count)
    arrived = lax.all_to_all(outgoing, DP, split_axis=0, concat_axis=0, tiled=True)
    grad_block = arrived.reshape(dp_count * row_count, block_width)
    stays, passes, norms = precondition(
        flags, grad_block, left_roots_old[0, 0], right_roots_old[0, 0], blocks_here, mp_count, row_count
    )
    passed = lax.ppermute(passes, "dp_0h", [(0, 1), (1, 0)])
    row_norms = lax.all_to_all(norms, MP, split_axis=0, concat_axis=0, tiled=True)
    slots = fill_slots(flags, row_norms, passed, stays)
    returned = lax.all_to_all(slots, DP, split_axis=0, concat_axis=0, tiled=True)
    left_root, right_root = refresh(flags, grad_block, left_stats[0, 0], right_stats[0, 0])
    update = scale_blocks(owners, returned)[None]
    return (update, left_root[None, None], right_root[None, None])


def solution(mesh):
    finer = Mesh(
        mesh.devices.reshape(2, 2, 8, 2, 4, 2),
        ("dp_0h", "dp_0l", "dp_1", "dp_2", "mp_0", "mp_1"),
    )
    placed = (
        P(MP, None, DP, None),
        P(MP, None),
        P(MP, DP, None, None),
        P(MP, DP, None, None),
        P(MP, DP, None, None),
        P(MP, DP, None, None),
    )
    return jax.shard_map(
        shards,
        mesh=finer,
        in_specs=placed,
        out_specs=(P(MP, None, DP, None), P(MP, DP, None, None), P(MP, DP, None, None)),
        check_vma=False,
    )
```

time: 102 us -> 86.3 us (0.85)
  blocking collectives: 10.1 us -> 49.2 us
  waiting for transfers between devices: 36.7 us -> 12.5 us
  starting transfers between devices: 27.5 us -> 8.26 us
  Pallas kernels: 23.8 us -> 13.7 us
    all_to_all x1 -> x2, blocking collectives: 10.1 us -> 49.2 us  [the longest x1 40.8 us: shards(): lax.all_to_all(outgoing, DP, split_axis=0, concat_axis=0, tiled=True)]
    all_to_all x2 -> x1, waiting for transfers between devices: 36.7 us -> 12.5 us  [shards(): lax.all_to_all(slots, DP, split_axis=0, concat_axis=0, tiled=True)]
    all_to_all x2 -> x1, starting transfers between devices: 22.9 us -> 5.73 us  [shards(): lax.all_to_all(slots, DP, split_axis=0, concat_axis=0, tiled=True)]
    pallas_call x2, Pallas kernels: 19.5 us -> 3.62 us  [the longest x1 2.35 us: precondition(): pl.pallas_call(body, out_shape=(jax.ShapeDtypeStruct((slots, row_count, h...]
    pallas_call x1, Pallas kernels: 1.59 us -> 7.39 us  [refresh(): pl.pallas_call(body, out_shape=(root, root), in_specs=[SMEM, VMEM, VMEM,...]
    ppermute x1, starting transfers between devices: 4.57 us -> 2.53 us  [shards(): passed = lax.ppermute(passes, 'dp_0h', [(0, 1), (1, 0)])]
  transfers between devices with their start and end apart: 3 -> 2, of which waited for: 2 -> 1; matrix products, arithmetic and copies ran while one was open for 1% -> 0% of each run, Pallas kernels for 2% -> 9%
where the time goes in v3:
time: 86.3 us; the launch traced here: 86 us
  blocking collectives  49.2 us (57%)
  Pallas kernels  13.7 us (16%)
  waiting for transfers between devices  12.5 us (14%)
  starting transfers between devices  8.26 us (10%)
  local copies, waits for them, and re-layouts  1.62 us (2%)
    all_to_all x1, blocking collectives, shards(): lax.all_to_all(outgoing, DP, split_axis=0, concat_axis=0, tiled=True)  40.8 us
    all_to_all x1, waiting for transfers between devices, shards(): lax.all_to_all(slots, DP, split_axis=0, concat_axis=0, tiled=True)  12.5 us
    all_to_all x1, blocking collectives, shards(): lax.all_to_all(norms, MP, split_axis=0, concat_axis=0, tiled=True)  8.42 us
    pallas_call x1, Pallas kernels, refresh(): pl.pallas_call(body, out_shape=(root, root), in_specs=[SMEM, VMEM, VMEM,...  7.39 us
    all_to_all x1, starting transfers between devices, shards(): lax.all_to_all(slots, DP, split_axis=0, concat_axis=0, tiled=True)  5.73 us
    ppermute x1, starting transfers between devices, shards(): passed = lax.ppermute(passes, 'dp_0h', [(0, 1), (1, 0)])  2.53 us
    pallas_call x1, Pallas kernels, precondition(): pl.pallas_call(body, out_shape=(jax.ShapeDtypeStruct((slots, row_count, h...  2.35 us
  transfers between devices with their start and end apart: 2, of which 1 were waited for; matrix products, arithmetic and copies ran while one was open for 0% of the time, Pallas kernels for 9%

profile of v3, /device:TPU:8, one launch (start us, length us, event | category | flops | bytes accessed | tf_op | source)
XLA Modules:
  0.0 86.0 jit_solution(2470054212598890570)
XLA Ops:
  0.6 0.0 copy-start.5
  0.7 0.6 copy-done.5
  1.3 0.0 copy-start.4
  1.3 0.9 %copy-done.4 = bf16[1,32,8,512]{3,2,1,0:T(8,128)(2,1)S(1)} copy-done((bf16[1,32,8,512]{3,2,1,0:T(8,128)(2,1)S(1)}, bf16[1,32,8,512]{3,2,1,0:T(8,128)(2,1)}, u32[]{:S(2)}) %copy-start.4) | copy-done | bytes 262168
  2.2 1.3 %place_blocks.1 = (bf16[64,8,512]{2,1,0:T(8,128)(2,1)S(1)}, s32[2]{0:T(128)S(1)}) custom-call(s32[1,32]{1,0:T(1,128)S(1)} %copy-done.5, s32[1]{0:T(128)} %bitcast.index_ref, bf16[32,8,512]{2,1,0:T(8,128)(2,1)S(1)} %bitcast.16), custom_call_target="tpu_custom_call" | custom-call | tf_op jit(solution)/shard_map/place_blocks/pallas_call | solution.py:51
  3.5 0.0 copy-start.2
  3.5 0.0 copy-start.3
  3.6 40.8 %all_to_all.15 = bf16[64,8,512]{2,1,0:T(8,128)(2,1)S(1)} all-to-all(bf16[64,8,512]{2,1,0:T(8,128)(2,1)S(1)} %get-tuple-element.11), channel_id=1, replica_groups=mesh['dp_0h'=2,'dp_0l'=2,'dp_1'=8,'dp_2'=2,'mp_0'=4,'mp_1'=2] {'dp_0h','..., dimensions={0} | all-to-all | bytes 1048576 | tf_op jit(solution)/shard_map/all_to_all | solution.py:286
  44.4 0.0 copy-done.2
  44.4 0.0 copy-done.3
  44.4 0.0 copy-start.1
  44.4 2.3 %precondition.1 = (bf16[64,8,384]{2,1,0:T(8,128)(2,1)}, bf16[64,8,256]{2,1,0:T(8,128)(2,1)S(1)}, f32[8,1,128]{2,1,0:T(1,128)S(1)}) custom-call(s32[2]{0:T(128)S(1)} %get-tuple-element.10.flag_ref, bf16[512,512]{1,0:T(8,128)(2,1)S(1)} %bitcast.10, bf16[512,512]{1,0:T(8,128)(2,1)S(1)} %bitcast.14, bf16[512,512]{1,0:T(8,128)(2,1)S(1)} %bitcast.15), custom_call_target="tpu_custom_call" | custom-call | tf_op jit(solution)/shard_map/precondition/pallas_call | solution.py:92
  46.7 0.0 copy-start
  46.7 2.5 %collective-permute-start = (bf16[64,8,256]{2,1,0:T(8,128)(2,1)S(1)}, bf16[64,8,256]{2,1,0:T(8,128)(2,1)S(1)}, u32[]{:S(2)}, u32[]{:S(2)}) collective-permute-start(bf16[64,8,256]{2,1,0:T(8,128)(2,1)S(1)} %get-tuple-element.13), channel_id=1, source_target_pairs={{0,256},{256,0},{1,257},{257,1},{2,258},{258,2},{3,259},{259,3},{4... | collective-permute-start | bytes 786440 | tf_op jit(solution)/shard_map/ppermute | solution.py:291
  49.3 8.4 %all_to_all.16.norm_ref = f32[8,1,128]{2,1,0:T(1,128)S(1)} all-to-all(f32[8,1,128]{2,1,0:T(1,128)S(1)} %get-tuple-element.12), channel_id=1, replica_groups=mesh['dp_0h'=2,'dp_0l'=2,'dp_1'=8,'dp_2'=2,'mp_0'=4,'mp_1'=2] {'mp_0','m..., dimensions={0} | all-to-all | bytes 8192 | tf_op jit(solution)/shard_map/all_to_all | solution.py:292
  57.7 0.0 collective-permute-done.passed_ref
  57.7 1.3 %fill_slots.1 = bf16[64,8,384]{2,1,0:T(8,128)(2,1)} custom-call(s32[2]{0:T(128)S(1)} %get-tuple-element.10.flag_ref, f32[8,1,128]{2,1,0:T(1,128)S(1)} %all_to_all.16.norm_ref, bf16[64,8,256]{2,1,0:T(8,128)(2,1)S(1)} %collective-permute-done.passed_ref, bf16[64,8,384]{2,1,0:T(8,128)(2,1)} %get-tuple-element.14.slot_ref), custom_call_target="tpu_custom_call", output_to_operand_aliasing={{}: (3, {})} | custom-call | tf_op jit(solution)/shard_map/fill_slots/pallas_call | solution.py:143
  59.0 5.7 %all-to-all-start.2 = ((bf16[64,8,384]{2,1,0:T(8,128)(2,1)}), bf16[64,8,384]{2,1,0:T(8,128)(2,1)S(1)}, u32[]{:S(2)}, u32[]{:S(2)}) async-start(bf16[64,8,384]{2,1,0:T(8,128)(2,1)} %fill_slots.1), calls=%async_computation.2 | async-start | bytes 786432 | tf_op jit(solution)/shard_map/all_to_all | solution.py:294
  64.7 0.0 copy-done.1
  64.7 0.0 copy-done
  64.7 7.4 %refresh.1 = (bf16[512,512]{1,0:T(8,128)(2,1)}, bf16[512,512]{1,0:T(8,128)(2,1)}) custom-call(s32[2]{0:T(128)S(1)} %get-tuple-element.10.flag_ref, bf16[512,512]{1,0:T(8,128)(2,1)S(1)} %bitcast.11, f32[512,512]{1,0:T(8,128)S(1)} %bitcast.12, f32[512,512]{1,0:T(8,128)S(1)} %bitcast.13), custom_call_target="tpu_custom_call" | custom-call | tf_op jit(solution)/shard_map/refresh/pallas_call | solution.py:263
  72.1 12.5 %all-to-all-done.2.slot_ref = bf16[64,8,384]{2,1,0:T(8,128)(2,1)S(1)} async-done(((bf16[64,8,384]{2,1,0:T(8,128)(2,1)}), bf16[64,8,384]{2,1,0:T(8,128)(2,1)S(1)}, u32[]{:S(2)}, u32[]{:S(2)}) %all-to-all-start.2) | async-done | bytes 393248 | tf_op jit(solution)/shard_map/all_to_all | solution.py:294
  84.6 1.5 %scale_blocks.1 = bf16[32,8,512]{2,1,0:T(8,128)(2,1)} custom-call(s32[1,32]{1,0:T(1,128)S(1)} %copy-done.5, bf16[64,8,384]{2,1,0:T(8,128)(2,1)S(1)} %all-to-all-done.2.slot_ref), custom_call_target="tpu_custom_call" | custom-call | tf_op jit(solution)/shard_map/scale_blocks/pallas_call | solution.py:181
Async XLA Ops:
  0.6 0.7 copy-start.5
  1.3 0.9 %copy-start.4 = (bf16[1,32,8,512]{3,2,1,0:T(8,128)(2,1)S(1)}, bf16[1,32,8,512]{3,2,1,0:T(8,128)(2,1)}, u32[]{:S(2)}) copy-start(bf16[1,32,8,512]{3,2,1,0:T(8,128)(2,1)} %param.6) | copy-start | bytes 786436
  3.5 40.9 %copy-start.2 = (bf16[1,1,512,512]{3,2,1,0:T(8,128)(2,1)S(1)}, bf16[1,1,512,512]{3,2,1,0:T(8,128)(2,1)}, u32[]{:S(2)}) copy-start(bf16[1,1,512,512]{3,2,1,0:T(8,128)(2,1)} %param.10) | copy-start | bytes 1572868
  3.5 40.8 %copy-start.3 = (bf16[1,1,512,512]{3,2,1,0:T(8,128)(2,1)S(1)}, bf16[1,1,512,512]{3,2,1,0:T(8,128)(2,1)}, u32[]{:S(2)}) copy-start(bf16[1,1,512,512]{3,2,1,0:T(8,128)(2,1)} %param.11) | copy-start | bytes 1572868
  44.4 20.3 %copy-start.1 = (f32[1,1,512,512]{3,2,1,0:T(8,128)S(1)}, f32[1,1,512,512]{3,2,1,0:T(8,128)}, u32[]{:S(2)}) copy-start(f32[1,1,512,512]{3,2,1,0:T(8,128)} %param.9) | copy-start | bytes 3145732
  46.7 18.0 %copy-start = (f32[1,1,512,512]{3,2,1,0:T(8,128)S(1)}, f32[1,1,512,512]{3,2,1,0:T(8,128)}, u32[]{:S(2)}) copy-start(f32[1,1,512,512]{3,2,1,0:T(8,128)} %param.8) | copy-start | bytes 3145732
  46.7 11.0 %collective-permute-start = (bf16[64,8,256]{2,1,0:T(8,128)(2,1)S(1)}, bf16[64,8,256]{2,1,0:T(8,128)(2,1)S(1)}, u32[]{:S(2)}, u32[]{:S(2)}) collective-permute-start(bf16[64,8,256]{2,1,0:T(8,128)(2,1)S(1)} %get-tuple-element.13), channel_id=1, source_target_pairs={{0,256},{256,0},{1,257},{257,1},{2,258},{258,2},{3,259},{259,3},{4... | collective-permute-start | bytes 786440 | tf_op jit(solution)/shard_map/ppermute | solution.py:291
  59.0 25.6 %all-to-all-start.2 = ((bf16[64,8,384]{2,1,0:T(8,128)(2,1)}), bf16[64,8,384]{2,1,0:T(8,128)(2,1)S(1)}, u32[]{:S(2)}, u32[]{:S(2)}) async-start(bf16[64,8,384]{2,1,0:T(8,128)(2,1)} %fill_slots.1), calls=%async_computation.2 | async-start | bytes 786432 | tf_op jit(solution)/shard_map/all_to_all | solution.py:294

commit v4 on v3

--- a/solution.py
+++ b/solution.py
@@ -10,7 +10,9 @@
 DP = ("dp_0h", "dp_0l", "dp_1", "dp_2")
 MP = ("mp_0", "mp_1")
 LANES = 128
+TILE = 4
 MIB = 1024 * 1024
+PLACE_MIB = 54
 
 
 stat_decay = 0.9
@@ -26,15 +28,32 @@
     return pltpu.CompilerParams(vmem_limit_bytes=mib * MIB)
 
 
+def tiles_of(row_count, width):
+    return [
+        (slice(r, r + TILE), slice(c, c + LANES))
+        for c in range(0, width, LANES)
+        for r in range(0, row_count, TILE)
+    ]
+
+
 def partner_of(owner, dp_count):
     half = dp_count // 2
     return jnp.where(owner < half, owner + half, owner - half)
 
 
-def place_blocks(owners, my_index, blocks, dp_count):
+def place_blocks(owners, blocks, dp_count):
     blocks_here, row_count, width = blocks.shape
 
-    def body(owner_ref, index_ref, block_ref, slot_ref, flag_ref):
+    def body(owner_any, block_any, slot_ref, flag_ref, owner_ref, block_ref, sems):
+        fetches = (
+            pltpu.make_async_copy(owner_any, owner_ref, sems.at[0]),
+            pltpu.make_async_copy(block_any, block_ref, sems.at[1]),
+        )
+        for fetch in fetches:
+            fetch.start()
+        for fetch in fetches:
+            fetch.wait()
+        my_index = lax.axis_index(DP)
         busy = jnp.int32(0)
         mine = jnp.int32(0)
         for j in range(blocks_here):
@@ -42,59 +61,76 @@
             rows = block_ref[j]
             slot_ref[owner] = rows
             slot_ref[partner_of(owner, dp_count)] = rows
-            here = (owner == index_ref[0]).astype(jnp.int32)
+            here = (owner == my_index).astype(jnp.int32)
+            beside = (partner_of(owner, dp_count) == my_index).astype(jnp.int32)
             busy = busy + here
-            mine = mine + here * j
+            mine = mine + (here + beside) * j
+            flag_ref[2 + j] = owner
         flag_ref[0] = busy
         flag_ref[1] = mine
 
     return pl.pallas_call(
         body,
         out_shape=(
-            jax.ShapeDtypeStruct((dp_count, row_count, width), blocks.dtype),
-            jax.ShapeDtypeStruct((2,), jnp.int32),
+            pltpu.VMEM((dp_count, row_count, width), blocks.dtype),
+            pltpu.SMEM((2 + blocks_here,), jnp.int32),
         ),
-        in_specs=[SMEM, SMEM, VMEM],
+        in_specs=[ANY, ANY],
         out_specs=(VMEM, SMEM),
-        compiler_params=params(4),
+        scratch_shapes=[
+            pltpu.SMEM(owners.shape, owners.dtype),
+            pltpu.VMEM(blocks.shape, blocks.dtype),
+            pltpu.SemaphoreType.DMA((2,)),
+        ],
+        compiler_params=params(PLACE_MIB),
         name="place_blocks",
-    )(owners, my_index, blocks)
+    )(owners, blocks)
 
 
 def precondition(flags, grad_block, left, right, blocks_here, mp_count, row_count):
     order = grad_block.shape[0]
     half = order // 2
     slots = order // row_count
+    strip = 128
 
     def body(flag_ref, grad_ref, left_ref, right_ref, stay_ref, pass_ref, norm_ref):
+        def squares_of(total, rows):
+            wide = rows.astype(jnp.float32)
+            return total + jnp.sum((wide * wide).reshape(strip // 8, 8, order), axis=0)
+
+        def write_norm(lane_of, total):
+            lane = lax.broadcasted_iota(jnp.int32, (1, LANES), 1)
+            row = jnp.where(lane == lane_of, jnp.sum(total, keepdims=True), 0.0)
+            norm_ref[...] = jnp.broadcast_to(row[None], norm_ref.shape)
+
         @pl.when(flag_ref[0] == 1)
         def _():
-            grad = grad_ref[...]
-            shaded = jnp.dot(grad, right_ref[...], preferred_element_type=jnp.float32)
-            direction = jnp.dot(
-                left_ref[...], shaded.astype(jnp.bfloat16), preferred_element_type=jnp.float32
-            ).astype(jnp.bfloat16)
-            pass_ref[...] = direction[:, half:].reshape(slots, row_count, half)
-            stay_ref[:, :, 0:half] = direction[:, :half].reshape(slots, row_count, half)
-            wide = grad.astype(jnp.float32)
-            grad_square = jnp.sum(wide * wide, keepdims=True)
-            wide = direction.astype(jnp.float32)
-            dir_square = jnp.sum(wide * wide, keepdims=True)
-            lane = lax.broadcasted_iota(jnp.int32, (1, LANES), 1)
-            row = jnp.where(lane == flag_ref[1], grad_square, 0.0)
-            row = row + jnp.where(lane == flag_ref[1] + blocks_here, dir_square, 0.0)
-            norm_ref[...] = jnp.broadcast_to(row[None], norm_ref.shape)
+            shaded = jnp.dot(grad_ref[...], right_ref[...], preferred_element_type=jnp.float32)
+            shaded = shaded.astype(jnp.bfloat16)
+            total = jnp.zeros((8, order), jnp.float32)
+            for i in range(order // strip):
+                rows = jnp.dot(
+                    left_ref[i * strip : (i + 1) * strip], shaded, preferred_element_type=jnp.float32
+                ).astype(jnp.bfloat16)
+                at = slice(i * strip // row_count, (i + 1) * strip // row_count)
+                stay_ref[at] = rows[:, :half].reshape(strip // row_count, row_count, half)
+                pass_ref[at] = rows[:, half:].reshape(strip // row_count, row_count, half)
+                total = squares_of(total, rows)
+            write_norm(flag_ref[1] + blocks_here, total)
 
         @pl.when(flag_ref[0] == 0)
         def _():
-            norm_ref[...] = jnp.zeros_like(norm_ref)
+            total = jnp.zeros((8, order), jnp.float32)
+            for i in range(order // strip):
+                total = squares_of(total, grad_ref[i * strip : (i + 1) * strip])
+            write_norm(flag_ref[1], total)
 
     return pl.pallas_call(
         body,
         out_shape=(
-            jax.ShapeDtypeStruct((slots, row_count, half + LANES), jnp.bfloat16),
-            jax.ShapeDtypeStruct((slots, row_count, half), jnp.bfloat16),
-            jax.ShapeDtypeStruct((mp_count, 1, LANES), jnp.float32),
+            pltpu.VMEM((slots, row_count, half), jnp.bfloat16),
+            pltpu.VMEM((slots, row_count, half), jnp.bfloat16),
+            pltpu.VMEM((mp_count, 1, LANES), jnp.float32),
         ),
         in_specs=[SMEM, VMEM, VMEM, VMEM],
         out_specs=(VMEM, VMEM, VMEM),
@@ -103,24 +139,17 @@
     )(flags, grad_block, left, right)
 
 
-def fill_slots(flags, row_norms, passed, slots):
-    slot_count, row_count, width = slots.shape
-    half = width - LANES
-
-    def body(flag_ref, norm_ref, passed_ref, slot_ref, out_ref, rows_ref, sems):
-        del slot_ref
-        passed_copy = pltpu.make_async_copy(passed_ref, out_ref.at[:, :, 0:half], sems.at[0])
-
-        @pl.when(flag_ref[0] == 0)
-        def _():
-            passed_copy.start()
-
+def fill_slots(flags, row_norms, passed, stays):
+    slot_count, row_count, half = stays.shape
+    tiles = row_count * half // (TILE * LANES)
+
+    def body(flag_ref, norm_ref, passed_ref, stay_ref, out_ref):
         total = jnp.sum(norm_ref[...], axis=0)
         high = total.astype(jnp.bfloat16).astype(jnp.float32)
         rest = total - high
         middle = rest.astype(jnp.bfloat16).astype(jnp.float32)
         low = rest - middle
-        shape = rows_ref.shape[1:]
+        shape = (TILE, LANES)
         row = lax.broadcasted_iota(jnp.int32, shape, 0)
         packed = jnp.where(
             row == 0,
@@ -131,52 +160,51 @@
                 jnp.where(row == 2, jnp.broadcast_to(low, shape), 0.0),
             ),
         ).astype(jnp.bfloat16)
-        rows_ref[...] = jnp.broadcast_to(packed[None], rows_ref.shape)
-        norm_copy = pltpu.make_async_copy(rows_ref, out_ref.at[:, :, half:width], sems.at[1])
-        norm_copy.start()
-        norm_copy.wait()
+        out_ref[:, tiles] = jnp.broadcast_to(packed[None], (slot_count, TILE, LANES))
+
+        def fill(rows_ref):
+            for t, (rows, lanes) in enumerate(tiles_of(row_count, half)):
+                out_ref[:, t] = rows_ref[:, rows, lanes]
+
+        @pl.when(flag_ref[0] == 1)
+        def _():
+            fill(stay_ref)
 
         @pl.when(flag_ref[0] == 0)
         def _():
-            passed_copy.wait()
-
-    return pl.pallas_call(
-        body,
-        out_shape=jax.ShapeDtypeStruct(slots.shape, slots.dtype),
-        in_specs=[SMEM, VMEM, ANY, ANY],
-        out_specs=ANY,
-        scratch_shapes=[
-            pltpu.VMEM((slot_count, row_count, LANES), slots.dtype),
-            pltpu.SemaphoreType.DMA((2,)),
-        ],
-        input_output_aliases={3: 0},
+            fill(passed_ref)
+
+    return pl.pallas_call(
+        body,
+        out_shape=jax.ShapeDtypeStruct((slot_count, tiles + 1, TILE, LANES), stays.dtype),
+        in_specs=[SMEM, VMEM, VMEM, VMEM],
+        out_specs=VMEM,
         compiler_params=params(4),
         name="fill_slots",
-    )(flags, row_norms, passed, slots)
-
-
-def scale_blocks(owners, slots):
-    blocks_here = owners.shape[1]
-    slot_count, row_count, width = slots.shape
-    half = width - LANES
-
-    def body(owner_ref, slot_ref, out_ref):
-        norms = jnp.zeros((row_count, LANES), jnp.float32)
-        for p in range(slot_count):
-            norms = norms + slot_ref[p, :, half:width].astype(jnp.float32)
+    )(flags, row_norms, passed, stays)
+
+
+def scale_blocks(flags, slots, row_count):
+    blocks_here = flags.shape[0] - 2
+    slot_count = slots.shape[0]
+    tiles = slots.shape[1] - 1
+    half = tiles * TILE * LANES // row_count
+
+    def body(flag_ref, slot_ref, out_ref):
+        norms = jnp.sum(slot_ref[:, tiles].astype(jnp.float32), axis=0)
         totals = norms[0:1] + (norms[1:2] + norms[2:3])
         columns = jnp.broadcast_to(totals, (LANES, LANES)).T
         ratio = jnp.sqrt(
             columns[:blocks_here] / (columns[blocks_here : 2 * blocks_here] + tiny_term)
         )
         for j in range(blocks_here):
-            owner = owner_ref[0, j]
-            scale = jnp.broadcast_to(ratio[j : j + 1], (row_count, LANES))
+            owner = flag_ref[2 + j]
+            scale = jnp.broadcast_to(ratio[j : j + 1], (TILE, LANES))
             for k, slot in enumerate((owner, partner_of(owner, slot_count))):
-                for c in range(0, half, LANES):
-                    rows = slot_ref[slot, :, c : c + LANES].astype(jnp.float32)
-                    at = slice(k * half + c, k * half + c + LANES)
-                    out_ref[j, :, at] = (scale * rows).astype(out_ref.dtype)
+                for t, (rows, lanes) in enumerate(tiles_of(row_count, half)):
+                    at = slice(k * half + lanes.start, k * half + lanes.stop)
+                    tile = slot_ref[slot, t].astype(jnp.float32)
+                    out_ref[j, rows, at] = (scale * tile).astype(out_ref.dtype)
 
     return pl.pallas_call(
         body,
@@ -185,7 +213,7 @@
         out_specs=VMEM,
         compiler_params=params(4),
         name="scale_blocks",
-    )(owners, slots)
+    )(flags, slots)
 
 
 def refresh(flags, grad_block, left_stats, right_stats):
@@ -278,11 +306,10 @@
 def shards(gradient, owners, left_stats, right_stats, left_roots_old, right_roots_old):
     dp_count = lax.axis_size(DP)
     mp_count = lax.axis_size(MP)
-    my_index = lax.axis_index(DP).astype(jnp.int32).reshape(1)
     blocks_here = gradient.shape[1]
     row_count = gradient.shape[2]
     block_width = gradient.shape[3]
-    outgoing, flags = place_blocks(owners, my_index, gradient[0], dp_count)
+    outgoing, flags = place_blocks(owners, gradient[0], dp_count)
     arrived = lax.all_to_all(outgoing, DP, split_axis=0, concat_axis=0, tiled=True)
     grad_block = arrived.reshape(dp_count * row_count, block_width)
     stays, passes, norms = precondition(
@@ -293,7 +320,7 @@
     slots = fill_slots(flags, row_norms, passed, stays)
     returned = lax.all_to_all(slots, DP, split_axis=0, concat_axis=0, tiled=True)
     left_root, right_root = refresh(flags, grad_block, left_stats[0, 0], right_stats[0, 0])
-    update = scale_blocks(owners, returned)[None]
+    update = scale_blocks(flags, returned, row_count)[None]
     return (update, left_root[None, None], right_root[None, None])
 
 

time: 86.3 us -> 81.1 us (0.940)
  Pallas kernels: 13.7 us -> 4.25 us
  waiting for transfers between devices: 12.5 us -> 17.5 us
  starting transfers between devices: 8.26 us -> 10 us
  local copies, waits for them, and re-layouts: 1.62 us -> 0.02 us
  blocking collectives: 49.2 us -> 48.2 us
    pallas_call x1, Pallas kernels: 7.39 us -> 1.05 us  [refresh(): pl.pallas_call(body, out_shape=(root, root), in_specs=[SMEM, VMEM, VMEM,...]
    all_to_all x1, waiting for transfers between devices: 12.5 us -> 17.4 us  [shards(): lax.all_to_all(slots, DP, split_axis=0, concat_axis=0, tiled=True)]
    pallas_call x3, Pallas kernels: 4.87 us -> 2.21 us  [the longest x1 1.18 us: place_blocks(): pl.pallas_call(body, out_shape=(pltpu.VMEM((dp_count, row_count, width),...]
    ppermute x1, starting transfers between devices: 2.53 us -> 4.4 us  [shards(): passed = lax.ppermute(passes, 'dp_0h', [(0, 1), (1, 0)])]
    unnamed x12 -> x8, local copies, waits for them, and re-layouts: 1.62 us -> 0.02 us
    all_to_all x1, blocking collectives: 8.42 us -> 7.37 us  [shards(): lax.all_to_all(norms, MP, split_axis=0, concat_axis=0, tiled=True)]
  transfers between devices with their start and end apart: 2 -> 2, of which waited for: 1 -> 2; matrix products, arithmetic and copies ran while one was open for 0% -> 0% of each run, Pallas kernels for 9% -> 1%
where the time goes in v4:
time: 81.1 us; the launch traced here: 80.7 us
  blocking collectives  48.2 us (59%)
  waiting for transfers between devices  17.5 us (22%)
  starting transfers between devices  10 us (12%)
  Pallas kernels  4.25 us (5%)
    all_to_all x1, blocking collectives, shards(): lax.all_to_all(outgoing, DP, split_axis=0, concat_axis=0, tiled=True)  40.8 us
    all_to_all x1, waiting for transfers between devices, shards(): lax.all_to_all(slots, DP, split_axis=0, concat_axis=0, tiled=True)  17.4 us
    all_to_all x1, blocking collectives, shards(): lax.all_to_all(norms, MP, split_axis=0, concat_axis=0, tiled=True)  7.37 us
    all_to_all x1, starting transfers between devices, shards(): lax.all_to_all(slots, DP, split_axis=0, concat_axis=0, tiled=True)  5.63 us
    ppermute x1, starting transfers between devices, shards(): passed = lax.ppermute(passes, 'dp_0h', [(0, 1), (1, 0)])  4.4 us
  transfers between devices with their start and end apart: 2, of which 2 were waited for; matrix products, arithmetic and copies ran while one was open for 0% of the time, Pallas kernels for 1%

profile of v4, /device:TPU:8, one launch (start us, length us, event | category | flops | bytes accessed | tf_op | source)
XLA Modules:
  0.0 80.7 jit_solution(11800140271645916808)
XLA Ops:
  0.6 1.2 %place_blocks.1 = (bf16[64,8,512]{2,1,0:T(8,128)(2,1)S(1)}, s32[34]{0:T(128)S(4)}) custom-call(s32[1,32]{1,0:T(1,128)} %owner_any.1, bf16[32,8,512]{2,1,0:T(8,128)(2,1)} %bitcast.15), custom_call_target="tpu_custom_call" | custom-call | tf_op jit(solution)/shard_map/place_blocks/pallas_call | solution.py:72
  1.8 0.0 copy-start.2
  1.8 0.0 copy-start.3
  1.8 40.8 %all_to_all.15 = bf16[64,8,512]{2,1,0:T(8,128)(2,1)S(1)} all-to-all(bf16[64,8,512]{2,1,0:T(8,128)(2,1)S(1)} %get-tuple-element.11), channel_id=1, replica_groups=mesh['dp_0h'=2,'dp_0l'=2,'dp_1'=8,'dp_2'=2,'mp_0'=4,'mp_1'=2] {'dp_0h','..., dimensions={0} | all-to-all | bytes 1048576 | tf_op jit(solution)/shard_map/all_to_all | solution.py:313
  42.7 0.0 copy-done.2
  42.7 0.0 copy-done.3
  42.7 0.0 copy-start.1
  42.7 0.2 precondition.1
  42.9 0.0 copy-start
  42.9 4.4 %collective-permute-start = (bf16[64,8,256]{2,1,0:T(8,128)(2,1)S(1)}, bf16[64,8,256]{2,1,0:T(8,128)(2,1)S(1)}, u32[]{:S(2)}, u32[]{:S(2)}) collective-permute-start(bf16[64,8,256]{2,1,0:T(8,128)(2,1)S(1)} %get-tuple-element.13), channel_id=1, source_target_pairs={{0,256},{256,0},{1,257},{257,1},{2,258},{258,2},{3,259},{259,3},{4... | collective-permute-start | bytes 786440 | tf_op jit(solution)/shard_map/ppermute | solution.py:318
  47.3 7.4 %all_to_all.16.norm_ref = f32[8,1,128]{2,1,0:T(1,128)S(1)} all-to-all(f32[8,1,128]{2,1,0:T(1,128)S(1)} %get-tuple-element.12), channel_id=1, replica_groups=mesh['dp_0h'=2,'dp_0l'=2,'dp_1'=8,'dp_2'=2,'mp_0'=4,'mp_1'=2] {'mp_0','m..., dimensions={0} | all-to-all | bytes 8192 | tf_op jit(solution)/shard_map/all_to_all | solution.py:319
  54.6 0.1 collective-permute-done.passed_ref
  54.7 0.9 %fill_slots.1 = bf16[64,5,4,128]{3,2,1,0:T(4,128)(2,1)} custom-call(s32[34]{0:T(128)S(4)} %get-tuple-element.10.flag_ref, f32[8,1,128]{2,1,0:T(1,128)S(1)} %all_to_all.16.norm_ref, bf16[64,8,256]{2,1,0:T(8,128)(2,1)S(1)} %collective-permute-done.passed_ref, bf16[64,8,256]{2,1,0:T(8,128)(2,1)S(1)} %get-tuple-element.14.stay_ref), custom_call_target="tpu_custom_call" | custom-call | tf_op jit(solution)/shard_map/fill_slots/pallas_call | solution.py:177
  55.6 5.6 %all-to-all-start.2 = ((bf16[64,5,4,128]{3,2,1,0:T(4,128)(2,1)}), bf16[64,5,4,128]{3,2,1,0:T(4,128)(2,1)S(1)}, u32[]{:S(2)}, u32[]{:S(2)}) async-start(bf16[64,5,4,128]{3,2,1,0:T(4,128)(2,1)} %fill_slots.1), calls=%async_computation.2 | async-start | bytes 655360 | tf_op jit(solution)/shard_map/all_to_all | solution.py:321
  61.2 0.0 copy-done.1
  61.2 0.0 copy-done
  61.2 1.0 %refresh.1 = (bf16[512,512]{1,0:T(8,128)(2,1)}, bf16[512,512]{1,0:T(8,128)(2,1)}) custom-call(s32[34]{0:T(128)S(4)} %get-tuple-element.10.flag_ref, bf16[512,512]{1,0:T(8,128)(2,1)S(1)} %bitcast.10, f32[512,512]{1,0:T(8,128)S(1)} %bitcast.11, f32[512,512]{1,0:T(8,128)S(1)} %bitcast.12), custom_call_target="tpu_custom_call" | custom-call | tf_op jit(solution)/shard_map/refresh/pallas_call | solution.py:291
  62.3 17.4 %all-to-all-done.2.slot_ref = bf16[64,5,4,128]{3,2,1,0:T(4,128)(2,1)S(1)} async-done(((bf16[64,5,4,128]{3,2,1,0:T(4,128)(2,1)}), bf16[64,5,4,128]{3,2,1,0:T(4,128)(2,1)S(1)}, u32[]{:S(2)}, u32[]{:S(2)}) %all-to-all-start.2) | async-done | bytes 327712 | tf_op jit(solution)/shard_map/all_to_all | solution.py:321
  79.7 1.0 %scale_blocks.1 = bf16[32,8,512]{2,1,0:T(8,128)(2,1)} custom-call(s32[34]{0:T(128)S(4)} %get-tuple-element.10.flag_ref, bf16[64,5,4,128]{3,2,1,0:T(4,128)(2,1)S(1)} %all-to-all-done.2.slot_ref), custom_call_target="tpu_custom_call" | custom-call | tf_op jit(solution)/shard_map/scale_blocks/pallas_call | solution.py:209
Async XLA Ops:
  1.8 40.9 %copy-start.2 = (bf16[1,1,512,512]{3,2,1,0:T(8,128)(2,1)S(1)}, bf16[1,1,512,512]{3,2,1,0:T(8,128)(2,1)}, u32[]{:S(2)}) copy-start(bf16[1,1,512,512]{3,2,1,0:T(8,128)(2,1)} %param.10) | copy-start | bytes 1572868
  1.8 40.8 %copy-start.3 = (bf16[1,1,512,512]{3,2,1,0:T(8,128)(2,1)S(1)}, bf16[1,1,512,512]{3,2,1,0:T(8,128)(2,1)}, u32[]{:S(2)}) copy-start(bf16[1,1,512,512]{3,2,1,0:T(8,128)(2,1)} %param.11) | copy-start | bytes 1572868
  42.7 18.5 %copy-start.1 = (f32[1,1,512,512]{3,2,1,0:T(8,128)S(1)}, f32[1,1,512,512]{3,2,1,0:T(8,128)}, u32[]{:S(2)}) copy-start(f32[1,1,512,512]{3,2,1,0:T(8,128)} %param.9) | copy-start | bytes 3145732
  42.9 18.4 %copy-start = (f32[1,1,512,512]{3,2,1,0:T(8,128)S(1)}, f32[1,1,512,512]{3,2,1,0:T(8,128)}, u32[]{:S(2)}) copy-start(f32[1,1,512,512]{3,2,1,0:T(8,128)} %param.8) | copy-start | bytes 3145732
  42.9 11.8 %collective-permute-start = (bf16[64,8,256]{2,1,0:T(8,128)(2,1)S(1)}, bf16[64,8,256]{2,1,0:T(8,128)(2,1)S(1)}, u32[]{:S(2)}, u32[]{:S(2)}) collective-permute-start(bf16[64,8,256]{2,1,0:T(8,128)(2,1)S(1)} %get-tuple-element.13), channel_id=1, source_target_pairs={{0,256},{256,0},{1,257},{257,1},{2,258},{258,2},{3,259},{259,3},{4... | collective-permute-start | bytes 786440 | tf_op jit(solution)/shard_map/ppermute | solution.py:318
  55.6 24.1 %all-to-all-start.2 = ((bf16[64,5,4,128]{3,2,1,0:T(4,128)(2,1)}), bf16[64,5,4,128]{3,2,1,0:T(4,128)(2,1)S(1)}, u32[]{:S(2)}, u32[]{:S(2)}) async-start(bf16[64,5,4,128]{3,2,1,0:T(4,128)(2,1)} %fill_slots.1), calls=%async_computation.2 | async-start | bytes 655360 | tf_op jit(solution)/shard_map/all_to_all | solution.py:321

commit v5 on v4

--- a/solution.py
+++ b/solution.py
@@ -11,6 +11,7 @@
 MP = ("mp_0", "mp_1")
 LANES = 128
 TILE = 4
+PIECES = 4
 MIB = 1024 * 1024
 PLACE_MIB = 54
 
@@ -43,20 +44,24 @@
 
 def place_blocks(owners, blocks, dp_count):
     blocks_here, row_count, width = blocks.shape
+    per_piece = blocks_here // PIECES
 
     def body(owner_any, block_any, slot_ref, flag_ref, owner_ref, block_ref, sems):
-        fetches = (
-            pltpu.make_async_copy(owner_any, owner_ref, sems.at[0]),
-            pltpu.make_async_copy(block_any, block_ref, sems.at[1]),
-        )
-        for fetch in fetches:
+        owner_fetch = pltpu.make_async_copy(owner_any, owner_ref, sems.at[PIECES])
+        owner_fetch.start()
+        fetches = []
+        for piece in range(PIECES):
+            at = pl.ds(piece * per_piece, per_piece)
+            fetch = pltpu.make_async_copy(block_any.at[at], block_ref.at[at], sems.at[piece])
             fetch.start()
-        for fetch in fetches:
-            fetch.wait()
+            fetches.append(fetch)
+        owner_fetch.wait()
         my_index = lax.axis_index(DP)
         busy = jnp.int32(0)
         mine = jnp.int32(0)
         for j in range(blocks_here):
+            if j % per_piece == 0:
+                fetches[j // per_piece].wait()
             owner = owner_ref[0, j]
             rows = block_ref[j]
             slot_ref[owner] = rows
@@ -80,7 +85,7 @@
         scratch_shapes=[
             pltpu.SMEM(owners.shape, owners.dtype),
             pltpu.VMEM(blocks.shape, blocks.dtype),
-            pltpu.SemaphoreType.DMA((2,)),
+            pltpu.SemaphoreType.DMA((PIECES + 1,)),
         ],
         compiler_params=params(PLACE_MIB),
         name="place_blocks",
@@ -142,8 +147,9 @@
 def fill_slots(flags, row_norms, passed, stays):
     slot_count, row_count, half = stays.shape
     tiles = row_count * half // (TILE * LANES)
-
-    def body(flag_ref, norm_ref, passed_ref, stay_ref, out_ref):
+    per_piece = slot_count // PIECES
+
+    def body(flag_ref, norm_ref, passed_ref, stay_ref, out_any, out_ref, sems):
         total = jnp.sum(norm_ref[...], axis=0)
         high = total.astype(jnp.bfloat16).astype(jnp.float32)
         rest = total - high
@@ -160,11 +166,19 @@
                 jnp.where(row == 2, jnp.broadcast_to(low, shape), 0.0),
             ),
         ).astype(jnp.bfloat16)
-        out_ref[:, tiles] = jnp.broadcast_to(packed[None], (slot_count, TILE, LANES))
 
         def fill(rows_ref):
-            for t, (rows, lanes) in enumerate(tiles_of(row_count, half)):
-                out_ref[:, t] = rows_ref[:, rows, lanes]
+            copies = []
+            for piece in range(PIECES):
+                at = pl.ds(piece * per_piece, per_piece)
+                out_ref[at, tiles] = jnp.broadcast_to(packed[None], (per_piece, TILE, LANES))
+                for t, (rows, lanes) in enumerate(tiles_of(row_count, half)):
+                    out_ref[at, t] = rows_ref[at, rows, lanes]
+                copy = pltpu.make_async_copy(out_ref.at[at], out_any.at[at], sems.at[piece])
+                copy.start()
+                copies.append(copy)
+            for copy in copies:
+                copy.wait()
 
         @pl.when(flag_ref[0] == 1)
         def _():
@@ -178,7 +192,11 @@
         body,
         out_shape=jax.ShapeDtypeStruct((slot_count, tiles + 1, TILE, LANES), stays.dtype),
         in_specs=[SMEM, VMEM, VMEM, VMEM],
-        out_specs=VMEM,
+        out_specs=ANY,
+        scratch_shapes=[
+            pltpu.VMEM((slot_count, tiles + 1, TILE, LANES), stays.dtype),
+            pltpu.SemaphoreType.DMA((PIECES,)),
+        ],
         compiler_params=params(4),
         name="fill_slots",
     )(flags, row_norms, passed, stays)
@@ -189,8 +207,10 @@
     slot_count = slots.shape[0]
     tiles = slots.shape[1] - 1
     half = tiles * TILE * LANES // row_count
-
-    def body(flag_ref, slot_ref, out_ref):
+    per_piece = blocks_here // PIECES
+
+    def body(flag_ref, slot_ref, out_any, out_ref, sems):
+        copies = []
         norms = jnp.sum(slot_ref[:, tiles].astype(jnp.float32), axis=0)
         totals = norms[0:1] + (norms[1:2] + norms[2:3])
         columns = jnp.broadcast_to(totals, (LANES, LANES)).T
@@ -205,12 +225,24 @@
                     at = slice(k * half + lanes.start, k * half + lanes.stop)
                     tile = slot_ref[slot, t].astype(jnp.float32)
                     out_ref[j, rows, at] = (scale * tile).astype(out_ref.dtype)
+            if (j + 1) % per_piece == 0:
+                piece = j // per_piece
+                at = pl.ds(piece * per_piece, per_piece)
+                copy = pltpu.make_async_copy(out_ref.at[at], out_any.at[at], sems.at[piece])
+                copy.start()
+                copies.append(copy)
+        for copy in copies:
+            copy.wait()
 
     return pl.pallas_call(
         body,
         out_shape=jax.ShapeDtypeStruct((blocks_here, row_count, 2 * half), slots.dtype),
         in_specs=[SMEM, VMEM],
-        out_specs=VMEM,
+        out_specs=ANY,
+        scratch_shapes=[
+            pltpu.VMEM((blocks_here, row_count, 2 * half), slots.dtype),
+            pltpu.SemaphoreType.DMA((PIECES,)),
+        ],
         compiler_params=params(4),
         name="scale_blocks",
     )(flags, slots)

time: 81.1 us -> 80.9 us (level)
  transfers between devices with their start and end apart: 2 -> 2, of which waited for: 2 -> 1; matrix products, arithmetic and copies ran while one was open for 0% -> 0% of each run, Pallas kernels for 1% -> 1%
where the time goes in v5:
time: 80.9 us; the launch traced here: 80.5 us
  blocking collectives  48.1 us (59%)
  waiting for transfers between devices  17.4 us (22%)
  starting transfers between devices  10.2 us (13%)
  Pallas kernels  4.02 us (5%)
    all_to_all x1, blocking collectives, shards(): lax.all_to_all(outgoing, DP, split_axis=0, concat_axis=0, tiled=True)  40.8 us
    all_to_all x1, waiting for transfers between devices, shards(): lax.all_to_all(slots, DP, split_axis=0, concat_axis=0, tiled=True)  17.4 us
    all_to_all x1, blocking collectives, shards(): lax.all_to_all(norms, MP, split_axis=0, concat_axis=0, tiled=True)  7.24 us
    all_to_all x1, starting transfers between devices, shards(): lax.all_to_all(slots, DP, split_axis=0, concat_axis=0, tiled=True)  5.84 us
    ppermute x1, starting transfers between devices, shards(): passed = lax.ppermute(passes, 'dp_0h', [(0, 1), (1, 0)])  4.4 us
  transfers between devices with their start and end apart: 2, of which 1 were waited for; matrix products, arithmetic and copies ran while one was open for 0% of the time, Pallas kernels for 1%

profile of v5, /device:TPU:8, one launch (start us, length us, event | category | flops | bytes accessed | tf_op | source)
XLA Modules:
  0.0 80.5 jit_solution(18268949834530695327)
XLA Ops:
  0.6 1.0 %place_blocks.1 = (bf16[64,8,512]{2,1,0:T(8,128)(2,1)S(1)}, s32[34]{0:T(128)S(4)}) custom-call(s32[1,32]{1,0:T(1,128)} %owner_any.1, bf16[32,8,512]{2,1,0:T(8,128)(2,1)} %bitcast.15), custom_call_target="tpu_custom_call" | custom-call | tf_op jit(solution)/shard_map/place_blocks/pallas_call | solution.py:77
  1.7 0.0 copy-start.2
  1.7 0.0 copy-start.3
  1.7 40.8 %all_to_all.15 = bf16[64,8,512]{2,1,0:T(8,128)(2,1)S(1)} all-to-all(bf16[64,8,512]{2,1,0:T(8,128)(2,1)S(1)} %get-tuple-element.11), channel_id=1, replica_groups=mesh['dp_0h'=2,'dp_0l'=2,'dp_1'=8,'dp_2'=2,'mp_0'=4,'mp_1'=2] {'dp_0h','..., dimensions={0} | all-to-all | bytes 1048576 | tf_op jit(solution)/shard_map/all_to_all | solution.py:345
  42.5 0.0 copy-done.2
  42.5 0.0 copy-done.3
  42.5 0.0 copy-start.1
  42.5 0.2 precondition.1
  42.7 0.0 copy-start
  42.7 4.4 %collective-permute-start = (bf16[64,8,256]{2,1,0:T(8,128)(2,1)S(1)}, bf16[64,8,256]{2,1,0:T(8,128)(2,1)S(1)}, u32[]{:S(2)}, u32[]{:S(2)}) collective-permute-start(bf16[64,8,256]{2,1,0:T(8,128)(2,1)S(1)} %get-tuple-element.13), channel_id=1, source_target_pairs={{0,256},{256,0},{1,257},{257,1},{2,258},{258,2},{3,259},{259,3},{4... | collective-permute-start | bytes 786440 | tf_op jit(solution)/shard_map/ppermute | solution.py:350
  47.1 7.2 %all_to_all.16.norm_ref = f32[8,1,128]{2,1,0:T(1,128)S(1)} all-to-all(f32[8,1,128]{2,1,0:T(1,128)S(1)} %get-tuple-element.12), channel_id=1, replica_groups=mesh['dp_0h'=2,'dp_0l'=2,'dp_1'=8,'dp_2'=2,'mp_0'=4,'mp_1'=2] {'mp_0','m..., dimensions={0} | all-to-all | bytes 8192 | tf_op jit(solution)/shard_map/all_to_all | solution.py:351
  54.4 0.0 collective-permute-done.passed_ref
  54.4 0.8 %fill_slots.1 = bf16[64,5,4,128]{3,2,1,0:T(4,128)(2,1)} custom-call(s32[34]{0:T(128)S(4)} %get-tuple-element.10.flag_ref, f32[8,1,128]{2,1,0:T(1,128)S(1)} %all_to_all.16.norm_ref, bf16[64,8,256]{2,1,0:T(8,128)(2,1)S(1)} %collective-permute-done.passed_ref, bf16[64,8,256]{2,1,0:T(8,128)(2,1)S(1)} %get-tuple-element.14.stay_ref), custom_call_target="tpu_custom_call" | custom-call | tf_op jit(solution)/shard_map/fill_slots/pallas_call | solution.py:191
  55.2 5.8 %all-to-all-start.2 = ((bf16[64,5,4,128]{3,2,1,0:T(4,128)(2,1)}), bf16[64,5,4,128]{3,2,1,0:T(4,128)(2,1)S(1)}, u32[]{:S(2)}, u32[]{:S(2)}) async-start(bf16[64,5,4,128]{3,2,1,0:T(4,128)(2,1)} %fill_slots.1), calls=%async_computation.2 | async-start | bytes 655360 | tf_op jit(solution)/shard_map/all_to_all | solution.py:353
  61.0 0.0 copy-done.1
  61.0 0.0 copy-done
  61.1 1.0 %refresh.1 = (bf16[512,512]{1,0:T(8,128)(2,1)}, bf16[512,512]{1,0:T(8,128)(2,1)}) custom-call(s32[34]{0:T(128)S(4)} %get-tuple-element.10.flag_ref, bf16[512,512]{1,0:T(8,128)(2,1)S(1)} %bitcast.10, f32[512,512]{1,0:T(8,128)S(1)} %bitcast.11, f32[512,512]{1,0:T(8,128)S(1)} %bitcast.12), custom_call_target="tpu_custom_call" | custom-call | tf_op jit(solution)/shard_map/refresh/pallas_call | solution.py:323
  62.1 17.4 %all-to-all-done.2.slot_ref = bf16[64,5,4,128]{3,2,1,0:T(4,128)(2,1)S(1)} async-done(((bf16[64,5,4,128]{3,2,1,0:T(4,128)(2,1)}), bf16[64,5,4,128]{3,2,1,0:T(4,128)(2,1)S(1)}, u32[]{:S(2)}, u32[]{:S(2)}) %all-to-all-start.2) | async-done | bytes 327712 | tf_op jit(solution)/shard_map/all_to_all | solution.py:353
  79.5 1.0 %scale_blocks.1 = bf16[32,8,512]{2,1,0:T(8,128)(2,1)} custom-call(s32[34]{0:T(128)S(4)} %get-tuple-element.10.flag_ref, bf16[64,5,4,128]{3,2,1,0:T(4,128)(2,1)S(1)} %all-to-all-done.2.slot_ref), custom_call_target="tpu_custom_call" | custom-call | tf_op jit(solution)/shard_map/scale_blocks/pallas_call | solution.py:237
Async XLA Ops:
  1.7 40.9 %copy-start.2 = (bf16[1,1,512,512]{3,2,1,0:T(8,128)(2,1)S(1)}, bf16[1,1,512,512]{3,2,1,0:T(8,128)(2,1)}, u32[]{:S(2)}) copy-start(bf16[1,1,512,512]{3,2,1,0:T(8,128)(2,1)} %param.10) | copy-start | bytes 1572868
  1.7 40.8 %copy-start.3 = (bf16[1,1,512,512]{3,2,1,0:T(8,128)(2,1)S(1)}, bf16[1,1,512,512]{3,2,1,0:T(8,128)(2,1)}, u32[]{:S(2)}) copy-start(bf16[1,1,512,512]{3,2,1,0:T(8,128)(2,1)} %param.11) | copy-start | bytes 1572868
  42.5 18.5 %copy-start.1 = (f32[1,1,512,512]{3,2,1,0:T(8,128)S(1)}, f32[1,1,512,512]{3,2,1,0:T(8,128)}, u32[]{:S(2)}) copy-start(f32[1,1,512,512]{3,2,1,0:T(8,128)} %param.9) | copy-start | bytes 3145732
  42.7 18.3 %copy-start = (f32[1,1,512,512]{3,2,1,0:T(8,128)S(1)}, f32[1,1,512,512]{3,2,1,0:T(8,128)}, u32[]{:S(2)}) copy-start(f32[1,1,512,512]{3,2,1,0:T(8,128)} %param.8) | copy-start | bytes 3145732
  42.7 11.7 %collective-permute-start = (bf16[64,8,256]{2,1,0:T(8,128)(2,1)S(1)}, bf16[64,8,256]{2,1,0:T(8,128)(2,1)S(1)}, u32[]{:S(2)}, u32[]{:S(2)}) collective-permute-start(bf16[64,8,256]{2,1,0:T(8,128)(2,1)S(1)} %get-tuple-element.13), channel_id=1, source_target_pairs={{0,256},{256,0},{1,257},{257,1},{2,258},{258,2},{3,259},{259,3},{4... | collective-permute-start | bytes 786440 | tf_op jit(solution)/shard_map/ppermute | solution.py:350
  55.2 24.3 %all-to-all-start.2 = ((bf16[64,5,4,128]{3,2,1,0:T(4,128)(2,1)}), bf16[64,5,4,128]{3,2,1,0:T(4,128)(2,1)S(1)}, u32[]{:S(2)}, u32[]{:S(2)}) async-start(bf16[64,5,4,128]{3,2,1,0:T(4,128)(2,1)} %fill_slots.1), calls=%async_computation.2 | async-start | bytes 655360 | tf_op jit(solution)/shard_map/all_to_all | solution.py:353

commit v6 on v5

--- a/solution.py
+++ b/solution.py
@@ -92,127 +92,107 @@
     )(owners, blocks)
 
 
-def precondition(flags, grad_block, left, right, blocks_here, mp_count, row_count):
+def precondition(flags, grad_block, left, right, blocks_here, row_count):
     order = grad_block.shape[0]
-    half = order // 2
     slots = order // row_count
-    strip = 128
-
-    def body(flag_ref, grad_ref, left_ref, right_ref, stay_ref, pass_ref, norm_ref):
+    tiles = row_count * order // (TILE * LANES)
+    strip = order // PIECES
+    per_piece = slots // PIECES
+
+    def body(flag_ref, grad_ref, left_ref, right_ref, out_any, out_ref, sems):
         def squares_of(total, rows):
             wide = rows.astype(jnp.float32)
             return total + jnp.sum((wide * wide).reshape(strip // 8, 8, order), axis=0)
 
-        def write_norm(lane_of, total):
-            lane = lax.broadcasted_iota(jnp.int32, (1, LANES), 1)
-            row = jnp.where(lane == lane_of, jnp.sum(total, keepdims=True), 0.0)
-            norm_ref[...] = jnp.broadcast_to(row[None], norm_ref.shape)
+        def send_norm(lane_of, total):
+            square = jnp.sum(total, keepdims=True)
+            high = square.astype(jnp.bfloat16).astype(jnp.float32)
+            rest = square - high
+            middle = rest.astype(jnp.bfloat16).astype(jnp.float32)
+            low = rest - middle
+            lane = lax.broadcasted_iota(jnp.int32, (TILE, LANES), 1)
+            row = lax.broadcasted_iota(jnp.int32, (TILE, LANES), 0)
+            part = jnp.where(row == 0, high, jnp.where(row == 1, middle, low))
+            packed = jnp.where((lane == lane_of) & (row < 3), part, 0.0).astype(jnp.bfloat16)
+            out_ref[:, tiles] = jnp.broadcast_to(packed[None], (slots, TILE, LANES))
+            copy = pltpu.make_async_copy(out_ref.at[:, tiles], out_any.at[:, tiles], sems.at[PIECES])
+            copy.start()
+            return copy
 
         @pl.when(flag_ref[0] == 1)
         def _():
             shaded = jnp.dot(grad_ref[...], right_ref[...], preferred_element_type=jnp.float32)
             shaded = shaded.astype(jnp.bfloat16)
             total = jnp.zeros((8, order), jnp.float32)
-            for i in range(order // strip):
+            copies = []
+            for i in range(PIECES):
                 rows = jnp.dot(
                     left_ref[i * strip : (i + 1) * strip], shaded, preferred_element_type=jnp.float32
                 ).astype(jnp.bfloat16)
-                at = slice(i * strip // row_count, (i + 1) * strip // row_count)
-                stay_ref[at] = rows[:, :half].reshape(strip // row_count, row_count, half)
-                pass_ref[at] = rows[:, half:].reshape(strip // row_count, row_count, half)
+                at = pl.ds(i * per_piece, per_piece)
+                by_slot = rows.reshape(per_piece, row_count, order)
+                for t, (part, lanes) in enumerate(tiles_of(row_count, order)):
+                    out_ref[at, t] = by_slot[:, part, lanes]
+                copy = pltpu.make_async_copy(
+                    out_ref.at[at, pl.ds(0, tiles)], out_any.at[at, pl.ds(0, tiles)], sems.at[i]
+                )
+                copy.start()
+                copies.append(copy)
                 total = squares_of(total, rows)
-            write_norm(flag_ref[1] + blocks_here, total)
+            copies.append(send_norm(flag_ref[1] + blocks_here, total))
+            for copy in copies:
+                copy.wait()
 
         @pl.when(flag_ref[0] == 0)
         def _():
             total = jnp.zeros((8, order), jnp.float32)
-            for i in range(order // strip):
+            for i in range(PIECES):
                 total = squares_of(total, grad_ref[i * strip : (i + 1) * strip])
-            write_norm(flag_ref[1], total)
-
-    return pl.pallas_call(
-        body,
-        out_shape=(
-            pltpu.VMEM((slots, row_count, half), jnp.bfloat16),
-            pltpu.VMEM((slots, row_count, half), jnp.bfloat16),
-            pltpu.VMEM((mp_count, 1, LANES), jnp.float32),
-        ),
+            send_norm(flag_ref[1], total).wait()
+
+    shape = (slots, tiles + 1, TILE, LANES)
+    return pl.pallas_call(
+        body,
+        out_shape=jax.ShapeDtypeStruct(shape, jnp.bfloat16),
         in_specs=[SMEM, VMEM, VMEM, VMEM],
-        out_specs=(VMEM, VMEM, VMEM),
+        out_specs=ANY,
+        scratch_shapes=[
+            pltpu.VMEM(shape, jnp.bfloat16),
+            pltpu.SemaphoreType.DMA((PIECES + 1,)),
+        ],
         compiler_params=params(12),
         name="precondition",
     )(flags, grad_block, left, right)
 
 
-def fill_slots(flags, row_norms, passed, stays):
-    slot_count, row_count, half = stays.shape
-    tiles = row_count * half // (TILE * LANES)
-    per_piece = slot_count // PIECES
-
-    def body(flag_ref, norm_ref, passed_ref, stay_ref, out_any, out_ref, sems):
-        total = jnp.sum(norm_ref[...], axis=0)
-        high = total.astype(jnp.bfloat16).astype(jnp.float32)
-        rest = total - high
-        middle = rest.astype(jnp.bfloat16).astype(jnp.float32)
-        low = rest - middle
-        shape = (TILE, LANES)
-        row = lax.broadcasted_iota(jnp.int32, shape, 0)
-        packed = jnp.where(
-            row == 0,
-            jnp.broadcast_to(high, shape),
-            jnp.where(
-                row == 1,
-                jnp.broadcast_to(middle, shape),
-                jnp.where(row == 2, jnp.broadcast_to(low, shape), 0.0),
-            ),
-        ).astype(jnp.bfloat16)
-
-        def fill(rows_ref):
-            copies = []
-            for piece in range(PIECES):
-                at = pl.ds(piece * per_piece, per_piece)
-                out_ref[at, tiles] = jnp.broadcast_to(packed[None], (per_piece, TILE, LANES))
-                for t, (rows, lanes) in enumerate(tiles_of(row_count, half)):
-                    out_ref[at, t] = rows_ref[at, rows, lanes]
-                copy = pltpu.make_async_copy(out_ref.at[at], out_any.at[at], sems.at[piece])
-                copy.start()
-                copies.append(copy)
-            for copy in copies:
-                copy.wait()
-
-        @pl.when(flag_ref[0] == 1)
-        def _():
-            fill(stay_ref)
-
-        @pl.when(flag_ref[0] == 0)
-        def _():
-            fill(passed_ref)
-
-    return pl.pallas_call(
-        body,
-        out_shape=jax.ShapeDtypeStruct((slot_count, tiles + 1, TILE, LANES), stays.dtype),
-        in_specs=[SMEM, VMEM, VMEM, VMEM],
-        out_specs=ANY,
-        scratch_shapes=[
-            pltpu.VMEM((slot_count, tiles + 1, TILE, LANES), stays.dtype),
-            pltpu.SemaphoreType.DMA((PIECES,)),
-        ],
+def add_norms(slots, done, mp_count):
+    tiles = slots.shape[1] - 1
+
+    def body(slot_ref, done_ref, norm_ref):
+        del done_ref
+        parts = jnp.sum(slot_ref[:, tiles].astype(jnp.float32), axis=0)
+        norms = parts[0:1] + (parts[1:2] + parts[2:3])
+        norm_ref[...] = jnp.broadcast_to(norms[None], norm_ref.shape)
+
+    return pl.pallas_call(
+        body,
+        out_shape=pltpu.VMEM((mp_count, 1, LANES), jnp.float32),
+        in_specs=[VMEM, SMEM],
+        out_specs=VMEM,
         compiler_params=params(4),
-        name="fill_slots",
-    )(flags, row_norms, passed, stays)
-
-
-def scale_blocks(flags, slots, row_count):
+        name="add_norms",
+    )(slots, done)
+
+
+def scale_blocks(flags, row_norms, slots, row_count):
     blocks_here = flags.shape[0] - 2
-    slot_count = slots.shape[0]
     tiles = slots.shape[1] - 1
-    half = tiles * TILE * LANES // row_count
+    order = tiles * TILE * LANES // row_count
     per_piece = blocks_here // PIECES
 
-    def body(flag_ref, slot_ref, out_any, out_ref, sems):
+    def body(flag_ref, norm_ref, slot_ref, out_any, out_ref, sems):
         copies = []
-        norms = jnp.sum(slot_ref[:, tiles].astype(jnp.float32), axis=0)
-        totals = norms[0:1] + (norms[1:2] + norms[2:3])
+        totals = jnp.sum(norm_ref[...], axis=0)
         columns = jnp.broadcast_to(totals, (LANES, LANES)).T
         ratio = jnp.sqrt(
             columns[:blocks_here] / (columns[blocks_here : 2 * blocks_here] + tiny_term)
@@ -220,11 +200,9 @@
         for j in range(blocks_here):
             owner = flag_ref[2 + j]
             scale = jnp.broadcast_to(ratio[j : j + 1], (TILE, LANES))
-            for k, slot in enumerate((owner, partner_of(owner, slot_count))):
-                for t, (rows, lanes) in enumerate(tiles_of(row_count, half)):
-                    at = slice(k * half + lanes.start, k * half + lanes.stop)
-                    tile = slot_ref[slot, t].astype(jnp.float32)
-                    out_ref[j, rows, at] = (scale * tile).astype(out_ref.dtype)
+            for t, (rows, lanes) in enumerate(tiles_of(row_count, order)):
+                tile = slot_ref[owner, t].astype(jnp.float32)
+                out_ref[j, rows, lanes] = (scale * tile).astype(out_ref.dtype)
             if (j + 1) % per_piece == 0:
                 piece = j // per_piece
                 at = pl.ds(piece * per_piece, per_piece)
@@ -234,25 +212,26 @@
         for copy in copies:
             copy.wait()
 
-    return pl.pallas_call(
-        body,
-        out_shape=jax.ShapeDtypeStruct((blocks_here, row_count, 2 * half), slots.dtype),
-        in_specs=[SMEM, VMEM],
+    shape = (blocks_here, row_count, order)
+    return pl.pallas_call(
+        body,
+        out_shape=jax.ShapeDtypeStruct(shape, slots.dtype),
+        in_specs=[SMEM, VMEM, VMEM],
         out_specs=ANY,
         scratch_shapes=[
-            pltpu.VMEM((blocks_here, row_count, 2 * half), slots.dtype),
+            pltpu.VMEM(shape, slots.dtype),
             pltpu.SemaphoreType.DMA((PIECES,)),
         ],
         compiler_params=params(4),
         name="scale_blocks",
-    )(flags, slots)
+    )(flags, row_norms, slots)
 
 
 def refresh(flags, grad_block, left_stats, right_stats):
     order = grad_block.shape[0]
     strip = 64
 
-    def body(flag_ref, grad_ref, left_ref, right_ref, left_out, right_out, wide, low, first):
+    def body(flag_ref, grad_ref, left_ref, right_ref, left_out, right_out, done_ref, wide, low, first):
         def one(stat_ref, out_ref, dims):
             grad = grad_ref[...]
             wide[...] = lax.dot_general(grad, grad, dims, preferred_element_type=jnp.float32)
@@ -309,6 +288,8 @@
             lax.fori_loop(0, order // strip, again, 0)
             out_ref[...] = dot(first[...], low[2]).astype(jnp.bfloat16)
 
+        done_ref[0] = flag_ref[0]
+
         @pl.when(flag_ref[0] == 1)
         def _():
             one(left_ref, left_out, (((1,), (1,)), ((), ())))
@@ -322,9 +303,9 @@
     root = jax.ShapeDtypeStruct((order, order), jnp.bfloat16)
     return pl.pallas_call(
         body,
-        out_shape=(root, root),
+        out_shape=(root, root, pltpu.SMEM((1,), jnp.int32)),
         in_specs=[SMEM, VMEM, VMEM, VMEM],
-        out_specs=(VMEM, VMEM),
+        out_specs=(VMEM, VMEM, SMEM),
         scratch_shapes=[
             pltpu.VMEM((order, order), jnp.float32),
             pltpu.VMEM((3, order, order), jnp.bfloat16),
@@ -344,15 +325,14 @@
     outgoing, flags = place_blocks(owners, gradient[0], dp_count)
     arrived = lax.all_to_all(outgoing, DP, split_axis=0, concat_axis=0, tiled=True)
     grad_block = arrived.reshape(dp_count * row_count, block_width)
-    stays, passes, norms = precondition(
-        flags, grad_block, left_roots_old[0, 0], right_roots_old[0, 0], blocks_here, mp_count, row_count
+    slots = precondition(
+        flags, grad_block, left_roots_old[0, 0], right_roots_old[0, 0], blocks_here, row_count
     )
-    passed = lax.ppermute(passes, "dp_0h", [(0, 1), (1, 0)])
+    returned = lax.all_to_all(slots, DP, split_axis=0, concat_axis=0, tiled=True)
+    left_root, right_root, done = refresh(flags, grad_block, left_stats[0, 0], right_stats[0, 0])
+    norms = add_norms(returned, done, mp_count)
     row_norms = lax.all_to_all(norms, MP, split_axis=0, concat_axis=0, tiled=True)
-    slots = fill_slots(flags, row_norms, passed, stays)
-    returned = lax.all_to_all(slots, DP, split_axis=0, concat_axis=0, tiled=True)
-    left_root, right_root = refresh(flags, grad_block, left_stats[0, 0], right_stats[0, 0])
-    update = scale_blocks(flags, returned, row_count)[None]
+    update = scale_blocks(flags, row_norms, returned, row_count)[None]
     return (update, left_root[None, None], right_root[None, None])
 
 

time: 80.9 us -> 83.6 us (1.033)
  the two profiles are of different devices: /device:TPU:8 before, /device:TPU:1 now
where the time goes in v6:
time: 83.6 us; the launch traced here: 83.2 us
  blocking collectives  50.7 us (61%)
  waiting for transfers between devices  17.5 us (21%)
  starting transfers between devices  10.4 us (12%)
  Pallas kernels  3.92 us (5%)
    all_to_all x1, blocking collectives, shards(): lax.all_to_all(outgoing, DP, split_axis=0, concat_axis=0, tiled=True)  37.2 us
    all_to_all x1, waiting for transfers between devices, shards(): lax.all_to_all(slots, DP, split_axis=0, concat_axis=0, tiled=True)  17.5 us
    all_to_all x1, blocking collectives, shards(): lax.all_to_all(norms, MP, split_axis=0, concat_axis=0, tiled=True)  13.5 us
    all_to_all x1, starting transfers between devices, shards(): lax.all_to_all(slots, DP, split_axis=0, concat_axis=0, tiled=True)  10.4 us
  transfers between devices with their start and end apart: 1, of which 1 were waited for; matrix products, arithmetic and copies ran while one was open for 0% of the time, Pallas kernels for 1%

profile of v6, /device:TPU:1, one launch (start us, length us, event | category | flops | bytes accessed | tf_op | source)
XLA Modules:
  0.0 83.2 jit_solution(9101291300201705520)
XLA Ops:
  0.6 1.0 %place_blocks.1 = (bf16[64,8,512]{2,1,0:T(8,128)(2,1)S(1)}, s32[34]{0:T(128)S(4)}) custom-call(s32[1,32]{1,0:T(1,128)} %owner_any.1, bf16[32,8,512]{2,1,0:T(8,128)(2,1)} %bitcast.16), custom_call_target="tpu_custom_call" | custom-call | tf_op jit(solution)/shard_map/place_blocks/pallas_call | solution.py:77
  1.7 0.0 copy-start.2
  1.7 0.0 copy-start.3
  1.7 37.2 %all_to_all.15 = bf16[64,8,512]{2,1,0:T(8,128)(2,1)S(1)} all-to-all(bf16[64,8,512]{2,1,0:T(8,128)(2,1)S(1)} %get-tuple-element.9), channel_id=1, replica_groups=mesh['dp_0h'=2,'dp_0l'=2,'dp_1'=8,'dp_2'=2,'mp_0'=4,'mp_1'=2] {'dp_0h','..., dimensions={0} | all-to-all | bytes 1048576 | tf_op jit(solution)/shard_map/all_to_all | solution.py:326
  38.9 0.0 copy-done.2
  38.9 0.0 copy-done.3
  38.9 0.0 copy-start.1
  38.9 0.9 %precondition.1 = bf16[64,9,4,128]{3,2,1,0:T(4,128)(2,1)} custom-call(s32[34]{0:T(128)S(4)} %get-tuple-element.8.flag_ref, bf16[512,512]{1,0:T(8,128)(2,1)S(1)} %bitcast.9, bf16[512,512]{1,0:T(8,128)(2,1)S(1)} %bitcast.13, bf16[512,512]{1,0:T(8,128)(2,1)S(1)} %bitcast.14), custom_call_target="tpu_custom_call" | custom-call | tf_op jit(solution)/shard_map/precondition/pallas_call | solution.py:154
  39.8 0.0 copy-start
  39.8 10.4 %all-to-all-start.1 = ((bf16[64,9,4,128]{3,2,1,0:T(4,128)(2,1)}), bf16[64,9,4,128]{3,2,1,0:T(4,128)(2,1)S(1)}, u32[]{:S(2)}, u32[]{:S(2)}) async-start(bf16[64,9,4,128]{3,2,1,0:T(4,128)(2,1)} %precondition.1), calls=%async_computation.1 | async-start | bytes 1179648 | tf_op jit(solution)/shard_map/all_to_all | solution.py:331
  50.2 0.0 copy-done.1
  50.2 0.0 copy-done
  50.2 1.0 %refresh.1 = (bf16[512,512]{1,0:T(8,128)(2,1)}, bf16[512,512]{1,0:T(8,128)(2,1)}, s32[1]{0:T(128)S(4)}) custom-call(s32[34]{0:T(128)S(4)} %get-tuple-element.8.flag_ref, bf16[512,512]{1,0:T(8,128)(2,1)S(1)} %bitcast.10, f32[512,512]{1,0:T(8,128)S(1)} %bitcast.11, f32[512,512]{1,0:T(8,128)S(1)} %bitcast.12), custom_call_target="tpu_custom_call" | custom-call | tf_op jit(solution)/shard_map/refresh/pallas_call | solution.py:304
  51.2 17.5 %all-to-all-done.1.slot_ref = bf16[64,9,4,128]{3,2,1,0:T(4,128)(2,1)S(1)} async-done(((bf16[64,9,4,128]{3,2,1,0:T(4,128)(2,1)}), bf16[64,9,4,128]{3,2,1,0:T(4,128)(2,1)S(1)}, u32[]{:S(2)}, u32[]{:S(2)}) %all-to-all-start.1) | async-done | bytes 589856 | tf_op jit(solution)/shard_map/all_to_all | solution.py:331
  68.7 0.1 add_norms.1
  68.8 13.5 %all_to_all.16.norm_ref = f32[8,1,128]{2,1,0:T(1,128)S(1)} all-to-all(f32[8,1,128]{2,1,0:T(1,128)S(1)} %add_norms.1), channel_id=1, replica_groups=mesh['dp_0h'=2,'dp_0l'=2,'dp_1'=8,'dp_2'=2,'mp_0'=4,'mp_1'=2] {'mp_0','m..., dimensions={0} | all-to-all | bytes 8192 | tf_op jit(solution)/shard_map/all_to_all | solution.py:334
  82.3 0.9 %scale_blocks.1 = bf16[32,8,512]{2,1,0:T(8,128)(2,1)} custom-call(s32[34]{0:T(128)S(4)} %get-tuple-element.8.flag_ref, f32[8,1,128]{2,1,0:T(1,128)S(1)} %all_to_all.16.norm_ref, bf16[64,9,4,128]{3,2,1,0:T(4,128)(2,1)S(1)} %all-to-all-done.1.slot_ref), custom_call_target="tpu_custom_call" | custom-call | tf_op jit(solution)/shard_map/scale_blocks/pallas_call | solution.py:216
Async XLA Ops:
  1.7 37.2 %copy-start.2 = (bf16[1,1,512,512]{3,2,1,0:T(8,128)(2,1)S(1)}, bf16[1,1,512,512]{3,2,1,0:T(8,128)(2,1)}, u32[]{:S(2)}) copy-start(bf16[1,1,512,512]{3,2,1,0:T(8,128)(2,1)} %param.10) | copy-start | bytes 1572868
  1.7 37.2 %copy-start.3 = (bf16[1,1,512,512]{3,2,1,0:T(8,128)(2,1)S(1)}, bf16[1,1,512,512]{3,2,1,0:T(8,128)(2,1)}, u32[]{:S(2)}) copy-start(bf16[1,1,512,512]{3,2,1,0:T(8,128)(2,1)} %param.11) | copy-start | bytes 1572868
  38.9 11.3 %copy-start.1 = (f32[1,1,512,512]{3,2,1,0:T(8,128)S(1)}, f32[1,1,512,512]{3,2,1,0:T(8,128)}, u32[]{:S(2)}) copy-start(f32[1,1,512,512]{3,2,1,0:T(8,128)} %param.9) | copy-start | bytes 3145732
  39.8 10.4 %copy-start = (f32[1,1,512,512]{3,2,1,0:T(8,128)S(1)}, f32[1,1,512,512]{3,2,1,0:T(8,128)}, u32[]{:S(2)}) copy-start(f32[1,1,512,512]{3,2,1,0:T(8,128)} %param.8) | copy-start | bytes 3145732
  39.8 28.9 %all-to-all-start.1 = ((bf16[64,9,4,128]{3,2,1,0:T(4,128)(2,1)}), bf16[64,9,4,128]{3,2,1,0:T(4,128)(2,1)S(1)}, u32[]{:S(2)}, u32[]{:S(2)}) async-start(bf16[64,9,4,128]{3,2,1,0:T(4,128)(2,1)} %precondition.1), calls=%async_computation.1 | async-start | bytes 1179648 | tf_op jit(solution)/shard_map/all_to_all | solution.py:331

commit v7 on v5

--- a/solution.py
+++ b/solution.py
@@ -9,6 +9,8 @@
 ITERS = 2
 DP = ("dp_0h", "dp_0l", "dp_1", "dp_2")
 MP = ("mp_0", "mp_1")
+NEAR = ("dp_0h", "mp_0", "mp_1")
+PAIRS = ("dp_0l", "dp_1", "dp_2")
 LANES = 128
 TILE = 4
 PIECES = 4
@@ -92,10 +94,10 @@
     )(owners, blocks)
 
 
-def precondition(flags, grad_block, left, right, blocks_here, mp_count, row_count):
+def precondition(flags, grad_block, left, right, blocks_here, near_count, row_count):
     order = grad_block.shape[0]
     half = order // 2
-    slots = order // row_count
+    slots = half // row_count
     strip = 128
 
     def body(flag_ref, grad_ref, left_ref, right_ref, stay_ref, pass_ref, norm_ref):
@@ -113,14 +115,16 @@
             shaded = jnp.dot(grad_ref[...], right_ref[...], preferred_element_type=jnp.float32)
             shaded = shaded.astype(jnp.bfloat16)
             total = jnp.zeros((8, order), jnp.float32)
-            for i in range(order // strip):
-                rows = jnp.dot(
-                    left_ref[i * strip : (i + 1) * strip], shaded, preferred_element_type=jnp.float32
-                ).astype(jnp.bfloat16)
-                at = slice(i * strip // row_count, (i + 1) * strip // row_count)
-                stay_ref[at] = rows[:, :half].reshape(strip // row_count, row_count, half)
-                pass_ref[at] = rows[:, half:].reshape(strip // row_count, row_count, half)
-                total = squares_of(total, rows)
+            here = lax.axis_index("dp_0h")
+            for which, out_ref in ((1 - here, pass_ref), (here, stay_ref)):
+                for i in range(half // strip):
+                    first = pl.multiple_of(which * half + i * strip, strip)
+                    rows = jnp.dot(
+                        left_ref[pl.ds(first, strip)], shaded, preferred_element_type=jnp.float32
+                    ).astype(jnp.bfloat16)
+                    at = slice(i * strip // row_count, (i + 1) * strip // row_count)
+                    out_ref[at] = rows.reshape(strip // row_count, row_count, order)
+                    total = squares_of(total, rows)
             write_norm(flag_ref[1] + blocks_here, total)
 
         @pl.when(flag_ref[0] == 0)
@@ -133,9 +137,9 @@
     return pl.pallas_call(
         body,
         out_shape=(
-            pltpu.VMEM((slots, row_count, half), jnp.bfloat16),
-            pltpu.VMEM((slots, row_count, half), jnp.bfloat16),
-            pltpu.VMEM((mp_count, 1, LANES), jnp.float32),
+            pltpu.VMEM((slots, row_count, order), jnp.bfloat16),
+            pltpu.VMEM((slots, row_count, order), jnp.bfloat16),
+            pltpu.VMEM((near_count, 1, LANES), jnp.float32),
         ),
         in_specs=[SMEM, VMEM, VMEM, VMEM],
         out_specs=(VMEM, VMEM, VMEM),
@@ -144,9 +148,9 @@
     )(flags, grad_block, left, right)
 
 
-def fill_slots(flags, row_norms, passed, stays):
-    slot_count, row_count, half = stays.shape
-    tiles = row_count * half // (TILE * LANES)
+def fill_slots(flags, near_norms, passed, stays):
+    slot_count, row_count, order = stays.shape
+    tiles = row_count * order // (TILE * LANES)
     per_piece = slot_count // PIECES
 
     def body(flag_ref, norm_ref, passed_ref, stay_ref, out_any, out_ref, sems):
@@ -172,7 +176,7 @@
             for piece in range(PIECES):
                 at = pl.ds(piece * per_piece, per_piece)
                 out_ref[at, tiles] = jnp.broadcast_to(packed[None], (per_piece, TILE, LANES))
-                for t, (rows, lanes) in enumerate(tiles_of(row_count, half)):
+                for t, (rows, lanes) in enumerate(tiles_of(row_count, order)):
                     out_ref[at, t] = rows_ref[at, rows, lanes]
                 copy = pltpu.make_async_copy(out_ref.at[at], out_any.at[at], sems.at[piece])
                 copy.start()
@@ -199,14 +203,14 @@
         ],
         compiler_params=params(4),
         name="fill_slots",
-    )(flags, row_norms, passed, stays)
+    )(flags, near_norms, passed, stays)
 
 
 def scale_blocks(flags, slots, row_count):
     blocks_here = flags.shape[0] - 2
     slot_count = slots.shape[0]
     tiles = slots.shape[1] - 1
-    half = tiles * TILE * LANES // row_count
+    order = tiles * TILE * LANES // row_count
     per_piece = blocks_here // PIECES
 
     def body(flag_ref, slot_ref, out_any, out_ref, sems):
@@ -220,11 +224,10 @@
         for j in range(blocks_here):
             owner = flag_ref[2 + j]
             scale = jnp.broadcast_to(ratio[j : j + 1], (TILE, LANES))
-            for k, slot in enumerate((owner, partner_of(owner, slot_count))):
-                for t, (rows, lanes) in enumerate(tiles_of(row_count, half)):
-                    at = slice(k * half + lanes.start, k * half + lanes.stop)
-                    tile = slot_ref[slot, t].astype(jnp.float32)
-                    out_ref[j, rows, at] = (scale * tile).astype(out_ref.dtype)
+            slot = jnp.where(owner < slot_count, owner, owner - slot_count)
+            for t, (rows, lanes) in enumerate(tiles_of(row_count, order)):
+                tile = slot_ref[slot, t].astype(jnp.float32)
+                out_ref[j, rows, lanes] = (scale * tile).astype(out_ref.dtype)
             if (j + 1) % per_piece == 0:
                 piece = j // per_piece
                 at = pl.ds(piece * per_piece, per_piece)
@@ -236,11 +239,11 @@
 
     return pl.pallas_call(
         body,
-        out_shape=jax.ShapeDtypeStruct((blocks_here, row_count, 2 * half), slots.dtype),
+        out_shape=jax.ShapeDtypeStruct((blocks_here, row_count, order), slots.dtype),
         in_specs=[SMEM, VMEM],
         out_specs=ANY,
         scratch_shapes=[
-            pltpu.VMEM((blocks_here, row_count, 2 * half), slots.dtype),
+            pltpu.VMEM((blocks_here, row_count, order), slots.dtype),
             pltpu.SemaphoreType.DMA((PIECES,)),
         ],
         compiler_params=params(4),
@@ -337,7 +340,7 @@
 
 def shards(gradient, owners, left_stats, right_stats, left_roots_old, right_roots_old):
     dp_count = lax.axis_size(DP)
-    mp_count = lax.axis_size(MP)
+    near_count = lax.axis_size(NEAR)
     blocks_here = gradient.shape[1]
     row_count = gradient.shape[2]
     block_width = gradient.shape[3]
@@ -345,12 +348,12 @@
     arrived = lax.all_to_all(outgoing, DP, split_axis=0, concat_axis=0, tiled=True)
     grad_block = arrived.reshape(dp_count * row_count, block_width)
     stays, passes, norms = precondition(
-        flags, grad_block, left_roots_old[0, 0], right_roots_old[0, 0], blocks_here, mp_count, row_count
+        flags, grad_block, left_roots_old[0, 0], right_roots_old[0, 0], blocks_here, near_count, row_count
     )
     passed = lax.ppermute(passes, "dp_0h", [(0, 1), (1, 0)])
-    row_norms = lax.all_to_all(norms, MP, split_axis=0, concat_axis=0, tiled=True)
-    slots = fill_slots(flags, row_norms, passed, stays)
-    returned = lax.all_to_all(slots, DP, split_axis=0, concat_axis=0, tiled=True)
+    near_norms = lax.all_to_all(norms, NEAR, split_axis=0, concat_axis=0, tiled=True)
+    slots = fill_slots(flags, near_norms, passed, stays)
+    returned = lax.all_to_all(slots, PAIRS, split_axis=0, concat_axis=0, tiled=True)
     left_root, right_root = refresh(flags, grad_block, left_stats[0, 0], right_stats[0, 0])
     update = scale_blocks(flags, returned, row_count)[None]
     return (update, left_root[None, None], right_root[None, None])

time: 80.9 us -> 81.2 us (level)
  waiting for transfers between devices: 17.4 us -> 10.3 us
  Pallas kernels: 4.02 us -> 10.6 us
  blocking collectives: 48.1 us -> 52.7 us
  starting transfers between devices: 10.2 us -> 6.65 us
    all_to_all x1, waiting for transfers between devices: 17.4 us -> 10.3 us  [shards(): lax.all_to_all(slots, PAIRS, split_axis=0, concat_axis=0, tiled=True)]
    pallas_call x1, Pallas kernels: 1.05 us -> 6.85 us  [refresh(): pl.pallas_call(body, out_shape=(root, root), in_specs=[SMEM, VMEM, VMEM,...]
    all_to_all x1, blocking collectives: 7.24 us -> 11.9 us  [shards(): lax.all_to_all(norms, NEAR, split_axis=0, concat_axis=0, tiled=True)]
    all_to_all x1, starting transfers between devices: 5.84 us -> 3.89 us  [shards(): lax.all_to_all(slots, PAIRS, split_axis=0, concat_axis=0, tiled=True)]
    ppermute x1, starting transfers between devices: 4.4 us -> 2.77 us  [shards(): passed = lax.ppermute(passes, 'dp_0h', [(0, 1), (1, 0)])]
    pallas_call x1, Pallas kernels: 0.16 us -> 0.99 us  [precondition(): pl.pallas_call(body, out_shape=(pltpu.VMEM((slots, row_count, order), jnp...]
  transfers between devices with their start and end apart: 2 -> 2, of which waited for: 1 -> 1; matrix products, arithmetic and copies ran while one was open for 0% -> 0% of each run, Pallas kernels for 1% -> 8%
where the time goes in v7:
time: 81.2 us; the launch traced here: 81 us
  blocking collectives  52.7 us (65%)
  Pallas kernels  10.6 us (13%)
  waiting for transfers between devices  10.3 us (13%)
  starting transfers between devices  6.65 us (8%)
    all_to_all x1, blocking collectives, shards(): lax.all_to_all(outgoing, DP, split_axis=0, concat_axis=0, tiled=True)  40.8 us
    all_to_all x1, blocking collectives, shards(): lax.all_to_all(norms, NEAR, split_axis=0, concat_axis=0, tiled=True)  11.9 us
    all_to_all x1, waiting for transfers between devices, shards(): lax.all_to_all(slots, PAIRS, split_axis=0, concat_axis=0, tiled=True)  10.3 us
    pallas_call x1, Pallas kernels, refresh(): pl.pallas_call(body, out_shape=(root, root), in_specs=[SMEM, VMEM, VMEM,...  6.85 us
    all_to_all x1, starting transfers between devices, shards(): lax.all_to_all(slots, PAIRS, split_axis=0, concat_axis=0, tiled=True)  3.89 us
    ppermute x1, starting transfers between devices, shards(): passed = lax.ppermute(passes, 'dp_0h', [(0, 1), (1, 0)])  2.77 us
  transfers between devices with their start and end apart: 2, of which 1 were waited for; matrix products, arithmetic and copies ran while one was open for 0% of the time, Pallas kernels for 8%

profile of v7, /device:TPU:8, one launch (start us, length us, event | category | flops | bytes accessed | tf_op | source)
XLA Modules:
  0.0 81.0 jit_solution(15279236001432107458)
XLA Ops:
  0.6 1.0 %place_blocks.1 = (bf16[64,8,512]{2,1,0:T(8,128)(2,1)S(1)}, s32[34]{0:T(128)S(4)}) custom-call(s32[1,32]{1,0:T(1,128)} %owner_any.1, bf16[32,8,512]{2,1,0:T(8,128)(2,1)} %bitcast.16), custom_call_target="tpu_custom_call" | custom-call | tf_op jit(solution)/shard_map/place_blocks/pallas_call | solution.py:79
  1.7 0.0 copy-start.2
  1.7 0.0 copy-start.3
  1.7 40.8 %all_to_all.15 = bf16[64,8,512]{2,1,0:T(8,128)(2,1)S(1)} all-to-all(bf16[64,8,512]{2,1,0:T(8,128)(2,1)S(1)} %get-tuple-element.11), channel_id=1, replica_groups=mesh['dp_0h'=2,'dp_0l'=2,'dp_1'=8,'dp_2'=2,'mp_0'=4,'mp_1'=2] {'dp_0h','..., dimensions={0} | all-to-all | bytes 1048576 | tf_op jit(solution)/shard_map/all_to_all | solution.py:348
  42.5 0.0 copy-done.2
  42.5 0.0 copy-done.3
  42.5 0.0 copy-start.1
  42.5 1.0 %precondition.1 = (bf16[32,8,512]{2,1,0:T(8,128)(2,1)S(1)}, bf16[32,8,512]{2,1,0:T(8,128)(2,1)S(1)}, f32[16,1,128]{2,1,0:T(1,128)S(1)}) custom-call(s32[34]{0:T(128)S(4)} %get-tuple-element.10.flag_ref, bf16[512,512]{1,0:T(8,128)(2,1)S(1)} %bitcast.9, bf16[512,512]{1,0:T(8,128)(2,1)S(1)} %bitcast.13, bf16[512,512]{1,0:T(8,128)(2,1)S(1)} %bitcast.14), custom_call_target="tpu_custom_call" | custom-call | tf_op jit(solution)/shard_map/precondition/pallas_call | solution.py:137
  43.5 0.0 copy-start
  43.5 2.8 %collective-permute-start = (bf16[32,8,512]{2,1,0:T(8,128)(2,1)S(1)}, bf16[32,8,512]{2,1,0:T(8,128)(2,1)S(1)}, u32[]{:S(2)}, u32[]{:S(2)}) collective-permute-start(bf16[32,8,512]{2,1,0:T(8,128)(2,1)S(1)} %get-tuple-element.13), channel_id=1, source_target_pairs={{0,256},{256,0},{1,257},{257,1},{2,258},{258,2},{3,259},{259,3},{4... | collective-permute-start | bytes 786440 | tf_op jit(solution)/shard_map/ppermute | solution.py:353
  46.3 11.9 %all_to_all.16.norm_ref = f32[16,1,128]{2,1,0:T(1,128)S(1)} all-to-all(f32[16,1,128]{2,1,0:T(1,128)S(1)} %get-tuple-element.12), channel_id=1, replica_groups=mesh['dp_0h'=2,'dp_0l'=2,'dp_1'=8,'dp_2'=2,'mp_0'=4,'mp_1'=2] {'dp_0h','..., dimensions={0} | all-to-all | bytes 16384 | tf_op jit(solution)/shard_map/all_to_all | solution.py:354
  58.2 0.0 collective-permute-done.passed_ref
  58.2 0.8 fill_slots.1
  59.0 3.9 %all-to-all-start.2 = ((bf16[32,9,4,128]{3,2,1,0:T(4,128)(2,1)}), bf16[32,9,4,128]{3,2,1,0:T(4,128)(2,1)S(1)}, u32[]{:S(2)}, u32[]{:S(2)}) async-start(bf16[32,9,4,128]{3,2,1,0:T(4,128)(2,1)} %fill_slots.1), calls=%async_computation.2 | async-start | bytes 589824 | tf_op jit(solution)/shard_map/all_to_all | solution.py:356
  62.9 0.0 copy-done.1
  62.9 0.0 copy-done
  62.9 6.8 %refresh.1 = (bf16[512,512]{1,0:T(8,128)(2,1)}, bf16[512,512]{1,0:T(8,128)(2,1)}) custom-call(s32[34]{0:T(128)S(4)} %get-tuple-element.10.flag_ref, bf16[512,512]{1,0:T(8,128)(2,1)S(1)} %bitcast.10, f32[512,512]{1,0:T(8,128)S(1)} %bitcast.11, f32[512,512]{1,0:T(8,128)S(1)} %bitcast.12), custom_call_target="tpu_custom_call" | custom-call | tf_op jit(solution)/shard_map/refresh/pallas_call | solution.py:326
  69.8 10.3 %all-to-all-done.2.slot_ref = bf16[32,9,4,128]{3,2,1,0:T(4,128)(2,1)S(1)} async-done(((bf16[32,9,4,128]{3,2,1,0:T(4,128)(2,1)}), bf16[32,9,4,128]{3,2,1,0:T(4,128)(2,1)S(1)}, u32[]{:S(2)}, u32[]{:S(2)}) %all-to-all-start.2) | async-done | bytes 294944 | tf_op jit(solution)/shard_map/all_to_all | solution.py:356
  80.1 0.9 %scale_blocks.1 = bf16[32,8,512]{2,1,0:T(8,128)(2,1)} custom-call(s32[34]{0:T(128)S(4)} %get-tuple-element.10.flag_ref, bf16[32,9,4,128]{3,2,1,0:T(4,128)(2,1)S(1)} %all-to-all-done.2.slot_ref), custom_call_target="tpu_custom_call" | custom-call | tf_op jit(solution)/shard_map/scale_blocks/pallas_call | solution.py:240
Async XLA Ops:
  1.7 40.9 %copy-start.2 = (bf16[1,1,512,512]{3,2,1,0:T(8,128)(2,1)S(1)}, bf16[1,1,512,512]{3,2,1,0:T(8,128)(2,1)}, u32[]{:S(2)}) copy-start(bf16[1,1,512,512]{3,2,1,0:T(8,128)(2,1)} %param.10) | copy-start | bytes 1572868
  1.7 40.8 %copy-start.3 = (bf16[1,1,512,512]{3,2,1,0:T(8,128)(2,1)S(1)}, bf16[1,1,512,512]{3,2,1,0:T(8,128)(2,1)}, u32[]{:S(2)}) copy-start(bf16[1,1,512,512]{3,2,1,0:T(8,128)(2,1)} %param.11) | copy-start | bytes 1572868
  42.5 20.4 %copy-start.1 = (f32[1,1,512,512]{3,2,1,0:T(8,128)S(1)}, f32[1,1,512,512]{3,2,1,0:T(8,128)}, u32[]{:S(2)}) copy-start(f32[1,1,512,512]{3,2,1,0:T(8,128)} %param.9) | copy-start | bytes 3145732
  43.5 19.4 %copy-start = (f32[1,1,512,512]{3,2,1,0:T(8,128)S(1)}, f32[1,1,512,512]{3,2,1,0:T(8,128)}, u32[]{:S(2)}) copy-start(f32[1,1,512,512]{3,2,1,0:T(8,128)} %param.8) | copy-start | bytes 3145732
  43.5 14.6 %collective-permute-start = (bf16[32,8,512]{2,1,0:T(8,128)(2,1)S(1)}, bf16[32,8,512]{2,1,0:T(8,128)(2,1)S(1)}, u32[]{:S(2)}, u32[]{:S(2)}) collective-permute-start(bf16[32,8,512]{2,1,0:T(8,128)(2,1)S(1)} %get-tuple-element.13), channel_id=1, source_target_pairs={{0,256},{256,0},{1,257},{257,1},{2,258},{258,2},{3,259},{259,3},{4... | collective-permute-start | bytes 786440 | tf_op jit(solution)/shard_map/ppermute | solution.py:353
  59.0 21.1 %all-to-all-start.2 = ((bf16[32,9,4,128]{3,2,1,0:T(4,128)(2,1)}), bf16[32,9,4,128]{3,2,1,0:T(4,128)(2,1)S(1)}, u32[]{:S(2)}, u32[]{:S(2)}) async-start(bf16[32,9,4,128]{3,2,1,0:T(4,128)(2,1)} %fill_slots.1), calls=%async_computation.2 | async-start | bytes 589824 | tf_op jit(solution)/shard_map/all_to_all | solution.py:356

commit v8 on v5

--- a/solution.py
+++ b/solution.py
@@ -12,6 +12,7 @@
 LANES = 128
 TILE = 4
 PIECES = 4
+CHAINS = 8
 MIB = 1024 * 1024
 PLACE_MIB = 54
 
@@ -150,6 +151,25 @@
     per_piece = slot_count // PIECES
 
     def body(flag_ref, norm_ref, passed_ref, stay_ref, out_any, out_ref, sems):
+        def piece_copy(piece):
+            at = (pl.ds(piece * per_piece, per_piece), pl.ds(0, tiles))
+            return pltpu.make_async_copy(out_ref.at[at], out_any.at[at], sems.at[piece])
+
+        def fill(rows_ref):
+            for piece in range(PIECES):
+                at = pl.ds(piece * per_piece, per_piece)
+                for t, (rows, lanes) in enumerate(tiles_of(row_count, half)):
+                    out_ref[at, t] = rows_ref[at, rows, lanes]
+                piece_copy(piece).start()
+
+        @pl.when(flag_ref[0] == 1)
+        def _():
+            fill(stay_ref)
+
+        @pl.when(flag_ref[0] == 0)
+        def _():
+            fill(passed_ref)
+
         total = jnp.sum(norm_ref[...], axis=0)
         high = total.astype(jnp.bfloat16).astype(jnp.float32)
         rest = total - high
@@ -166,27 +186,12 @@
                 jnp.where(row == 2, jnp.broadcast_to(low, shape), 0.0),
             ),
         ).astype(jnp.bfloat16)
-
-        def fill(rows_ref):
-            copies = []
-            for piece in range(PIECES):
-                at = pl.ds(piece * per_piece, per_piece)
-                out_ref[at, tiles] = jnp.broadcast_to(packed[None], (per_piece, TILE, LANES))
-                for t, (rows, lanes) in enumerate(tiles_of(row_count, half)):
-                    out_ref[at, t] = rows_ref[at, rows, lanes]
-                copy = pltpu.make_async_copy(out_ref.at[at], out_any.at[at], sems.at[piece])
-                copy.start()
-                copies.append(copy)
-            for copy in copies:
-                copy.wait()
-
-        @pl.when(flag_ref[0] == 1)
-        def _():
-            fill(stay_ref)
-
-        @pl.when(flag_ref[0] == 0)
-        def _():
-            fill(passed_ref)
+        out_ref[:, tiles] = jnp.broadcast_to(packed[None], (slot_count, TILE, LANES))
+        norm_copy = pltpu.make_async_copy(out_ref.at[:, tiles], out_any.at[:, tiles], sems.at[PIECES])
+        norm_copy.start()
+        for piece in range(PIECES):
+            piece_copy(piece).wait()
+        norm_copy.wait()
 
     return pl.pallas_call(
         body,
@@ -195,7 +200,7 @@
         out_specs=ANY,
         scratch_shapes=[
             pltpu.VMEM((slot_count, tiles + 1, TILE, LANES), stays.dtype),
-            pltpu.SemaphoreType.DMA((PIECES,)),
+            pltpu.SemaphoreType.DMA((PIECES + 1,)),
         ],
         compiler_params=params(4),
         name="fill_slots",
@@ -211,7 +216,12 @@
 
     def body(flag_ref, slot_ref, out_any, out_ref, sems):
         copies = []
-        norms = jnp.sum(slot_ref[:, tiles].astype(jnp.float32), axis=0)
+        chains = [slot_ref[p, tiles].astype(jnp.float32) for p in range(CHAINS)]
+        for p in range(CHAINS, slot_count):
+            chains[p % CHAINS] = chains[p % CHAINS] + slot_ref[p, tiles].astype(jnp.float32)
+        while len(chains) > 1:
+            chains = [one + two for one, two in zip(chains[::2], chains[1::2])]
+        norms = chains[0]
         totals = norms[0:1] + (norms[1:2] + norms[2:3])
         columns = jnp.broadcast_to(totals, (LANES, LANES)).T
         ratio = jnp.sqrt(

time: 80.9 us -> 80.9 us (level)
  no operation moved by 1% of the time
where the time goes in v8:
time: 80.9 us; the launch traced here: 80.5 us
  blocking collectives  48.1 us (59%)
  waiting for transfers between devices  17.4 us (22%)
  starting transfers between devices  10.2 us (13%)
  Pallas kernels  4.01 us (5%)
    all_to_all x1, blocking collectives, shards(): lax.all_to_all(outgoing, DP, split_axis=0, concat_axis=0, tiled=True)  40.8 us
    all_to_all x1, waiting for transfers between devices, shards(): lax.all_to_all(slots, DP, split_axis=0, concat_axis=0, tiled=True)  17.4 us
    all_to_all x1, blocking collectives, shards(): lax.all_to_all(norms, MP, split_axis=0, concat_axis=0, tiled=True)  7.24 us
    all_to_all x1, starting transfers between devices, shards(): lax.all_to_all(slots, DP, split_axis=0, concat_axis=0, tiled=True)  5.84 us
    ppermute x1, starting transfers between devices, shards(): passed = lax.ppermute(passes, 'dp_0h', [(0, 1), (1, 0)])  4.4 us
  transfers between devices with their start and end apart: 2, of which 1 were waited for; matrix products, arithmetic and copies ran while one was open for 0% of the time, Pallas kernels for 1%

profile of v8, /device:TPU:8, one launch (start us, length us, event | category | flops | bytes accessed | tf_op | source)
XLA Modules:
  0.0 80.5 jit_solution(7838423145102139089)
XLA Ops:
  0.6 1.0 %place_blocks.1 = (bf16[64,8,512]{2,1,0:T(8,128)(2,1)S(1)}, s32[34]{0:T(128)S(4)}) custom-call(s32[1,32]{1,0:T(1,128)} %owner_any.1, bf16[32,8,512]{2,1,0:T(8,128)(2,1)} %bitcast.15), custom_call_target="tpu_custom_call" | custom-call | tf_op jit(solution)/shard_map/place_blocks/pallas_call | solution.py:78
  1.7 0.0 copy-start.2
  1.7 0.0 copy-start.3
  1.7 40.8 %all_to_all.15 = bf16[64,8,512]{2,1,0:T(8,128)(2,1)S(1)} all-to-all(bf16[64,8,512]{2,1,0:T(8,128)(2,1)S(1)} %get-tuple-element.11), channel_id=1, replica_groups=mesh['dp_0h'=2,'dp_0l'=2,'dp_1'=8,'dp_2'=2,'mp_0'=4,'mp_1'=2] {'dp_0h','..., dimensions={0} | all-to-all | bytes 1048576 | tf_op jit(solution)/shard_map/all_to_all | solution.py:355
  42.5 0.0 copy-done.2
  42.5 0.0 copy-done.3
  42.5 0.0 copy-start.1
  42.5 0.2 precondition.1
  42.7 0.0 copy-start
  42.7 4.4 %collective-permute-start = (bf16[64,8,256]{2,1,0:T(8,128)(2,1)S(1)}, bf16[64,8,256]{2,1,0:T(8,128)(2,1)S(1)}, u32[]{:S(2)}, u32[]{:S(2)}) collective-permute-start(bf16[64,8,256]{2,1,0:T(8,128)(2,1)S(1)} %get-tuple-element.13), channel_id=1, source_target_pairs={{0,256},{256,0},{1,257},{257,1},{2,258},{258,2},{3,259},{259,3},{4... | collective-permute-start | bytes 786440 | tf_op jit(solution)/shard_map/ppermute | solution.py:360
  47.1 7.2 %all_to_all.16.norm_ref = f32[8,1,128]{2,1,0:T(1,128)S(1)} all-to-all(f32[8,1,128]{2,1,0:T(1,128)S(1)} %get-tuple-element.12), channel_id=1, replica_groups=mesh['dp_0h'=2,'dp_0l'=2,'dp_1'=8,'dp_2'=2,'mp_0'=4,'mp_1'=2] {'mp_0','m..., dimensions={0} | all-to-all | bytes 8192 | tf_op jit(solution)/shard_map/all_to_all | solution.py:361
  54.4 0.0 collective-permute-done.passed_ref
  54.4 0.9 %fill_slots.1 = bf16[64,5,4,128]{3,2,1,0:T(4,128)(2,1)} custom-call(s32[34]{0:T(128)S(4)} %get-tuple-element.10.flag_ref, f32[8,1,128]{2,1,0:T(1,128)S(1)} %all_to_all.16.norm_ref, bf16[64,8,256]{2,1,0:T(8,128)(2,1)S(1)} %collective-permute-done.passed_ref, bf16[64,8,256]{2,1,0:T(8,128)(2,1)S(1)} %get-tuple-element.14.stay_ref), custom_call_target="tpu_custom_call" | custom-call | tf_op jit(solution)/shard_map/fill_slots/pallas_call | solution.py:196
  55.2 5.8 %all-to-all-start.2 = ((bf16[64,5,4,128]{3,2,1,0:T(4,128)(2,1)}), bf16[64,5,4,128]{3,2,1,0:T(4,128)(2,1)S(1)}, u32[]{:S(2)}, u32[]{:S(2)}) async-start(bf16[64,5,4,128]{3,2,1,0:T(4,128)(2,1)} %fill_slots.1), calls=%async_computation.2 | async-start | bytes 655360 | tf_op jit(solution)/shard_map/all_to_all | solution.py:363
  61.1 0.0 copy-done.1
  61.1 0.0 copy-done
  61.1 1.0 %refresh.1 = (bf16[512,512]{1,0:T(8,128)(2,1)}, bf16[512,512]{1,0:T(8,128)(2,1)}) custom-call(s32[34]{0:T(128)S(4)} %get-tuple-element.10.flag_ref, bf16[512,512]{1,0:T(8,128)(2,1)S(1)} %bitcast.10, f32[512,512]{1,0:T(8,128)S(1)} %bitcast.11, f32[512,512]{1,0:T(8,128)S(1)} %bitcast.12), custom_call_target="tpu_custom_call" | custom-call | tf_op jit(solution)/shard_map/refresh/pallas_call | solution.py:333
  62.2 17.4 %all-to-all-done.2.slot_ref = bf16[64,5,4,128]{3,2,1,0:T(4,128)(2,1)S(1)} async-done(((bf16[64,5,4,128]{3,2,1,0:T(4,128)(2,1)}), bf16[64,5,4,128]{3,2,1,0:T(4,128)(2,1)S(1)}, u32[]{:S(2)}, u32[]{:S(2)}) %all-to-all-start.2) | async-done | bytes 327712 | tf_op jit(solution)/shard_map/all_to_all | solution.py:363
  79.6 0.9 %scale_blocks.1 = bf16[32,8,512]{2,1,0:T(8,128)(2,1)} custom-call(s32[34]{0:T(128)S(4)} %get-tuple-element.10.flag_ref, bf16[64,5,4,128]{3,2,1,0:T(4,128)(2,1)S(1)} %all-to-all-done.2.slot_ref), custom_call_target="tpu_custom_call" | custom-call | tf_op jit(solution)/shard_map/scale_blocks/pallas_call | solution.py:247
Async XLA Ops:
  1.7 40.9 %copy-start.2 = (bf16[1,1,512,512]{3,2,1,0:T(8,128)(2,1)S(1)}, bf16[1,1,512,512]{3,2,1,0:T(8,128)(2,1)}, u32[]{:S(2)}) copy-start(bf16[1,1,512,512]{3,2,1,0:T(8,128)(2,1)} %param.10) | copy-start | bytes 1572868
  1.7 40.8 %copy-start.3 = (bf16[1,1,512,512]{3,2,1,0:T(8,128)(2,1)S(1)}, bf16[1,1,512,512]{3,2,1,0:T(8,128)(2,1)}, u32[]{:S(2)}) copy-start(bf16[1,1,512,512]{3,2,1,0:T(8,128)(2,1)} %param.11) | copy-start | bytes 1572868
  42.5 18.6 %copy-start.1 = (f32[1,1,512,512]{3,2,1,0:T(8,128)S(1)}, f32[1,1,512,512]{3,2,1,0:T(8,128)}, u32[]{:S(2)}) copy-start(f32[1,1,512,512]{3,2,1,0:T(8,128)} %param.9) | copy-start | bytes 3145732
  42.7 18.4 %copy-start = (f32[1,1,512,512]{3,2,1,0:T(8,128)S(1)}, f32[1,1,512,512]{3,2,1,0:T(8,128)}, u32[]{:S(2)}) copy-start(f32[1,1,512,512]{3,2,1,0:T(8,128)} %param.8) | copy-start | bytes 3145732
  42.7 11.7 %collective-permute-start = (bf16[64,8,256]{2,1,0:T(8,128)(2,1)S(1)}, bf16[64,8,256]{2,1,0:T(8,128)(2,1)S(1)}, u32[]{:S(2)}, u32[]{:S(2)}) collective-permute-start(bf16[64,8,256]{2,1,0:T(8,128)(2,1)S(1)} %get-tuple-element.13), channel_id=1, source_target_pairs={{0,256},{256,0},{1,257},{257,1},{2,258},{258,2},{3,259},{259,3},{4... | collective-permute-start | bytes 786440 | tf_op jit(solution)/shard_map/ppermute | solution.py:360
  55.2 24.3 %all-to-all-start.2 = ((bf16[64,5,4,128]{3,2,1,0:T(4,128)(2,1)}), bf16[64,5,4,128]{3,2,1,0:T(4,128)(2,1)S(1)}, u32[]{:S(2)}, u32[]{:S(2)}) async-start(bf16[64,5,4,128]{3,2,1,0:T(4,128)(2,1)} %fill_slots.1), calls=%async_computation.2 | async-start | bytes 655360 | tf_op jit(solution)/shard_map/all_to_all | solution.py:363

commit v9 on v8

--- a/solution.py
+++ b/solution.py
@@ -11,7 +11,7 @@
 MP = ("mp_0", "mp_1")
 LANES = 128
 TILE = 4
-PIECES = 4
+PIECES = 8
 CHAINS = 8
 MIB = 1024 * 1024
 PLACE_MIB = 54

time: 80.9 us -> 80.9 us (level)
  Pallas kernels: 4.01 us -> 10.7 us
  waiting for transfers between devices: 17.4 us -> 11.7 us
  starting transfers between devices: 10.2 us -> 8.42 us
  blocking collectives: 48.1 us -> 49 us
    all_to_all x1, waiting for transfers between devices: 17.4 us -> 11.6 us  [shards(): lax.all_to_all(slots, DP, split_axis=0, concat_axis=0, tiled=True)]
    pallas_call x1, Pallas kernels: 1.05 us -> 6.85 us  [refresh(): pl.pallas_call(body, out_shape=(root, root), in_specs=[SMEM, VMEM, VMEM,...]
    ppermute x1, starting transfers between devices: 4.4 us -> 2.78 us  [shards(): passed = lax.ppermute(passes, 'dp_0h', [(0, 1), (1, 0)])]
    all_to_all x1, blocking collectives: 7.24 us -> 8.18 us  [shards(): lax.all_to_all(norms, MP, split_axis=0, concat_axis=0, tiled=True)]
    pallas_call x1, Pallas kernels: 0.16 us -> 0.98 us  [precondition(): pl.pallas_call(body, out_shape=(pltpu.VMEM((slots, row_count, half), jnp....]
  transfers between devices with their start and end apart: 2 -> 2, of which waited for: 1 -> 2; matrix products, arithmetic and copies ran while one was open for 0% -> 0% of each run, Pallas kernels for 1% -> 9%
where the time goes in v9:
time: 80.9 us; the launch traced here: 80.5 us
  blocking collectives  49 us (61%)
  waiting for transfers between devices  11.7 us (14%)
  Pallas kernels  10.7 us (13%)
  starting transfers between devices  8.42 us (10%)
    all_to_all x1, blocking collectives, shards(): lax.all_to_all(outgoing, DP, split_axis=0, concat_axis=0, tiled=True)  40.8 us
    all_to_all x1, waiting for transfers between devices, shards(): lax.all_to_all(slots, DP, split_axis=0, concat_axis=0, tiled=True)  11.6 us
    all_to_all x1, blocking collectives, shards(): lax.all_to_all(norms, MP, split_axis=0, concat_axis=0, tiled=True)  8.18 us
    pallas_call x1, Pallas kernels, refresh(): pl.pallas_call(body, out_shape=(root, root), in_specs=[SMEM, VMEM, VMEM,...  6.85 us
    all_to_all x1, starting transfers between devices, shards(): lax.all_to_all(slots, DP, split_axis=0, concat_axis=0, tiled=True)  5.65 us
    ppermute x1, starting transfers between devices, shards(): passed = lax.ppermute(passes, 'dp_0h', [(0, 1), (1, 0)])  2.78 us
  transfers between devices with their start and end apart: 2, of which 2 were waited for; matrix products, arithmetic and copies ran while one was open for 0% of the time, Pallas kernels for 9%

profile of v9, /device:TPU:8, one launch (start us, length us, event | category | flops | bytes accessed | tf_op | source)
XLA Modules:
  0.0 80.5 jit_solution(10176019381783373123)
XLA Ops:
  0.6 1.0 %place_blocks.1 = (bf16[64,8,512]{2,1,0:T(8,128)(2,1)S(1)}, s32[34]{0:T(128)S(4)}) custom-call(s32[1,32]{1,0:T(1,128)} %owner_any.1, bf16[32,8,512]{2,1,0:T(8,128)(2,1)} %bitcast.15), custom_call_target="tpu_custom_call" | custom-call | tf_op jit(solution)/shard_map/place_blocks/pallas_call | solution.py:78
  1.6 0.0 copy-start.2
  1.7 0.0 copy-start.3
  1.7 40.8 %all_to_all.15 = bf16[64,8,512]{2,1,0:T(8,128)(2,1)S(1)} all-to-all(bf16[64,8,512]{2,1,0:T(8,128)(2,1)S(1)} %get-tuple-element.11), channel_id=1, replica_groups=mesh['dp_0h'=2,'dp_0l'=2,'dp_1'=8,'dp_2'=2,'mp_0'=4,'mp_1'=2] {'dp_0h','..., dimensions={0} | all-to-all | bytes 1048576 | tf_op jit(solution)/shard_map/all_to_all | solution.py:355
  42.5 0.0 copy-done.2
  42.5 0.0 copy-done.3
  42.5 0.0 copy-start.1
  42.5 1.0 %precondition.1 = (bf16[64,8,256]{2,1,0:T(8,128)(2,1)S(1)}, bf16[64,8,256]{2,1,0:T(8,128)(2,1)S(1)}, f32[8,1,128]{2,1,0:T(1,128)S(1)}) custom-call(s32[34]{0:T(128)S(4)} %get-tuple-element.10.flag_ref, bf16[512,512]{1,0:T(8,128)(2,1)S(1)} %bitcast.9, bf16[512,512]{1,0:T(8,128)(2,1)S(1)} %bitcast.13, bf16[512,512]{1,0:T(8,128)(2,1)S(1)} %bitcast.14), custom_call_target="tpu_custom_call" | custom-call | tf_op jit(solution)/shard_map/precondition/pallas_call | solution.py:134
  43.5 0.0 copy-start
  43.5 2.8 %collective-permute-start = (bf16[64,8,256]{2,1,0:T(8,128)(2,1)S(1)}, bf16[64,8,256]{2,1,0:T(8,128)(2,1)S(1)}, u32[]{:S(2)}, u32[]{:S(2)}) collective-permute-start(bf16[64,8,256]{2,1,0:T(8,128)(2,1)S(1)} %get-tuple-element.13), channel_id=1, source_target_pairs={{0,256},{256,0},{1,257},{257,1},{2,258},{258,2},{3,259},{259,3},{4... | collective-permute-start | bytes 786440 | tf_op jit(solution)/shard_map/ppermute | solution.py:360
  46.3 8.2 %all_to_all.16.norm_ref = f32[8,1,128]{2,1,0:T(1,128)S(1)} all-to-all(f32[8,1,128]{2,1,0:T(1,128)S(1)} %get-tuple-element.12), channel_id=1, replica_groups=mesh['dp_0h'=2,'dp_0l'=2,'dp_1'=8,'dp_2'=2,'mp_0'=4,'mp_1'=2] {'mp_0','m..., dimensions={0} | all-to-all | bytes 8192 | tf_op jit(solution)/shard_map/all_to_all | solution.py:361
  54.5 0.1 collective-permute-done.passed_ref
  54.5 0.9 %fill_slots.1 = bf16[64,5,4,128]{3,2,1,0:T(4,128)(2,1)} custom-call(s32[34]{0:T(128)S(4)} %get-tuple-element.10.flag_ref, f32[8,1,128]{2,1,0:T(1,128)S(1)} %all_to_all.16.norm_ref, bf16[64,8,256]{2,1,0:T(8,128)(2,1)S(1)} %collective-permute-done.passed_ref, bf16[64,8,256]{2,1,0:T(8,128)(2,1)S(1)} %get-tuple-element.14.stay_ref), custom_call_target="tpu_custom_call" | custom-call | tf_op jit(solution)/shard_map/fill_slots/pallas_call | solution.py:196
  55.4 5.6 %all-to-all-start.2 = ((bf16[64,5,4,128]{3,2,1,0:T(4,128)(2,1)}), bf16[64,5,4,128]{3,2,1,0:T(4,128)(2,1)S(1)}, u32[]{:S(2)}, u32[]{:S(2)}) async-start(bf16[64,5,4,128]{3,2,1,0:T(4,128)(2,1)} %fill_slots.1), calls=%async_computation.2 | async-start | bytes 655360 | tf_op jit(solution)/shard_map/all_to_all | solution.py:363
  61.1 0.0 copy-done.1
  61.1 0.0 copy-done
  61.1 6.8 %refresh.1 = (bf16[512,512]{1,0:T(8,128)(2,1)}, bf16[512,512]{1,0:T(8,128)(2,1)}) custom-call(s32[34]{0:T(128)S(4)} %get-tuple-element.10.flag_ref, bf16[512,512]{1,0:T(8,128)(2,1)S(1)} %bitcast.10, f32[512,512]{1,0:T(8,128)S(1)} %bitcast.11, f32[512,512]{1,0:T(8,128)S(1)} %bitcast.12), custom_call_target="tpu_custom_call" | custom-call | tf_op jit(solution)/shard_map/refresh/pallas_call | solution.py:333
  68.0 11.6 %all-to-all-done.2.slot_ref = bf16[64,5,4,128]{3,2,1,0:T(4,128)(2,1)S(1)} async-done(((bf16[64,5,4,128]{3,2,1,0:T(4,128)(2,1)}), bf16[64,5,4,128]{3,2,1,0:T(4,128)(2,1)S(1)}, u32[]{:S(2)}, u32[]{:S(2)}) %all-to-all-start.2) | async-done | bytes 327712 | tf_op jit(solution)/shard_map/all_to_all | solution.py:363
  79.6 0.9 %scale_blocks.1 = bf16[32,8,512]{2,1,0:T(8,128)(2,1)} custom-call(s32[34]{0:T(128)S(4)} %get-tuple-element.10.flag_ref, bf16[64,5,4,128]{3,2,1,0:T(4,128)(2,1)S(1)} %all-to-all-done.2.slot_ref), custom_call_target="tpu_custom_call" | custom-call | tf_op jit(solution)/shard_map/scale_blocks/pallas_call | solution.py:247
Async XLA Ops:
  1.6 40.9 %copy-start.2 = (bf16[1,1,512,512]{3,2,1,0:T(8,128)(2,1)S(1)}, bf16[1,1,512,512]{3,2,1,0:T(8,128)(2,1)}, u32[]{:S(2)}) copy-start(bf16[1,1,512,512]{3,2,1,0:T(8,128)(2,1)} %param.10) | copy-start | bytes 1572868
  1.7 40.8 %copy-start.3 = (bf16[1,1,512,512]{3,2,1,0:T(8,128)(2,1)S(1)}, bf16[1,1,512,512]{3,2,1,0:T(8,128)(2,1)}, u32[]{:S(2)}) copy-start(bf16[1,1,512,512]{3,2,1,0:T(8,128)(2,1)} %param.11) | copy-start | bytes 1572868
  42.5 18.6 %copy-start.1 = (f32[1,1,512,512]{3,2,1,0:T(8,128)S(1)}, f32[1,1,512,512]{3,2,1,0:T(8,128)}, u32[]{:S(2)}) copy-start(f32[1,1,512,512]{3,2,1,0:T(8,128)} %param.9) | copy-start | bytes 3145732
  43.5 17.6 %copy-start = (f32[1,1,512,512]{3,2,1,0:T(8,128)S(1)}, f32[1,1,512,512]{3,2,1,0:T(8,128)}, u32[]{:S(2)}) copy-start(f32[1,1,512,512]{3,2,1,0:T(8,128)} %param.8) | copy-start | bytes 3145732
  43.5 11.0 %collective-permute-start = (bf16[64,8,256]{2,1,0:T(8,128)(2,1)S(1)}, bf16[64,8,256]{2,1,0:T(8,128)(2,1)S(1)}, u32[]{:S(2)}, u32[]{:S(2)}) collective-permute-start(bf16[64,8,256]{2,1,0:T(8,128)(2,1)S(1)} %get-tuple-element.13), channel_id=1, source_target_pairs={{0,256},{256,0},{1,257},{257,1},{2,258},{258,2},{3,259},{259,3},{4... | collective-permute-start | bytes 786440 | tf_op jit(solution)/shard_map/ppermute | solution.py:360
  55.4 24.1 %all-to-all-start.2 = ((bf16[64,5,4,128]{3,2,1,0:T(4,128)(2,1)}), bf16[64,5,4,128]{3,2,1,0:T(4,128)(2,1)S(1)}, u32[]{:S(2)}, u32[]{:S(2)}) async-start(bf16[64,5,4,128]{3,2,1,0:T(4,128)(2,1)} %fill_slots.1), calls=%async_computation.2 | async-start | bytes 655360 | tf_op jit(solution)/shard_map/all_to_all | solution.py:363

commit v10 on v5

--- a/solution.py
+++ b/solution.py
@@ -11,7 +11,8 @@
 MP = ("mp_0", "mp_1")
 LANES = 128
 TILE = 4
-PIECES = 4
+PIECES = 8
+CHAINS = 8
 MIB = 1024 * 1024
 PLACE_MIB = 54
 
@@ -211,7 +212,12 @@
 
     def body(flag_ref, slot_ref, out_any, out_ref, sems):
         copies = []
-        norms = jnp.sum(slot_ref[:, tiles].astype(jnp.float32), axis=0)
+        chains = [slot_ref[p, tiles].astype(jnp.float32) for p in range(CHAINS)]
+        for p in range(CHAINS, slot_count):
+            chains[p % CHAINS] = chains[p % CHAINS] + slot_ref[p, tiles].astype(jnp.float32)
+        while len(chains) > 1:
+            chains = [one + two for one, two in zip(chains[::2], chains[1::2])]
+        norms = chains[0]
         totals = norms[0:1] + (norms[1:2] + norms[2:3])
         columns = jnp.broadcast_to(totals, (LANES, LANES)).T
         ratio = jnp.sqrt(

time: 80.9 us -> 81 us (level)
  Pallas kernels: 4.02 us -> 10.6 us
  waiting for transfers between devices: 17.4 us -> 12.5 us
  starting transfers between devices: 10.2 us -> 8.57 us
    pallas_call x1, Pallas kernels: 1.05 us -> 6.85 us  [refresh(): pl.pallas_call(body, out_shape=(root, root), in_specs=[SMEM, VMEM, VMEM,...]
    all_to_all x1, waiting for transfers between devices: 17.4 us -> 11.6 us  [shards(): lax.all_to_all(slots, DP, split_axis=0, concat_axis=0, tiled=True)]
    ppermute x1, starting transfers between devices: 4.4 us -> 2.78 us  [shards(): passed = lax.ppermute(passes, 'dp_0h', [(0, 1), (1, 0)])]
    ppermute x1, waiting for transfers between devices: 0.01 us -> 0.88 us  [shards(): passed = lax.ppermute(passes, 'dp_0h', [(0, 1), (1, 0)])]
    pallas_call x1, Pallas kernels: 0.16 us -> 0.98 us  [precondition(): pl.pallas_call(body, out_shape=(pltpu.VMEM((slots, row_count, half), jnp....]
  transfers between devices with their start and end apart: 2 -> 2, of which waited for: 1 -> 2; matrix products, arithmetic and copies ran while one was open for 0% -> 0% of each run, Pallas kernels for 1% -> 9%
where the time goes in v10:
time: 81 us; the launch traced here: 80.6 us
  blocking collectives  48.2 us (60%)
  waiting for transfers between devices  12.5 us (15%)
  Pallas kernels  10.6 us (13%)
  starting transfers between devices  8.57 us (11%)
    all_to_all x1, blocking collectives, shards(): lax.all_to_all(outgoing, DP, split_axis=0, concat_axis=0, tiled=True)  40.8 us
    all_to_all x1, waiting for transfers between devices, shards(): lax.all_to_all(slots, DP, split_axis=0, concat_axis=0, tiled=True)  11.6 us
    all_to_all x1, blocking collectives, shards(): lax.all_to_all(norms, MP, split_axis=0, concat_axis=0, tiled=True)  7.37 us
    pallas_call x1, Pallas kernels, refresh(): pl.pallas_call(body, out_shape=(root, root), in_specs=[SMEM, VMEM, VMEM,...  6.85 us
    all_to_all x1, starting transfers between devices, shards(): lax.all_to_all(slots, DP, split_axis=0, concat_axis=0, tiled=True)  5.79 us
    ppermute x1, starting transfers between devices, shards(): passed = lax.ppermute(passes, 'dp_0h', [(0, 1), (1, 0)])  2.78 us
  transfers between devices with their start and end apart: 2, of which 2 were waited for; matrix products, arithmetic and copies ran while one was open for 0% of the time, Pallas kernels for 9%

profile of v10, /device:TPU:8, one launch (start us, length us, event | category | flops | bytes accessed | tf_op | source)
XLA Modules:
  0.0 80.6 jit_solution(3823781428991290047)
XLA Ops:
  0.6 1.0 %place_blocks.1 = (bf16[64,8,512]{2,1,0:T(8,128)(2,1)S(1)}, s32[34]{0:T(128)S(4)}) custom-call(s32[1,32]{1,0:T(1,128)} %owner_any.1, bf16[32,8,512]{2,1,0:T(8,128)(2,1)} %bitcast.15), custom_call_target="tpu_custom_call" | custom-call | tf_op jit(solution)/shard_map/place_blocks/pallas_call | solution.py:78
  1.6 0.0 copy-start.2
  1.7 0.0 copy-start.3
  1.7 40.8 %all_to_all.15 = bf16[64,8,512]{2,1,0:T(8,128)(2,1)S(1)} all-to-all(bf16[64,8,512]{2,1,0:T(8,128)(2,1)S(1)} %get-tuple-element.11), channel_id=1, replica_groups=mesh['dp_0h'=2,'dp_0l'=2,'dp_1'=8,'dp_2'=2,'mp_0'=4,'mp_1'=2] {'dp_0h','..., dimensions={0} | all-to-all | bytes 1048576 | tf_op jit(solution)/shard_map/all_to_all | solution.py:351
  42.5 0.0 copy-done.2
  42.5 0.0 copy-done.3
  42.5 0.0 copy-start.1
  42.5 1.0 %precondition.1 = (bf16[64,8,256]{2,1,0:T(8,128)(2,1)S(1)}, bf16[64,8,256]{2,1,0:T(8,128)(2,1)S(1)}, f32[8,1,128]{2,1,0:T(1,128)S(1)}) custom-call(s32[34]{0:T(128)S(4)} %get-tuple-element.10.flag_ref, bf16[512,512]{1,0:T(8,128)(2,1)S(1)} %bitcast.9, bf16[512,512]{1,0:T(8,128)(2,1)S(1)} %bitcast.13, bf16[512,512]{1,0:T(8,128)(2,1)S(1)} %bitcast.14), custom_call_target="tpu_custom_call" | custom-call | tf_op jit(solution)/shard_map/precondition/pallas_call | solution.py:134
  43.5 0.0 copy-start
  43.5 2.8 %collective-permute-start = (bf16[64,8,256]{2,1,0:T(8,128)(2,1)S(1)}, bf16[64,8,256]{2,1,0:T(8,128)(2,1)S(1)}, u32[]{:S(2)}, u32[]{:S(2)}) collective-permute-start(bf16[64,8,256]{2,1,0:T(8,128)(2,1)S(1)} %get-tuple-element.13), channel_id=1, source_target_pairs={{0,256},{256,0},{1,257},{257,1},{2,258},{258,2},{3,259},{259,3},{4... | collective-permute-start | bytes 786440 | tf_op jit(solution)/shard_map/ppermute | solution.py:356
  46.3 7.4 %all_to_all.16.norm_ref = f32[8,1,128]{2,1,0:T(1,128)S(1)} all-to-all(f32[8,1,128]{2,1,0:T(1,128)S(1)} %get-tuple-element.12), channel_id=1, replica_groups=mesh['dp_0h'=2,'dp_0l'=2,'dp_1'=8,'dp_2'=2,'mp_0'=4,'mp_1'=2] {'mp_0','m..., dimensions={0} | all-to-all | bytes 8192 | tf_op jit(solution)/shard_map/all_to_all | solution.py:357
  53.7 0.9 %collective-permute-done.passed_ref = bf16[64,8,256]{2,1,0:T(8,128)(2,1)S(1)} collective-permute-done((bf16[64,8,256]{2,1,0:T(8,128)(2,1)S(1)}, bf16[64,8,256]{2,1,0:T(8,128)(2,1)S(1)}, u32[]{:S(2)}, u32[]{:S(2)}) %collective-permute-start) | collective-permute-done | bytes 262176 | tf_op jit(solution)/shard_map/ppermute | solution.py:356
  54.5 0.8 %fill_slots.1 = bf16[64,5,4,128]{3,2,1,0:T(4,128)(2,1)} custom-call(s32[34]{0:T(128)S(4)} %get-tuple-element.10.flag_ref, f32[8,1,128]{2,1,0:T(1,128)S(1)} %all_to_all.16.norm_ref, bf16[64,8,256]{2,1,0:T(8,128)(2,1)S(1)} %collective-permute-done.passed_ref, bf16[64,8,256]{2,1,0:T(8,128)(2,1)S(1)} %get-tuple-element.14.stay_ref), custom_call_target="tpu_custom_call" | custom-call | tf_op jit(solution)/shard_map/fill_slots/pallas_call | solution.py:192
  55.4 5.8 %all-to-all-start.2 = ((bf16[64,5,4,128]{3,2,1,0:T(4,128)(2,1)}), bf16[64,5,4,128]{3,2,1,0:T(4,128)(2,1)S(1)}, u32[]{:S(2)}, u32[]{:S(2)}) async-start(bf16[64,5,4,128]{3,2,1,0:T(4,128)(2,1)} %fill_slots.1), calls=%async_computation.2 | async-start | bytes 655360 | tf_op jit(solution)/shard_map/all_to_all | solution.py:359
  61.2 0.0 copy-done.1
  61.2 0.0 copy-done
  61.2 6.9 %refresh.1 = (bf16[512,512]{1,0:T(8,128)(2,1)}, bf16[512,512]{1,0:T(8,128)(2,1)}) custom-call(s32[34]{0:T(128)S(4)} %get-tuple-element.10.flag_ref, bf16[512,512]{1,0:T(8,128)(2,1)S(1)} %bitcast.10, f32[512,512]{1,0:T(8,128)S(1)} %bitcast.11, f32[512,512]{1,0:T(8,128)S(1)} %bitcast.12), custom_call_target="tpu_custom_call" | custom-call | tf_op jit(solution)/shard_map/refresh/pallas_call | solution.py:329
  68.0 11.6 %all-to-all-done.2.slot_ref = bf16[64,5,4,128]{3,2,1,0:T(4,128)(2,1)S(1)} async-done(((bf16[64,5,4,128]{3,2,1,0:T(4,128)(2,1)}), bf16[64,5,4,128]{3,2,1,0:T(4,128)(2,1)S(1)}, u32[]{:S(2)}, u32[]{:S(2)}) %all-to-all-start.2) | async-done | bytes 327712 | tf_op jit(solution)/shard_map/all_to_all | solution.py:359
  79.6 0.9 %scale_blocks.1 = bf16[32,8,512]{2,1,0:T(8,128)(2,1)} custom-call(s32[34]{0:T(128)S(4)} %get-tuple-element.10.flag_ref, bf16[64,5,4,128]{3,2,1,0:T(4,128)(2,1)S(1)} %all-to-all-done.2.slot_ref), custom_call_target="tpu_custom_call" | custom-call | tf_op jit(solution)/shard_map/scale_blocks/pallas_call | solution.py:243
Async XLA Ops:
  1.6 40.9 %copy-start.2 = (bf16[1,1,512,512]{3,2,1,0:T(8,128)(2,1)S(1)}, bf16[1,1,512,512]{3,2,1,0:T(8,128)(2,1)}, u32[]{:S(2)}) copy-start(bf16[1,1,512,512]{3,2,1,0:T(8,128)(2,1)} %param.10) | copy-start | bytes 1572868
  1.7 40.8 %copy-start.3 = (bf16[1,1,512,512]{3,2,1,0:T(8,128)(2,1)S(1)}, bf16[1,1,512,512]{3,2,1,0:T(8,128)(2,1)}, u32[]{:S(2)}) copy-start(bf16[1,1,512,512]{3,2,1,0:T(8,128)(2,1)} %param.11) | copy-start | bytes 1572868
  42.5 18.7 %copy-start.1 = (f32[1,1,512,512]{3,2,1,0:T(8,128)S(1)}, f32[1,1,512,512]{3,2,1,0:T(8,128)}, u32[]{:S(2)}) copy-start(f32[1,1,512,512]{3,2,1,0:T(8,128)} %param.9) | copy-start | bytes 3145732
  43.5 17.7 %copy-start = (f32[1,1,512,512]{3,2,1,0:T(8,128)S(1)}, f32[1,1,512,512]{3,2,1,0:T(8,128)}, u32[]{:S(2)}) copy-start(f32[1,1,512,512]{3,2,1,0:T(8,128)} %param.8) | copy-start | bytes 3145732
  43.5 11.0 %collective-permute-start = (bf16[64,8,256]{2,1,0:T(8,128)(2,1)S(1)}, bf16[64,8,256]{2,1,0:T(8,128)(2,1)S(1)}, u32[]{:S(2)}, u32[]{:S(2)}) collective-permute-start(bf16[64,8,256]{2,1,0:T(8,128)(2,1)S(1)} %get-tuple-element.13), channel_id=1, source_target_pairs={{0,256},{256,0},{1,257},{257,1},{2,258},{258,2},{3,259},{259,3},{4... | collective-permute-start | bytes 786440 | tf_op jit(solution)/shard_map/ppermute | solution.py:356
  55.4 24.3 %all-to-all-start.2 = ((bf16[64,5,4,128]{3,2,1,0:T(4,128)(2,1)}), bf16[64,5,4,128]{3,2,1,0:T(4,128)(2,1)S(1)}, u32[]{:S(2)}, u32[]{:S(2)}) async-start(bf16[64,5,4,128]{3,2,1,0:T(4,128)(2,1)} %fill_slots.1), calls=%async_computation.2 | async-start | bytes 655360 | tf_op jit(solution)/shard_map/all_to_all | solution.py:359
